TPU v7x, 128 devices: a whole 4x4x4 slice. The times are simulated.
128 devices in a mesh: tok: 16 (over z_lo, y, core), blk: 8 (over x, z_hi).
Axes of the slice: x: 4, y: 4, z: 4 (z_hi: 2, z_lo: 2; z = z_hi * 2 + z_lo), core: 2. Of those that a mesh axis runs over, the one named last changes fastest.
Arguments:
- activations: bfloat16 [8192, 4096], P('tok', 'blk'), may hold values from -52 to 52, as said below
- out_grads: bfloat16 [8192, 4096], P('tok', 'blk'), may hold values from -52 to 52, as said below
Outputs:
- act_inverse: float32 [4096, 4096], P(('tok', 'blk'))
- grad_inverse: float32 [4096, 4096], P(('tok', 'blk'))
Inputs may be any that keep to these rules, and one draw needn't show every extreme that they name: `activations`: real entries. `out_grads`: real entries.
All inputs are finite; a program needn't handle non-finite values.
Results may differ from a plain program's by a relative error of at most 0.02.
Values may be sent and summed in bfloat16 or wider, within the bound.
A program may use at most 64 MiB of HBM per device.

v0:
```python
import jax
import jax.numpy as jnp
from jax import lax
from jax.sharding import PartitionSpec as P

D = 4096


damping = 0.3
epsilon = 1e-06
divisor = 2.0


def laid_out(pieces, dim):
    pieces = jnp.moveaxis(pieces, 0, dim)
    dims = pieces.shape
    return pieces.reshape(*dims[:dim], dims[dim] * dims[dim + 1], *dims[dim + 2 :])


def sent_to_all(value, axis):
    length = lax.axis_size(axis)
    return lax.all_to_all(
        jnp.broadcast_to(value[None], (length, *value.shape)), axis, 0, 0, tiled=True
    )


def gather_directly(value, axis, dim):
    return laid_out(sent_to_all(value, axis), dim)


def side_by_side(arrays, axis, dim, along):
    widths = [a.shape[along] for a in arrays]
    both = jnp.concatenate(arrays, axis=along)
    out = lax.all_gather(both, axis, axis=dim, tiled=True)
    return tuple(jnp.split(out, [sum(widths[:k]) for k in range(1, len(widths))], axis=along))


def of_everyone(value, axis):
    everything = sent_to_all(value, axis)
    return jnp.sum(everything.astype(jnp.float32), axis=0)


def column_squares(data):
    values = data.astype(jnp.float32)
    return jnp.sum(values * values, axis=0)


def newton_steps(scaled, identity):
    half = scaled.astype(jnp.bfloat16)
    row_block = gather_directly(half, "blk", 1)
    column_block = lax.all_gather(half, "tok", axis=0, tiled=True)
    square = jnp.dot(row_block, column_block, preferred_element_type=jnp.float32)
    square_block = gather_directly(square.astype(jnp.bfloat16), "blk", 1)
    cube = jnp.dot(square_block, column_block, preferred_element_type=jnp.float32)
    return 4.0 * identity - 6.0 * scaled + 4.0 * square - cube


def body(activations, out_grads):
    tok_count = lax.axis_size("tok")
    blk_count = lax.axis_size("blk")
    tok_id = lax.axis_index("tok")
    blk_id = lax.axis_index("blk")
    token_count = activations.shape[0] * tok_count
    tile_rows = D // tok_count
    tile_cols = D // blk_count
    full_acts, full_grads = side_by_side((activations, out_grads), "blk", 1, 0)
    sums_act, sums_grad = (
        of_everyone(column_squares(full_acts).astype(jnp.bfloat16), "tok").astype(jnp.float32),
        of_everyone(column_squares(full_grads).astype(jnp.bfloat16), "tok").astype(jnp.float32),
    )
    row_ids = tok_id * tile_rows + jnp.arange(tile_rows, dtype=jnp.int32)
    col_ids = blk_id * tile_cols + jnp.arange(tile_cols, dtype=jnp.int32)
    identity = (row_ids[:, None] == col_ids[None, :]).astype(jnp.float32)

    def damped_tile(full, local, sums):
        gram_tile = lax.psum_scatter(
            lax.dot_general(
                full, local, (((0,), (0,)), ((), ())), preferred_element_type=jnp.float32
            ).astype(jnp.bfloat16),
            "tok",
            scatter_dimension=0,
            tiled=True,
        ).astype(jnp.float32)
        inverse = lax.rsqrt(sums / token_count + epsilon)
        inverse_rows = lax.dynamic_slice_in_dim(inverse, tok_id * tile_rows, tile_rows)
        inverse_cols = lax.dynamic_slice_in_dim(inverse, blk_id * tile_cols, tile_cols)
        return (
            gram_tile / token_count * inverse_rows[:, None] * inverse_cols[None, :]
            + damping * identity
        )

    damped_act = damped_tile(full_acts, activations, sums_act)
    damped_grad = damped_tile(full_grads, out_grads, sums_grad)
    results = []
    for damped in (damped_act, damped_grad):
        scaled = damped / divisor
        result_tile = newton_steps(scaled, identity)
        results.append(
            lax.all_to_all(
                result_tile.astype(jnp.bfloat16), "blk", split_axis=0, concat_axis=1, tiled=True
            ).astype(result_tile.dtype)
        )
    return (results[0], results[1])


def solution(mesh):
    placed = (P("tok", "blk"), P("tok", "blk"))
    return jax.shard_map(
        body,
        mesh=mesh,
        in_specs=placed,
        out_specs=(P(("tok", "blk"), None), P(("tok", "blk"), None)),
        check_vma=False,
    )
```

profile of v0, /device:TPU:0, one launch (start us, length us, event | category | flops | bytes accessed | tf_op | source)
XLA Modules:
  0.0 490.7 jit_solution(2053735657801038295)
XLA Ops:
  7.2 2.3 pad_maximum_fusion
  9.6 122.6 %all-gather.4.cloned.1.call-done = bf16[1024,4096]{1,0:T(8,128)(2,1)} async-done(((bf16[1024,512]{1,0:T(8,128)(2,1)}), bf16[1024,4096]{1,0:T(8,128)(2,1)}) %all-gather.4.cloned.1.call-update) | async-done | bytes 8388624 | tf_op jit(solution)/shard_map/all_gather | solution.py:34
  132.2 6.7 %convolution_convert_fusion = bf16[4096,512]{1,0:T(8,128)(2,1)} fusion(bf16[512,512]{1,0:T(8,128)(2,1)} %param.3, bf16[1024,4096]{1,0:T(8,128)(2,1)} %all-gather.4.cloned.1.call-done), kind=kOutput, calls=%fused_computation.2 | convolution fusion | flops 2149580800 | bytes 8912896 | tf_op jit(solution)/shard_map/dot_general | solution.py:77
  139.0 1.0 copy-done.2
  139.9 6.5 %convolution_convert_fusion.1 = bf16[4096,512]{1,0:T(8,128)(2,1)} fusion(bf16[512,512]{1,0:T(8,128)(2,1)S(1)} %copy-done.2, bf16[1024,4096]{1,0:T(8,128)(2,1)} %all-gather.4.cloned.1.call-done), kind=kOutput, calls=%fused_computation.3 | convolution fusion | flops 2149580800 | bytes 8912896 | tf_op jit(solution)/shard_map/dot_general | solution.py:77
  146.5 4.4 multiply_reduce_fusion
  150.8 0.2 broadcast_in_dim.15
  151.0 0.5 broadcast.79
  151.6 1.4 reduce.2
  153.0 0.7 reshape.70
  153.7 4.7 all-to-all-start.4
  158.4 0.2 broadcast_in_dim.12
  158.6 1.4 reduce.3
  160.0 0.7 reshape.68
  160.8 4.1 all-to-all-done.4
  164.9 3.6 all-to-all-start
  168.6 0.2 convert_reduce_fusion
  168.9 6.4 %all-to-all-done = bf16[16,2,2048]{2,1,0:T(2,128)(2,1)S(1)} async-done(((bf16[16,2,2048]{2,1,0:T(2,128)(2,1)}), bf16[16,2,2048]{2,1,0:T(2,128)(2,1)S(1)}, u32[]{:S(2)}, u32[]{:S(2)}) %all-to-all-start) | async-done | bytes 131104 | tf_op jit(solution)/shard_map/all_to_all | solution.py:22
  175.4 0.2 convert_reduce_fusion.1
  175.9 31.3 %reduce-scatter.5.cloned.1.call-done = bf16[256,512]{1,0:T(8,128)(2,1)} async-done(((bf16[4096,512]{1,0:T(8,128)(2,1)}), bf16[256,512]{1,0:T(8,128)(2,1)}) %reduce-scatter.5.cloned.1.call-update) | async-done | bytes 262160 | tf_op jit(solution)/shard_map/reduce_scatter | solution.py:76
  207.1 67.9 %reduce-scatter.3.cloned.1.call-done = bf16[256,512]{1,0:T(8,128)(2,1)} async-done(((bf16[4096,512]{1,0:T(8,128)(2,1)}), bf16[256,512]{1,0:T(8,128)(2,1)}) %reduce-scatter.3.cloned.1.call-update) | async-done | bytes 262160 | tf_op jit(solution)/shard_map/reduce_scatter | solution.py:76
  275.0 2.1 multiply_convert_fusion
  277.2 0.5 all-gather.8.cloned.1.call-update
  277.7 1.1 copy.27
  278.8 1.5 broadcast_in_dim.13
  280.3 6.7 %all-to-all-start.1 = ((bf16[8,256,512]{1,2,0:T(8,128)(2,1)}), bf16[8,256,512]{1,2,0:T(8,128)(2,1)S(1)}, u32[]{:S(2)}, u32[]{:S(2)}) async-start(bf16[8,256,512]{1,2,0:T(8,128)(2,1)} %broadcast_in_dim.13), calls=%async_computation.2 | async-start | bytes 4194304 | tf_op jit(solution)/shard_map/all_to_all | solution.py:22
  287.2 29.2 %all-to-all-done.1 = bf16[8,256,512]{1,2,0:T(8,128)(2,1)S(1)} async-done(((bf16[8,256,512]{1,2,0:T(8,128)(2,1)}), bf16[8,256,512]{1,2,0:T(8,128)(2,1)S(1)}, u32[]{:S(2)}, u32[]{:S(2)}) %all-to-all-start.1) | async-done | bytes 2097184 | tf_op jit(solution)/shard_map/all_to_all | solution.py:22
  316.4 1.6 broadcast_in_dim.16
  318.0 0.4 copy-done.1
  318.4 4.7 all-to-all-start.5
  323.1 28.8 %all-gather.6.cloned.1.call-done = bf16[4096,512]{1,0:T(8,128)(2,1)} async-done(((bf16[256,512]{1,0:T(8,128)(2,1)}), bf16[4096,512]{1,0:T(8,128)(2,1)}) %all-gather.6.cloned.1.call-update) | async-done | bytes 4194320 | tf_op jit(solution)/shard_map/all_gather | solution.py:51
  351.9 4.1 fusion.8
  356.0 0.1 copy.28
  356.1 1.5 broadcast_in_dim.14
  357.6 7.7 %all-to-all-start.2 = ((bf16[8,256,512]{1,2,0:T(8,128)(2,1)}), bf16[8,256,512]{1,2,0:T(8,128)(2,1)}, u32[]{:S(2)}, u32[]{:S(2)}) async-start(bf16[8,256,512]{1,2,0:T(8,128)(2,1)} %broadcast_in_dim.14), calls=%async_computation.3 | async-start | bytes 4194304 | tf_op jit(solution)/shard_map/all_to_all | solution.py:22
  365.3 49.7 %all-gather.8.cloned.1.call-done = bf16[4096,512]{1,0:T(8,128)(2,1)} async-done(((bf16[256,512]{1,0:T(8,128)(2,1)}), bf16[4096,512]{1,0:T(8,128)(2,1)}) %all-gather.8.cloned.1.call-update) | async-done | bytes 4194320 | tf_op jit(solution)/shard_map/all_gather | solution.py:51
  415.0 4.2 fusion.9
  419.4 1.5 broadcast_in_dim.17
  420.9 6.8 %all-to-all-start.6 = ((bf16[8,256,512]{1,2,0:T(8,128)(2,1)}), bf16[8,256,512]{1,2,0:T(8,128)(2,1)S(1)}, u32[]{:S(2)}, u32[]{:S(2)}) async-start(bf16[8,256,512]{1,2,0:T(8,128)(2,1)} %broadcast_in_dim.17), calls=%async_computation.8 | async-start | bytes 4194304 | tf_op jit(solution)/shard_map/all_to_all | solution.py:22
  427.7 4.9 %fusion.2 = bf16[256,512]{1,0:T(8,128)(2,1)} fusion(bf16[256,4096]{0,1:T(8,128)(2,1)} %bitcast.3, bf16[4096,512]{1,0:T(8,128)(2,1)} %all-gather.6.cloned.1.call-done, f32[256,512]{1,0:T(8,128)S(1)} %get-tuple-element.7, bf16[256,512]{1,0:T(8,128)(2,1)S(1)} %copy-done.4, f32[512]{0:T(512)S(1)} %dynamic_slice.13, f32[256]{0:T(256)S(1)} %dynamic-slice_multiply_fusion.1, ...), kind=kOutput, calls=%fused_computation.8 | convolution fusion | flops 1075445760 | bytes 7346176 | tf_op jit(solution)/shard_map/dot_general | solution.py:54
  432.6 26.9 %all-to-all-done.6 = bf16[8,256,512]{1,2,0:T(8,128)(2,1)S(1)} async-done(((bf16[8,256,512]{1,2,0:T(8,128)(2,1)}), bf16[8,256,512]{1,2,0:T(8,128)(2,1)S(1)}, u32[]{:S(2)}, u32[]{:S(2)}) %all-to-all-start.6) | async-done | bytes 2097184 | tf_op jit(solution)/shard_map/all_to_all | solution.py:22
  459.5 3.5 all-to-all-start.3
  463.1 4.3 fusion.3
  467.4 4.1 all-to-all-done.3
  471.5 3.4 all-to-all-start.7
  475.0 0.8 copy.34
  475.8 7.5 %all-to-all-done.7 = bf16[8,32,512]{2,1,0:T(8,128)(2,1)S(1)} async-done(((bf16[8,32,512]{2,1,0:T(8,128)(2,1)}), bf16[8,32,512]{2,1,0:T(8,128)(2,1)S(1)}, u32[]{:S(2)}, u32[]{:S(2)}) %all-to-all-start.7) | async-done | bytes 262176 | tf_op jit(solution)/shard_map/all_to_all | solution.py:99
  483.3 0.8 copy.35
  (33 shorter events, 1.2 us)
Async XLA Ops:
  7.2 125.1 %all-gather.4.cloned.1.call-start = ((), (), s32[]{:S(2)}) async-start(), calls=%async_computation.10 | async-start | bytes 9437184 | tf_op jit(solution)/shard_map/all_gather | solution.py:34
  9.6 197.6 %reduce-scatter.5.cloned.1.call-start = ((), (), s32[]{:S(2)}) async-start(), calls=%async_computation.13 | async-start | bytes 4456448 | tf_op jit(solution)/shard_map/reduce_scatter | solution.py:76
  138.9 1.0 copy-start.2
  138.9 136.1 %reduce-scatter.3.cloned.1.call-start = ((), (), s32[]{:S(2)}) async-start(), calls=%async_computation.11 | async-start | bytes 4456448 | tf_op jit(solution)/shard_map/reduce_scatter | solution.py:76
  153.7 11.2 %all-to-all-start.4 = ((bf16[16,2,2048]{2,1,0:T(2,128)(2,1)}), bf16[16,2,2048]{2,1,0:T(2,128)(2,1)S(1)}, u32[]{:S(2)}, u32[]{:S(2)}) async-start(bf16[16,2,2048]{2,1,0:T(2,128)(2,1)} %reshape.70), calls=%async_computation.6 | async-start | bytes 262144 | tf_op jit(solution)/shard_map/all_to_all | solution.py:22
  164.9 10.4 %all-to-all-start = ((bf16[16,2,2048]{2,1,0:T(2,128)(2,1)}), bf16[16,2,2048]{2,1,0:T(2,128)(2,1)S(1)}, u32[]{:S(2)}, u32[]{:S(2)}) async-start(bf16[16,2,2048]{2,1,0:T(2,128)(2,1)} %reshape.68), calls=%async_computation.1 | async-start | bytes 262144 | tf_op jit(solution)/shard_map/all_to_all | solution.py:22
  168.5 183.4 %all-gather.6.cloned.1.call-start = ((), (), s32[]{:S(2)}) async-start(), calls=%async_computation.12 | async-start | bytes 4456448 | tf_op jit(solution)/shard_map/all_gather | solution.py:51
  277.1 10.0 %copy-start = (bf16[256,512]{1,0:T(8,128)(2,1)S(1)}, bf16[256,512]{1,0:T(8,128)(2,1)}, u32[]{:S(2)}) copy-start(bf16[256,512]{1,0:T(8,128)(2,1)} %get-tuple-element.4) | copy-start | bytes 786436
  277.1 137.9 %all-gather.8.cloned.1.call-start = ((), (), s32[]{:S(2)}) async-start(), calls=%async_computation.14 | async-start | bytes 4456448 | tf_op jit(solution)/shard_map/all_gather | solution.py:51
  280.3 36.1 %all-to-all-start.1 = ((bf16[8,256,512]{1,2,0:T(8,128)(2,1)}), bf16[8,256,512]{1,2,0:T(8,128)(2,1)S(1)}, u32[]{:S(2)}, u32[]{:S(2)}) async-start(bf16[8,256,512]{1,2,0:T(8,128)(2,1)} %broadcast_in_dim.13), calls=%async_computation.2 | async-start | bytes 4194304 | tf_op jit(solution)/shard_map/all_to_all | solution.py:22
  316.4 2.0 copy-start.1
  318.4 37.7 %all-to-all-start.5 = ((bf16[8,256,512]{1,2,0:T(8,128)(2,1)}), bf16[8,256,512]{1,2,0:T(8,128)(2,1)S(1)}, u32[]{:S(2)}, u32[]{:S(2)}) async-start(bf16[8,256,512]{1,2,0:T(8,128)(2,1)} %broadcast_in_dim.16), calls=%async_computation.7 | async-start | bytes 4194304 | tf_op jit(solution)/shard_map/all_to_all | solution.py:22
  357.6 61.8 %all-to-all-start.2 = ((bf16[8,256,512]{1,2,0:T(8,128)(2,1)}), bf16[8,256,512]{1,2,0:T(8,128)(2,1)}, u32[]{:S(2)}, u32[]{:S(2)}) async-start(bf16[8,256,512]{1,2,0:T(8,128)(2,1)} %broadcast_in_dim.14), calls=%async_computation.3 | async-start | bytes 4194304 | tf_op jit(solution)/shard_map/all_to_all | solution.py:22
  419.2 8.5 %copy-start.4 = (bf16[256,512]{1,0:T(8,128)(2,1)S(1)}, bf16[256,512]{1,0:T(8,128)(2,1)}, u32[]{:S(2)}) copy-start(bf16[256,512]{1,0:T(8,128)(2,1)} %reduce-scatter.3.cloned.1.call-done) | copy-start | bytes 786436
  420.9 38.6 %all-to-all-start.6 = ((bf16[8,256,512]{1,2,0:T(8,128)(2,1)}), bf16[8,256,512]{1,2,0:T(8,128)(2,1)S(1)}, u32[]{:S(2)}, u32[]{:S(2)}) async-start(bf16[8,256,512]{1,2,0:T(8,128)(2,1)} %broadcast_in_dim.17), calls=%async_computation.8 | async-start | bytes 4194304 | tf_op jit(solution)/shard_map/all_to_all | solution.py:22
  427.7 35.3 %copy-start.3 = (bf16[256,512]{1,0:T(8,128)(2,1)S(1)}, bf16[256,512]{1,0:T(8,128)(2,1)}, u32[]{:S(2)}) copy-start(bf16[256,512]{1,0:T(8,128)(2,1)} %reduce-scatter.5.cloned.1.call-done) | copy-start | bytes 786436
  459.5 12.0 %all-to-all-start.3 = ((bf16[8,32,512]{2,1,0:T(8,128)(2,1)}), bf16[8,32,512]{2,1,0:T(8,128)(2,1)S(1)}, u32[]{:S(2)}, u32[]{:S(2)}) async-start(bf16[8,32,512]{2,1,0:T(8,128)(2,1)} %bitcast.4), calls=%async_computation.4 | async-start | bytes 524288 | tf_op jit(solution)/shard_map/all_to_all | solution.py:99
  471.5 11.8 %all-to-all-start.7 = ((bf16[8,32,512]{2,1,0:T(8,128)(2,1)}), bf16[8,32,512]{2,1,0:T(8,128)(2,1)S(1)}, u32[]{:S(2)}, u32[]{:S(2)}) async-start(bf16[8,32,512]{2,1,0:T(8,128)(2,1)} %bitcast.10), calls=%async_computation.9 | async-start | bytes 524288 | tf_op jit(solution)/shard_map/all_to_all | solution.py:99
Sparse Core Ops, SparseCore 0:
  10.2 122.0 all-gather.3
  139.1 68.0 reduce-scatter.4
  209.5 65.4 reduce-scatter.2
  277.3 74.5 all-gather.5
  354.0 60.9 all-gather.7
where the time goes:
time: 492 us; the launch traced here: 491 us
  waiting for transfers between devices  379 us (77%)
  starting transfers between devices  41.3 us (8%)
  matrix products  30.8 us (6%)
  between operations  14 us (3%)
  local copies, waits for them, and re-layouts  13.4 us (3%)
  other arithmetic  12.2 us (2%)
    all_gather x1, waiting for transfers between devices, side_by_side(): out = lax.all_gather(both, axis, axis=dim, tiled=True)  123 us
    reduce_scatter x2, waiting for transfers between devices, damped_tile(): lax.psum_scatter(lax.dot_general(full, local, (((0,), (0,)), ((), ())), p...  99.2 us
    all_gather x2, waiting for transfers between devices, newton_steps(): column_block = lax.all_gather(half, 'tok', axis=0, tiled=True)  78.5 us
    all_to_all x6, waiting for transfers between devices, sent_to_all(): lax.all_to_all(jnp.broadcast_to(value[None], (length, *value.shape)), axi...  66.5 us
    all_to_all x6, starting transfers between devices, sent_to_all(): lax.all_to_all(jnp.broadcast_to(value[None], (length, *value.shape)), axi...  34.2 us
    dot_general x2, matrix products, damped_tile(): lax.dot_general(full, local, (((0,), (0,)), ((), ())), preferred_element_...  13.2 us
    all_to_all x2, waiting for transfers between devices, body(): lax.all_to_all(result_tile.astype(jnp.bfloat16), 'blk', split_axis=0, con...  11.6 us
  transfers between devices with their start and end apart: 13, of which 11 were waited for; matrix products, arithmetic and copies ran while one was open for 8% of the time, Pallas kernels for 0%

commit v1 on v0

v1 whole, which is shorter than its diff:
```python
import jax
import jax.numpy as jnp
from jax import lax
from jax.experimental import pallas as pl
from jax.experimental.pallas import tpu as pltpu
from jax.sharding import PartitionSpec as P

D = 4096
TOKENS = 8192
BLOCK = 512
HALF = 256
QUARTER = 128

damping = 0.3
epsilon = 1e-06
divisor = 2.0

MESH = pl.DeviceIdType.MESH
F32 = jnp.float32
BF16 = jnp.bfloat16

X_ID = 0
D_ID = 5
Y1_ID = 9
Y2_ID = 11
Z_ID = 15
ROW_ID = 16
COL_ID = 25
SQ_ID = 44
OUT_ID = 63
N_ID = 71


class Gather:
    def __init__(self, send, wait, base, ref, plus, minus, across, via_z, pass_on=None):
        self.send, self.wait, self.base, self.ref = send, wait, base, ref
        self.plus, self.minus, self.across, self.via_z = plus, minus, across, via_z
        self.pass_on = pass_on

    def incoming(self, k):
        return [
            (3, 0, None), (1, 0, None), (0, 1, None), (2, 0, 0), (2, 0, 1),
            (3, 1, None), (1, 1, None), (2, 1, 0), (2, 1, 1),
        ][k]

    def put(self, k, place, to):
        r = self.ref(*place)
        self.send(self.base + k, r, r, to)

    def take(self, k):
        r = self.ref(*self.incoming(k))
        self.wait(self.base + k, r)
        if self.pass_on is not None:
            self.pass_on(self.base + 10 + k, r)

    def start(self):
        own = (0, 0, None)
        self.put(0, own, self.plus)
        self.put(1, own, self.minus)
        self.put(2, own, self.across)
        if self.pass_on is not None:
            self.pass_on(self.base + 9, self.ref(*own))

    def near(self):
        self.take(0)
        self.put(3, (3, 0, 0), self.plus)
        self.take(1)
        self.put(4, (1, 0, 1), self.minus)

    def other(self):
        self.take(2)
        self.put(5, (0, 1, None), self.plus)
        self.put(6, (0, 1, None), self.minus)

    def far(self):
        if self.via_z:
            self.take(3)
            self.put(7, (2, 0, 0), self.across)
            self.take(4)
            self.put(8, (2, 0, 1), self.across)
        else:
            self.take(5)
            self.put(7, (3, 1, 0), self.plus)
            self.take(6)
            self.put(8, (1, 1, 1), self.minus)

    def finish(self):
        for k in (5, 6, 7, 8) if self.via_z else (3, 4, 7, 8):
            self.take(k)


def kernel(
    act_ref, grad_ref, act_out, grad_out,
    xbuf, zbuf, pown, dsend, drecv, y1s, y1r, y2s, y2r, tot, zs, zr, scaled,
    rowbuf, colbuf, sqrow, sqcol, sq, obuf, orecv, csend, crecv, totbuf,
    ssem, rsem, csem, crsem, tsem, trsem, lsem,
):
    tok, blk = lax.axis_index("tok"), lax.axis_index("blk")
    c, y, zl = tok % 2, (tok // 2) % 4, tok // 8
    x, zh = blk // 2, blk % 2

    def tok_of(zl_, y_, c_):
        return zl_ * 8 + y_ * 2 + c_

    def blk_of(x_, zh_):
        return x_ * 2 + zh_

    x_plus = (tok, blk_of((x + 1) % 4, zh))
    x_minus = (tok, blk_of((x + 3) % 4, zh))
    zh_mate = (tok, blk_of(x, 1 - zh))
    y_plus = (tok_of(zl, (y + 1) % 4, c), blk)
    y_minus = (tok_of(zl, (y + 3) % 4, c), blk)
    zl_mate = (tok_of(1 - zl, y, c), blk)
    sibling = (tok_of(zl, y, 1 - c), blk)

    def place(to):
        return {"tok": to[0], "blk": to[1]}

    out_tok = 4 * y + 2 * zh + c
    home = out_tok == tok
    phi = 2 * x + zl
    row_block = 2 * y + zh

    barrier = pltpu.get_barrier_semaphore()

    def greet_tok(j, carry):
        pl.semaphore_signal(
            barrier, inc=1, device_id=place(((tok + j) % 16, blk)), device_id_type=MESH
        )
        return carry

    def greet_blk(j, carry):
        pl.semaphore_signal(
            barrier, inc=1, device_id=place((tok, (blk + j) % 8)), device_id_type=MESH
        )
        return carry

    lax.fori_loop(1, 16, greet_tok, 0)
    lax.fori_loop(1, 8, greet_blk, 0)

    def source_of(j):
        return (tok_of(j % 2, tok // 4, c), blk_of(j // 2, (tok // 2) % 2))

    def greet_source(j, carry):
        to = source_of(j)
        me = (to[0] == tok) & (to[1] == blk)

        @pl.when(jnp.logical_not(me))
        def _():
            pl.semaphore_signal(barrier, inc=1, device_id=place(to), device_id_type=MESH)

        return carry

    lax.fori_loop(0, 8, greet_source, 0)

    def load_own(f):
        return pltpu.make_async_copy((act_ref, grad_ref)[f], xbuf.at[f, x], lsem.at[f])

    load_own(0).start()
    load_own(1).start()
    pl.semaphore_wait(barrier, 15 + 7 + 8 - home.astype(jnp.int32))

    sent = []

    def sender(f):
        def send(k, src, dst, to):
            copy = pltpu.make_async_remote_copy(
                src_ref=src, dst_ref=dst, send_sem=ssem.at[f, k], recv_sem=rsem.at[f, k],
                device_id=place(to), device_id_type=MESH,
            )
            copy.start()
            sent.append(copy)

        return send

    def waiter(f):
        def wait(k, dst):
            pltpu.make_async_remote_copy(
                src_ref=dst, dst_ref=dst, send_sem=ssem.at[f, k], recv_sem=rsem.at[f, k],
                device_id=place(sibling), device_id_type=MESH,
            ).wait_recv()

        return wait

    sends, waits = (sender(0), sender(1)), (waiter(0), waiter(1))
    low, high = pl.ds(0, HALF), pl.ds(HALF, HALF)

    def x_start(f):
        own = xbuf.at[f, x]
        sends[f](X_ID + 0, own, own, x_plus)
        sends[f](X_ID + 1, own, own, x_minus)
        sends[f](X_ID + 2, own, zbuf.at[f], zh_mate)

    def x_forward(f):
        left, right = (x + 3) % 4, (x + 1) % 4
        waits[f](X_ID + 0, xbuf.at[f, left])
        part = xbuf.at[f, left, low]
        sends[f](X_ID + 3, part, part, x_plus)
        waits[f](X_ID + 1, xbuf.at[f, right])
        part = xbuf.at[f, right, high]
        sends[f](X_ID + 4, part, part, x_minus)

    def x_finish(f):
        far = (x + 2) % 4
        waits[f](X_ID + 2, zbuf.at[f])
        waits[f](X_ID + 3, xbuf.at[f, far, low])
        waits[f](X_ID + 4, xbuf.at[f, far, high])

    def column_sums(f):
        values = xbuf[f, x].astype(F32)
        csend[f : f + 1, :] = jnp.sum(values * values, axis=0, keepdims=True)

    def sum_copy(j):
        return pltpu.make_async_remote_copy(
            src_ref=csend, dst_ref=crecv.at[j], send_sem=csem.at[j], recv_sem=crsem.at[j],
            device_id=place(((tok + j) % 16, blk)), device_id_type=MESH,
        )

    def sums_start():
        def step(j, carry):
            sum_copy(j).start()
            return carry

        lax.fori_loop(1, 16, step, 0)

    total_to = [(tok, blk_of((x + j) % 4, zh)) for j in (1, 2, 3)] + [zh_mate]

    def total_copy(j):
        slot = x if j < 3 else 4
        return pltpu.make_async_remote_copy(
            src_ref=totbuf.at[x], dst_ref=totbuf.at[slot], send_sem=tsem.at[j],
            recv_sem=trsem.at[j], device_id=place(total_to[j]), device_id_type=MESH,
        )

    def totals_start():
        def step(j, carry):
            sum_copy(j).wait_recv()
            return carry

        lax.fori_loop(1, 16, step, 0)
        total = csend[...]
        for j in range(1, 16):
            total = total + crecv[j]
        totbuf[x] = total
        for j in range(4):
            total_copy(j).start()

    def totals_finish():
        for j in range(4):
            total_copy(j).wait_recv()

    def gram(f):
        mine = pl.ds(pl.multiple_of(c * HALF, HALF), HALF)
        theirs = pl.ds(pl.multiple_of((1 - c) * HALF, HALF), HALF)

        def product(left, right):
            return lax.dot_general(
                left, right, (((0,), (0,)), ((), ())), preferred_element_type=F32
            ).astype(BF16)

        def step(i, carry):
            to = (y + 2 + i) % 4
            dsend[f, to, zh] = product(xbuf[f, to, :, theirs], xbuf[f, x])
            dsend[f, to, 1 - zh] = product(xbuf[f, to, :, theirs], zbuf[f])
            d_copy(f, to).start()
            pown[f, to, zh] = product(xbuf[f, to, :, mine], xbuf[f, x])
            pown[f, to, 1 - zh] = product(xbuf[f, to, :, mine], zbuf[f])
            return carry

        lax.fori_loop(0, 4, step, 0)

    def d_copy(f, to):
        return pltpu.make_async_remote_copy(
            src_ref=dsend.at[f, to], dst_ref=drecv.at[f, to], send_sem=ssem.at[f, D_ID + to],
            recv_sem=rsem.at[f, D_ID + to], device_id=place(sibling), device_id_type=MESH,
        )

    def both(f, to, b):
        return pown[f, to, b].astype(F32) + drecv[f, to, b].astype(F32)

    y_far, y_up, y_down = (y + 2) % 4, (y + 1) % 4, (y + 3) % 4

    def reduce_start(f):
        d_copy(f, y_far).wait_recv()
        y1s[f, 0] = both(f, y_far, 0).astype(BF16)
        sends[f](Y1_ID + 0, y1s.at[f, 0], y1r.at[f, 0], y_plus)
        y1s[f, 1] = both(f, y_far, 1).astype(BF16)
        sends[f](Y1_ID + 1, y1s.at[f, 1], y1r.at[f, 1], y_minus)
        d_copy(f, y_down).wait_recv()
        y2s[f, 2] = both(f, y_down, 0).astype(BF16)
        sends[f](Y2_ID + 2, y2s.at[f, 2], y2r.at[f, 2], y_minus)
        d_copy(f, y).wait_recv()
        d_copy(f, y_up).wait_recv()
        y2s[f, 0] = both(f, y_up, 1).astype(BF16)
        sends[f](Y2_ID + 0, y2s.at[f, 0], y2r.at[f, 0], y_plus)

    def reduce_middle(f):
        waits[f](Y1_ID + 0, y1r.at[f, 0])
        y2s[f, 1] = (both(f, y_up, 0) + y1r[f, 0].astype(F32)).astype(BF16)
        sends[f](Y2_ID + 1, y2s.at[f, 1], y2r.at[f, 1], y_plus)
        waits[f](Y1_ID + 1, y1r.at[f, 1])
        y2s[f, 3] = (both(f, y_down, 1) + y1r[f, 1].astype(F32)).astype(BF16)
        sends[f](Y2_ID + 3, y2s.at[f, 3], y2r.at[f, 3], y_minus)

    def reduce_last(f):
        for k in range(4):
            waits[f](Y2_ID + k, y2r.at[f, k])
        tot[f, 0] = both(f, y, 0) + y2r[f, 1].astype(F32) + y2r[f, 2].astype(F32)
        tot[f, 1] = both(f, y, 1) + y2r[f, 0].astype(F32) + y2r[f, 3].astype(F32)
        zs[f] = tot[f, 1 - zl].astype(BF16)
        sends[f](Z_ID, zs.at[f], zr.at[f], zl_mate)

    def eye(rows, start_col):
        r = lax.broadcasted_iota(jnp.int32, (rows, QUARTER), 0) + BLOCK * row_block + HALF * c
        k = lax.broadcasted_iota(jnp.int32, (rows, QUARTER), 1) + BLOCK * phi + start_col
        return (r == k).astype(F32)

    def inverse(sums):
        return lax.rsqrt(sums / TOKENS + epsilon)

    def normalise(f):
        waits[f](Z_ID, zr.at[f])
        of_col = jnp.where(zl == zh, x, 4)
        inv_col = inverse(totbuf[of_col, f : f + 1, :])
        mine = pl.ds(pl.multiple_of(c * HALF, HALF), HALF)
        inv_row = inverse(totbuf[y, f : f + 1, mine])
        inv_row = jnp.transpose(jnp.broadcast_to(inv_row, (QUARTER, HALF)))
        for j in range(4):
            cols = slice(j * QUARTER, (j + 1) * QUARTER)
            g = tot[f, zl, :, cols] + zr[f, :, cols].astype(F32)
            damped = g / TOKENS * inv_row * inv_col[:, cols] + damping * eye(HALF, j * QUARTER)
            value = damped / divisor
            scaled[f, :, cols] = value
            rowbuf[f, phi, :, cols] = value.astype(BF16)
            colbuf[f, row_block, c, :, cols] = value.astype(BF16)

    parts = (pl.ds(0, QUARTER), pl.ds(QUARTER, QUARTER))

    def row_gather(f, buf, base):
        def ref(step, other, part):
            slot = ((x + step) % 4) * 2 + (1 - zl if other else zl)
            piece = buf(slot)
            return piece if part is None else piece.at[parts[part]]

        return Gather(sends[f], waits[f], base, ref, x_plus, x_minus, zl_mate, True)

    def col_gather(f, buf, base):
        def ref(step, other, part):
            slot = ((y + step) % 4) * 2 + (1 - zh if other else zh)
            piece = buf(slot, c)
            return piece if part is None else piece.at[parts[part]]

        def pass_on(k, r):
            sends[f](k, r, r, sibling)

        return Gather(
            sends[f], waits[f], base, ref, y_plus, y_minus, zh_mate, False, pass_on
        )

    def sibling_finish(f, buf, base):
        whole = [9, 10, 11, 12, 15, 16]
        for k in range(9, 19):
            piece = buf(0, 1 - c)
            waits[f](base + k, piece if k in whole else piece.at[parts[0]])

    rows = [row_gather(f, lambda s, f=f: rowbuf.at[f, s], ROW_ID) for f in range(2)]
    cols = [col_gather(f, lambda s, k, f=f: colbuf.at[f, s, k], COL_ID) for f in range(2)]
    sq_rows = row_gather(0, lambda s: sqrow.at[s], SQ_ID)
    sq_cols = col_gather(1, lambda s, k: sqcol.at[s, k], SQ_ID)

    def product(f, left, right):
        sq[f] = jnp.zeros((HALF, BLOCK), F32)

        def step(k, carry):
            sq[f] += jnp.dot(
                left(k), right(k).reshape(BLOCK, BLOCK), preferred_element_type=F32
            )
            return carry

        lax.fori_loop(0, 8, step, 0)

    def square(f):
        product(f, lambda k: rowbuf[f, k], lambda k: colbuf[f, k])
        half = sq[f].astype(BF16)
        if f == 0:
            sqrow[phi] = half
        else:
            sqcol[row_block, c] = half
        for j in range(4):
            k = slice(j * QUARTER, (j + 1) * QUARTER)
            scaled[f, :, k] = (
                4.0 * eye(HALF, j * QUARTER) - 6.0 * scaled[f, :, k] + 4.0 * sq[f, :, k]
            )

    def out_copy(f, b):
        return pltpu.make_async_remote_copy(
            src_ref=obuf.at[f, pl.ds(b * 32, 32)], dst_ref=orecv.at[f, phi],
            send_sem=ssem.at[f, OUT_ID + b], recv_sem=rsem.at[f, OUT_ID + phi],
            device_id=place((out_tok, b)), device_id_type=MESH,
        )

    def cube(f):
        if f == 0:
            product(f, lambda k: sqrow[k], lambda k: colbuf[f, k])
        else:
            product(f, lambda k: rowbuf[f, k], lambda k: sqcol[k])
        obuf[f] = (scaled[f] - sq[f]).astype(BF16)
        for b in range(8):
            me = home & (blk == b)

            @pl.when(me)
            def _():
                orecv[f, phi] = obuf[f, b * 32 : (b + 1) * 32]

            @pl.when(jnp.logical_not(me))
            def _():
                out_copy(f, b).start()

    def emit(f):
        for k in range(8):
            @pl.when(jnp.logical_not(home & (phi == k)))
            def _():
                waits[f](OUT_ID + k, orecv.at[f, k])

        out = (act_out, grad_out)[f]
        for k in range(8):
            out[:, k * BLOCK : (k + 1) * BLOCK] = orecv[f, k].astype(F32)

    load_own(0).wait()
    x_start(0)
    load_own(1).wait()
    column_sums(0)
    column_sums(1)
    sums_start()
    x_forward(0)
    x_start(1)
    totals_start()
    x_finish(0)
    gram(0)
    reduce_start(0)
    x_forward(1)
    reduce_middle(0)
    x_finish(1)
    gram(1)
    reduce_start(1)
    reduce_last(0)
    totals_finish()
    normalise(0)
    rows[0].start()
    cols[0].start()
    reduce_middle(1)
    rows[0].near()
    cols[0].near()
    rows[0].other()
    cols[0].other()
    reduce_last(1)
    rows[0].far()
    cols[0].far()
    normalise(1)
    rows[1].start()
    cols[1].start()
    rows[0].finish()
    cols[0].finish()
    sibling_finish(0, lambda s, k: colbuf.at[0, s, k], COL_ID)
    square(0)
    sq_rows.start()
    rows[1].near()
    cols[1].near()
    rows[1].other()
    cols[1].other()
    sq_rows.near()
    sq_rows.other()
    rows[1].far()
    cols[1].far()
    sq_rows.far()
    rows[1].finish()
    cols[1].finish()
    sibling_finish(1, lambda s, k: colbuf.at[1, s, k], COL_ID)
    square(1)
    sq_cols.start()
    sq_rows.finish()
    cube(0)
    sq_cols.near()
    sq_cols.other()
    sq_cols.far()
    emit(0)
    sq_cols.finish()
    sibling_finish(1, lambda s, k: sqcol.at[s, k], SQ_ID)
    cube(1)
    emit(1)

    for copy in sent:
        copy.wait_send()

    def sums_left(j, carry):
        sum_copy(j).wait_send()
        return carry

    lax.fori_loop(1, 16, sums_left, 0)
    for j in range(4):
        total_copy(j).wait_send()
    for f in range(2):
        for k in range(4):
            d_copy(f, k).wait_send()
        for b in range(8):
            @pl.when(jnp.logical_not(home & (blk == b)))
            def _():
                out_copy(f, b).wait_send()


def body(activations, out_grads):
    hbm = pl.BlockSpec(memory_space=pltpu.HBM)
    vmem = pl.BlockSpec(memory_space=pltpu.VMEM)
    out = jax.ShapeDtypeStruct((32, D), F32)
    tile = (HALF, BLOCK)
    scratch = [
        pltpu.VMEM((2, 4, BLOCK, BLOCK), BF16),
        pltpu.VMEM((2, BLOCK, BLOCK), BF16),
        pltpu.VMEM((2, 4, 2, *tile), BF16),
        pltpu.VMEM((2, 4, 2, *tile), BF16),
        pltpu.VMEM((2, 4, 2, *tile), BF16),
        pltpu.VMEM((2, 2, *tile), BF16),
        pltpu.VMEM((2, 2, *tile), BF16),
        pltpu.VMEM((2, 4, *tile), BF16),
        pltpu.VMEM((2, 4, *tile), BF16),
        pltpu.VMEM((2, 2, *tile), F32),
        pltpu.VMEM((2, *tile), BF16),
        pltpu.VMEM((2, *tile), BF16),
        pltpu.VMEM((2, *tile), F32),
        pltpu.VMEM((2, 8, *tile), BF16),
        pltpu.VMEM((2, 8, 2, *tile), BF16),
        pltpu.VMEM((8, *tile), BF16),
        pltpu.VMEM((8, 2, *tile), BF16),
        pltpu.VMEM((2, *tile), F32),
        pltpu.VMEM((2, *tile), BF16),
        pltpu.VMEM((2, 8, 32, BLOCK), BF16),
        pltpu.VMEM((2, BLOCK), F32),
        pltpu.VMEM((16, 2, BLOCK), F32),
        pltpu.VMEM((5, 2, BLOCK), F32),
        pltpu.SemaphoreType.DMA((2, N_ID)),
        pltpu.SemaphoreType.DMA((2, N_ID)),
        pltpu.SemaphoreType.DMA((16,)),
        pltpu.SemaphoreType.DMA((16,)),
        pltpu.SemaphoreType.DMA((4,)),
        pltpu.SemaphoreType.DMA((4,)),
        pltpu.SemaphoreType.DMA((2,)),
    ]
    return pl.pallas_call(
        kernel,
        out_shape=(out, out),
        in_specs=[hbm, hbm],
        out_specs=(vmem, vmem),
        scratch_shapes=scratch,
        compiler_params=pltpu.CompilerParams(
            collective_id=0, has_side_effects=True, vmem_limit_bytes=62 * 1024 * 1024
        ),
    )(activations, out_grads)


def solution(mesh):
    placed = (P("tok", "blk"), P("tok", "blk"))
    return jax.shard_map(
        body,
        mesh=mesh,
        in_specs=placed,
        out_specs=(P(("tok", "blk"), None), P(("tok", "blk"), None)),
        check_vma=False,
    )
```

time: 492 us -> 162 us (0.33)
  waiting for transfers between devices: 379 us -> 0 us
  Pallas kernels: 0 us -> 156 us
  starting transfers between devices: 41.3 us -> 0 us
  matrix products: 30.8 us -> 0 us
  between operations: 14 us -> 0.65 us
  other arithmetic: 12.2 us -> 0 us
  local copies, waits for them, and re-layouts: 13.4 us -> 2.72 us
    all_gather x3 -> x0, waiting for transfers between devices: 201 us -> none  [the longest x1 123 us: side_by_side(): out = lax.all_gather(both, axis, axis=dim, tiled=True)]
    pallas_call x0 -> x1, Pallas kernels: none -> 156 us  [body(): pl.pallas_call(kernel, out_shape=(out, out), in_specs=[hbm, hbm], out_spe...]
    reduce_scatter x2 -> x0, waiting for transfers between devices: 99.2 us -> none  [damped_tile(): lax.psum_scatter(lax.dot_general(full, local, (((0,), (0,)), ((), ())), p...]
    all_to_all x8 -> x0, waiting for transfers between devices: 78.1 us -> none  [the longest x6 66.5 us: sent_to_all(): lax.all_to_all(jnp.broadcast_to(value[None], (length, *value.shape)), axi...]
    all_to_all x8 -> x0, starting transfers between devices: 41.1 us -> none  [the longest x6 34.2 us: sent_to_all(): lax.all_to_all(jnp.broadcast_to(value[None], (length, *value.shape)), axi...]
    dot_general x6 -> x0, matrix products: 30.8 us -> none  [the longest x2 13.2 us: damped_tile(): lax.dot_general(full, local, (((0,), (0,)), ((), ())), preferred_element_...]
    broadcast_in_dim x7 -> x0, local copies, waits for them, and re-layouts: 6.93 us -> none  [sent_to_all(): jnp.broadcast_to(value[None], (length, *value.shape))]
  transfers between devices with their start and end apart: 13 -> 0, of which waited for: 11 -> 0; matrix products, arithmetic and copies ran while one was open for 8% -> 0% of each run, Pallas kernels for 0% -> 0%
where the time goes in v1:
time: 162 us; the launch traced here: 159 us
  Pallas kernels  156 us (96%)
  local copies, waits for them, and re-layouts  2.72 us (2%)
    pallas_call x1, Pallas kernels, body(): pl.pallas_call(kernel, out_shape=(out, out), in_specs=[hbm, hbm], out_spe...  156 us

profile of v1, /device:TPU:0, one launch (start us, length us, event | category | flops | bytes accessed | tf_op | source)
XLA Modules:
  0.0 159.4 jit_solution(2003033405789320764)
XLA Ops:
  0.6 156.1 %shard_map.41 = (f32[32,4096]{1,0:T(8,128)}, f32[32,4096]{1,0:T(8,128)}) custom-call(bf16[512,512]{1,0:T(8,128)(2,1)} %act_ref.1, bf16[512,512]{1,0:T(8,128)(2,1)} %grad_ref.1), custom_call_target="tpu_custom_call" | custom-call | tf_op jit(solution)/shard_map/pallas_call | solution.py:548
  156.7 0.0 copy-start
  156.7 1.9 %copy.6 = f32[32,4096]{1,0:T(8,128)} copy(f32[32,4096]{1,0:T(8,128)} %get-tuple-element.4) | data formatting | bytes 1048576
  158.6 0.0 copy-done
  158.6 0.8 copy.7
Async XLA Ops:
  156.7 1.9 %copy-start = (f32[32,4096]{1,0:T(8,128)S(1)}, f32[32,4096]{1,0:T(8,128)}, u32[]{:S(2)}) copy-start(f32[32,4096]{1,0:T(8,128)} %get-tuple-element.5) | copy-start | bytes 1572868

commit v2 on v1

v2 whole, which is shorter than its diff:
```python
import jax
import jax.numpy as jnp
from jax import lax
from jax.experimental import pallas as pl
from jax.experimental.pallas import tpu as pltpu
from jax.sharding import PartitionSpec as P

D = 4096
TOKENS = 8192
BLOCK = 512
HALF = 256
QUARTER = 128

damping = 0.3
epsilon = 1e-06
divisor = 2.0

MESH = pl.DeviceIdType.MESH
F32 = jnp.float32
BF16 = jnp.bfloat16

NX_ID = 20
D_ID = 0
Y1_ID = 4
Y2_ID = 6
ROW_ID = 10
COL_ID = 14
SQ_ID = 33
OUT_ID = 37
N_ID = 45


class Line:
    def __init__(self, send, wait, base, ref, plus, minus):
        self.send, self.wait, self.base, self.ref = send, wait, base, ref
        self.plus, self.minus = plus, minus

    def put(self, k, place, to):
        r = self.ref(*place)
        self.send(self.base + k, r, r, to)

    def take(self, k):
        self.wait(self.base + k, self.ref(*[(3, None), (1, None), (2, 0), (2, 1)][k]))

    def start(self):
        self.put(0, (0, None), self.plus)
        self.put(1, (0, None), self.minus)

    def near(self):
        self.take(0)
        self.put(2, (3, 0), self.plus)
        self.take(1)
        self.put(3, (1, 1), self.minus)

    def finish(self):
        self.take(2)
        self.take(3)


class Gather:
    def __init__(self, send, wait, base, ref, plus, minus, across, via_z, pass_on=None):
        self.send, self.wait, self.base, self.ref = send, wait, base, ref
        self.plus, self.minus, self.across, self.via_z = plus, minus, across, via_z
        self.pass_on = pass_on

    def incoming(self, k):
        return [
            (3, 0, None), (1, 0, None), (0, 1, None), (2, 0, 0), (2, 0, 1),
            (3, 1, None), (1, 1, None), (2, 1, 0), (2, 1, 1),
        ][k]

    def put(self, k, place, to):
        r = self.ref(*place)
        self.send(self.base + k, r, r, to)

    def take(self, k):
        r = self.ref(*self.incoming(k))
        self.wait(self.base + k, r)
        if self.pass_on is not None:
            self.pass_on(self.base + 10 + k, r)

    def start(self):
        own = (0, 0, None)
        self.put(0, own, self.plus)
        self.put(1, own, self.minus)
        self.put(2, own, self.across)
        if self.pass_on is not None:
            self.pass_on(self.base + 9, self.ref(*own))

    def near(self):
        self.take(0)
        self.put(3, (3, 0, 0), self.plus)
        self.take(1)
        self.put(4, (1, 0, 1), self.minus)

    def other(self):
        self.take(2)
        self.put(5, (0, 1, None), self.plus)
        self.put(6, (0, 1, None), self.minus)

    def far(self):
        if self.via_z:
            self.take(3)
            self.put(7, (2, 0, 0), self.across)
            self.take(4)
            self.put(8, (2, 0, 1), self.across)
        else:
            self.take(5)
            self.put(7, (3, 1, 0), self.plus)
            self.take(6)
            self.put(8, (1, 1, 1), self.minus)

    def finish(self):
        for k in (5, 6, 7, 8) if self.via_z else (3, 4, 7, 8):
            self.take(k)


def kernel(
    act_ref, grad_ref, act_out, grad_out,
    xall, give, acc, dsend, drecv, y1s, y1r, y2s, y2r, scaled,
    rowbuf, colbuf, sqrow, sq, obuf, orecv, csend, crecv, totbuf,
    xssem, xrsem, ssem, rsem, csem, crsem, tsem, trsem, lsem,
):
    tok, blk = lax.axis_index("tok"), lax.axis_index("blk")
    c, y, zl = tok % 2, (tok // 2) % 4, tok // 8
    x, zh = blk // 2, blk % 2

    def tok_of(zl_, y_, c_):
        return zl_ * 8 + y_ * 2 + c_

    def blk_of(x_, zh_):
        return x_ * 2 + zh_

    x_plus = (tok, blk_of((x + 1) % 4, zh))
    x_minus = (tok, blk_of((x + 3) % 4, zh))
    zh_mate = (tok, blk_of(x, 1 - zh))
    y_plus = (tok_of(zl, (y + 1) % 4, c), blk)
    y_minus = (tok_of(zl, (y + 3) % 4, c), blk)
    zl_mate = (tok_of(1 - zl, y, c), blk)
    z_cross = (tok_of(1 - zl, y, c), blk_of(x, 1 - zh))
    sibling = (tok_of(zl, y, 1 - c), blk)

    def place(to):
        return {"tok": to[0], "blk": to[1]}

    out_tok = 4 * y + 2 * zh + c
    home = out_tok == tok
    line_slot = 2 * x + zl
    row_block = 2 * y + zh

    barrier = pltpu.get_barrier_semaphore()

    def greet(to):
        pl.semaphore_signal(barrier, inc=1, device_id=place(to), device_id_type=MESH)

    def greet_tok(j, carry):
        greet(((tok + j) % 16, blk))
        return carry

    def greet_blk(j, carry):
        greet((tok, (blk + j) % 8))
        return carry

    lax.fori_loop(1, 16, greet_tok, 0)
    lax.fori_loop(1, 8, greet_blk, 0)
    greet(z_cross)

    def greet_source(j, carry):
        to = (tok_of(j % 2, tok // 4, c), blk_of(j // 2, (tok // 2) % 2))

        @pl.when(jnp.logical_not((to[0] == tok) & (to[1] == blk)))
        def _():
            greet(to)

        return carry

    lax.fori_loop(0, 8, greet_source, 0)

    def load(src, dst, k):
        return pltpu.make_async_copy(src, dst, lsem.at[k])

    @pl.when(zl == 0)
    def _():
        load(act_ref, xall.at[0, x], 0).start()
        load(grad_ref, give, 1).start()

    @pl.when(zl == 1)
    def _():
        load(grad_ref, xall.at[0, x], 0).start()
        load(act_ref, give, 1).start()

    pl.semaphore_wait(barrier, 15 + 7 + 1 + 8 - home.astype(jnp.int32))

    sent = []

    def sender(ss, rs):
        def send(k, src, dst, to):
            copy = pltpu.make_async_remote_copy(
                src_ref=src, dst_ref=dst, send_sem=ss.at[k], recv_sem=rs.at[k],
                device_id=place(to), device_id_type=MESH,
            )
            copy.start()
            sent.append(copy)

        return send

    def waiter(ss, rs):
        def wait(k, dst):
            pltpu.make_async_remote_copy(
                src_ref=dst, dst_ref=dst, send_sem=ss.at[k], recv_sem=rs.at[k],
                device_id=place(sibling), device_id_type=MESH,
            ).wait_recv()

        return wait

    x_send, x_wait = sender(xssem, xrsem), waiter(xssem, xrsem)
    sends = [sender(ssem.at[h], rsem.at[h]) for h in range(2)]
    waits = [waiter(ssem.at[h], rsem.at[h]) for h in range(2)]

    token_half = (pl.ds(0, HALF), pl.ds(HALF, HALF))

    def x_block(t, step, half):
        return xall.at[t, (x + step) % 4, token_half[half]]

    def x_put(t, k):
        step, half, to = [
            (0, 0, x_plus), (0, 1, x_plus), (0, 1, x_minus), (0, 0, x_minus),
            (3, 0, x_plus), (1, 1, x_minus),
        ][k]
        r = x_block(t, step, half)
        x_send(8 * t + k, r, r, to)

    def x_take(t, k):
        step, half = [(3, 0), (3, 1), (1, 1), (1, 0), (2, 0), (2, 1)][k]
        x_wait(8 * t + k, x_block(t, step, half))

    def z_start():
        for half in range(2):
            x_send(18 + half, give.at[token_half[half]], x_block(1, 0, half), zl_mate)

    def z_rest():
        x_send(17, give, xall.at[1, 4], z_cross)
        x_send(16, xall.at[0, x], xall.at[0, 4], zh_mate)

    def column_sums():
        def of(ref):
            values = ref.astype(F32)
            return jnp.sum(values * values, axis=0, keepdims=True)

        csend[zl] = of(xall[0, x])
        csend[1 - zl] = of(give[...])

    def sum_copy(j):
        return pltpu.make_async_remote_copy(
            src_ref=csend, dst_ref=crecv.at[j], send_sem=csem.at[j], recv_sem=crsem.at[j],
            device_id=place(((tok + j) % 16, blk)), device_id_type=MESH,
        )

    def sums_start():
        def step(j, carry):
            sum_copy(j).start()
            return carry

        lax.fori_loop(1, 16, step, 0)

    total_to = [(tok, blk_of((x + j) % 4, zh)) for j in (1, 2, 3)] + [zh_mate]

    def total_copy(j):
        slot = x if j < 3 else 4
        return pltpu.make_async_remote_copy(
            src_ref=totbuf.at[x], dst_ref=totbuf.at[slot], send_sem=tsem.at[j],
            recv_sem=trsem.at[j], device_id=place(total_to[j]), device_id_type=MESH,
        )

    def totals_start():
        def step(j, carry):
            sum_copy(j).wait_recv()
            return carry

        lax.fori_loop(1, 16, step, 0)
        total = csend[...]
        for j in range(1, 16):
            total = total + crecv[j]
        totbuf[x] = total
        for j in range(4):
            total_copy(j).start()

    def totals_finish():
        for j in range(4):
            total_copy(j).wait_recv()

    mine = pl.ds(pl.multiple_of(c * HALF, HALF), HALF)
    theirs = pl.ds(pl.multiple_of((1 - c) * HALF, HALF), HALF)
    col_slot = [jnp.where(zh == h, x, 4) for h in range(2)]

    def product_of(t, to, h, part):
        return lax.dot_general(
            xall[t, to, :, part], xall[t, col_slot[h]], (((0,), (0,)), ((), ())),
            preferred_element_type=F32,
        )

    def gram_first():
        def step(to, carry):
            for h in range(2):
                acc[h, to, 0] = product_of(0, to, h, mine)
                acc[h, to, 1] = product_of(0, to, h, theirs)
            return carry

        lax.fori_loop(0, 4, step, 0)

    def gram_second(begin, end):
        def step(i, carry):
            to = (x + 3 + i) % 4
            for h in range(2):
                dsend[h, to] = (acc[h, to, 1] + product_of(1, to, h, theirs)).astype(BF16)
                d_copy(h, to).start()
            for h in range(2):
                acc[h, to, 0] = acc[h, to, 0] + product_of(1, to, h, mine)
            return carry

        lax.fori_loop(begin, end, step, 0)

    def d_copy(h, to):
        return pltpu.make_async_remote_copy(
            src_ref=dsend.at[h, to], dst_ref=drecv.at[h, to], send_sem=ssem.at[h, D_ID + to],
            recv_sem=rsem.at[h, D_ID + to], device_id=place(sibling), device_id_type=MESH,
        )

    lo, hi = pl.ds(0, QUARTER), pl.ds(QUARTER, QUARTER)

    def both(h, to, part):
        return acc[h, to, 0, part] + drecv[h, to, part].astype(F32)

    y_far, y_up, y_down = (y + 2) % 4, (y + 1) % 4, (y + 3) % 4

    def reduce_start(h):
        d_copy(h, y_far).wait_recv()
        y1s[h, 0] = both(h, y_far, lo).astype(BF16)
        sends[h](Y1_ID + 0, y1s.at[h, 0], y1r.at[h, 0], y_plus)
        y1s[h, 1] = both(h, y_far, hi).astype(BF16)
        sends[h](Y1_ID + 1, y1s.at[h, 1], y1r.at[h, 1], y_minus)
        d_copy(h, y_up).wait_recv()
        y2s[h, 0] = both(h, y_up, hi).astype(BF16)
        sends[h](Y2_ID + 0, y2s.at[h, 0], y2r.at[h, 0], y_plus)
        d_copy(h, y_down).wait_recv()
        y2s[h, 2] = both(h, y_down, lo).astype(BF16)
        sends[h](Y2_ID + 2, y2s.at[h, 2], y2r.at[h, 2], y_minus)
        d_copy(h, y).wait_recv()

    def reduce_middle(h):
        waits[h](Y1_ID + 0, y1r.at[h, 0])
        y2s[h, 1] = (both(h, y_up, lo) + y1r[h, 0].astype(F32)).astype(BF16)
        sends[h](Y2_ID + 1, y2s.at[h, 1], y2r.at[h, 1], y_plus)
        waits[h](Y1_ID + 1, y1r.at[h, 1])
        y2s[h, 3] = (both(h, y_down, hi) + y1r[h, 1].astype(F32)).astype(BF16)
        sends[h](Y2_ID + 3, y2s.at[h, 3], y2r.at[h, 3], y_minus)

    def eye(h, start_col):
        shape = (HALF, QUARTER)
        r = lax.broadcasted_iota(jnp.int32, shape, 0) + BLOCK * row_block + HALF * c
        k = lax.broadcasted_iota(jnp.int32, shape, 1) + BLOCK * (2 * x + h) + start_col
        return (r == k).astype(F32)

    def inverse(sums):
        return lax.rsqrt(sums / TOKENS + epsilon)

    def normalise(h):
        for k in range(4):
            waits[h](Y2_ID + k, y2r.at[h, k])
        inv_col = inverse(totbuf[col_slot[h], zl])
        inv_row = inverse(totbuf[y, zl, :, mine])
        inv_row = jnp.transpose(jnp.broadcast_to(inv_row, (QUARTER, HALF)))
        acc[h, y, 0, lo] = both(h, y, lo) + y2r[h, 1].astype(F32) + y2r[h, 2].astype(F32)
        acc[h, y, 0, hi] = both(h, y, hi) + y2r[h, 0].astype(F32) + y2r[h, 3].astype(F32)
        for j in range(4):
            k = slice(j * QUARTER, (j + 1) * QUARTER)
            g = acc[h, y, 0, :, k]
            damped = g / TOKENS * inv_row * inv_col[:, k] + damping * eye(h, j * QUARTER)
            value = damped / divisor
            scaled[h, :, k] = value
            rowbuf[2 * x + h, :, k] = value.astype(BF16)
            colbuf[h, row_block, c, :, k] = value.astype(BF16)

    parts = (lo, hi)

    def row_line(h, buf, base):
        def ref(step, part):
            piece = buf.at[((x + step) % 4) * 2 + h]
            return piece if part is None else piece.at[parts[part]]

        return Line(sends[h], waits[h], base, ref, x_plus, x_minus)

    def col_gather(h):
        def ref(step, other, part):
            piece = colbuf.at[h, ((y + step) % 4) * 2 + (1 - zh if other else zh), c]
            return piece if part is None else piece.at[parts[part]]

        def pass_on(k, r):
            sends[h](k, r, r, sibling)

        return Gather(
            sends[h], waits[h], COL_ID, ref, y_plus, y_minus, zh_mate, True, pass_on
        )

    def sibling_finish(h):
        whole = [9, 10, 11, 12, 15, 16]
        for k in range(9, 19):
            piece = colbuf.at[h, 0, 1 - c]
            waits[h](COL_ID + k, piece if k in whole else piece.at[lo])

    rows = [row_line(h, rowbuf, ROW_ID) for h in range(2)]
    cols = [col_gather(h) for h in range(2)]
    sq_rows = [row_line(h, sqrow, SQ_ID) for h in range(2)]

    def product(h, left):
        sq[h] = jnp.zeros((HALF, BLOCK), F32)

        def step(k, carry):
            sq[h] += jnp.dot(
                left[k], colbuf[h, k].reshape(BLOCK, BLOCK), preferred_element_type=F32
            )
            return carry

        lax.fori_loop(0, 8, step, 0)

    def square(h):
        product(h, rowbuf)
        sqrow[2 * x + h] = sq[h].astype(BF16)
        sq_rows[h].start()
        for j in range(4):
            k = slice(j * QUARTER, (j + 1) * QUARTER)
            scaled[h, :, k] = (
                4.0 * eye(h, j * QUARTER) - 6.0 * scaled[h, :, k] + 4.0 * sq[h, :, k]
            )

    def out_copy(h, b):
        return pltpu.make_async_remote_copy(
            src_ref=obuf.at[h, pl.ds(b * 32, 32)], dst_ref=orecv.at[h, line_slot],
            send_sem=ssem.at[h, OUT_ID + b], recv_sem=rsem.at[h, OUT_ID + line_slot],
            device_id=place((out_tok, b)), device_id_type=MESH,
        )

    def cube(h):
        product(h, sqrow)
        obuf[h] = (scaled[h] - sq[h]).astype(BF16)
        for b in range(8):
            me = home & (blk == b)

            @pl.when(me)
            def _():
                orecv[h, line_slot] = obuf[h, b * 32 : (b + 1) * 32]

            @pl.when(jnp.logical_not(me))
            def _():
                out_copy(h, b).start()

    def emit(h):
        for k in range(8):
            @pl.when(jnp.logical_not(home & (line_slot == k)))
            def _():
                waits[h](OUT_ID + k, orecv.at[h, k])

        for k in range(8):
            out = (act_out, grad_out)[k % 2]
            start = (2 * (k // 2) + h) * BLOCK
            out[:, start : start + BLOCK] = orecv[h, k].astype(F32)

    load(act_ref, give, 1).wait()
    z_start()
    load(act_ref, give, 0).wait()
    x_put(0, 0)
    x_put(0, 2)
    x_put(0, 1)
    x_put(0, 3)
    z_rest()
    column_sums()
    sums_start()
    x_take(0, 0)
    x_put(0, 4)
    x_take(0, 2)
    x_put(0, 5)
    x_wait(18, x_block(1, 0, 0))
    x_put(1, 0)
    x_wait(19, x_block(1, 0, 1))
    x_put(1, 2)
    x_put(1, 1)
    x_put(1, 3)
    totals_start()
    x_take(0, 1)
    x_take(0, 3)
    x_take(0, 4)
    x_take(0, 5)
    x_wait(16, xall.at[0, 4])
    gram_first()
    x_take(1, 0)
    x_put(1, 4)
    x_take(1, 2)
    x_put(1, 5)
    x_wait(17, xall.at[1, 4])
    x_take(1, 1)
    x_take(1, 3)
    gram_second(0, 3)
    x_take(1, 4)
    x_take(1, 5)
    gram_second(3, 4)
    reduce_start(0)
    reduce_start(1)
    reduce_middle(0)
    reduce_middle(1)
    totals_finish()
    normalise(0)
    cols[0].start()
    rows[0].start()
    normalise(1)
    rows[1].start()
    cols[0].near()
    cols[0].other()
    cols[1].start()
    rows[0].near()
    rows[1].near()
    cols[0].far()
    cols[1].near()
    cols[1].other()
    rows[0].finish()
    rows[1].finish()
    cols[0].finish()
    sibling_finish(0)
    square(0)
    cols[1].far()
    sq_rows[0].near()
    cols[1].finish()
    sibling_finish(1)
    square(1)
    sq_rows[0].finish()
    sq_rows[1].near()
    sq_rows[1].finish()
    cube(0)
    cube(1)
    emit(0)
    emit(1)

    for copy in sent:
        copy.wait_send()

    def sums_left(j, carry):
        sum_copy(j).wait_send()
        return carry

    lax.fori_loop(1, 16, sums_left, 0)
    for j in range(4):
        total_copy(j).wait_send()
    for h in range(2):
        for k in range(4):
            d_copy(h, k).wait_send()
        for b in range(8):
            @pl.when(jnp.logical_not(home & (blk == b)))
            def _():
                out_copy(h, b).wait_send()


def body(activations, out_grads):
    hbm = pl.BlockSpec(memory_space=pltpu.HBM)
    vmem = pl.BlockSpec(memory_space=pltpu.VMEM)
    out = jax.ShapeDtypeStruct((32, D), F32)
    tile = (HALF, BLOCK)
    part = (QUARTER, BLOCK)
    scratch = [
        pltpu.VMEM((2, 5, BLOCK, BLOCK), BF16),
        pltpu.VMEM((BLOCK, BLOCK), BF16),
        pltpu.VMEM((2, 4, 2, *tile), F32),
        pltpu.VMEM((2, 4, *tile), BF16),
        pltpu.VMEM((2, 4, *tile), BF16),
        pltpu.VMEM((2, 2, *part), BF16),
        pltpu.VMEM((2, 2, *part), BF16),
        pltpu.VMEM((2, 4, *part), BF16),
        pltpu.VMEM((2, 4, *part), BF16),
        pltpu.VMEM((2, *tile), F32),
        pltpu.VMEM((8, *tile), BF16),
        pltpu.VMEM((2, 8, 2, *tile), BF16),
        pltpu.VMEM((8, *tile), BF16),
        pltpu.VMEM((2, *tile), F32),
        pltpu.VMEM((2, *tile), BF16),
        pltpu.VMEM((2, 8, 32, BLOCK), BF16),
        pltpu.VMEM((2, 1, BLOCK), F32),
        pltpu.VMEM((16, 2, 1, BLOCK), F32),
        pltpu.VMEM((5, 2, 1, BLOCK), F32),
        pltpu.SemaphoreType.DMA((NX_ID,)),
        pltpu.SemaphoreType.DMA((NX_ID,)),
        pltpu.SemaphoreType.DMA((2, N_ID)),
        pltpu.SemaphoreType.DMA((2, N_ID)),
        pltpu.SemaphoreType.DMA((16,)),
        pltpu.SemaphoreType.DMA((16,)),
        pltpu.SemaphoreType.DMA((4,)),
        pltpu.SemaphoreType.DMA((4,)),
        pltpu.SemaphoreType.DMA((2,)),
    ]
    return pl.pallas_call(
        kernel,
        out_shape=(out, out),
        in_specs=[hbm, hbm],
        out_specs=(vmem, vmem),
        scratch_shapes=scratch,
        compiler_params=pltpu.CompilerParams(
            collective_id=0, has_side_effects=True, vmem_limit_bytes=62 * 1024 * 1024
        ),
    )(activations, out_grads)


def solution(mesh):
    placed = (P("tok", "blk"), P("tok", "blk"))
    return jax.shard_map(
        body,
        mesh=mesh,
        in_specs=placed,
        out_specs=(P(("tok", "blk"), None), P(("tok", "blk"), None)),
        check_vma=False,
    )
```

time: 162 us -> 139 us (0.86)
  the two profiles are of different devices: /device:TPU:0 before, /device:TPU:24 now
where the time goes in v2:
time: 139 us
  Pallas kernels  136 us (98%)
  local copies, waits for them, and re-layouts  2.72 us (2%)
    pallas_call x1, Pallas kernels, body(): pl.pallas_call(kernel, out_shape=(out, out), in_specs=[hbm, hbm], out_spe...  136 us

profile of v2, /device:TPU:24, one launch (start us, length us, event | category | flops | bytes accessed | tf_op | source)
XLA Modules:
  0.0 139.1 jit_solution(16461432037570470515)
XLA Ops:
  0.6 135.8 %shard_map.41 = (f32[32,4096]{1,0:T(8,128)}, f32[32,4096]{1,0:T(8,128)}) custom-call(bf16[512,512]{1,0:T(8,128)(2,1)} %act_ref.1, bf16[512,512]{1,0:T(8,128)(2,1)} %grad_ref.1), custom_call_target="tpu_custom_call" | custom-call | tf_op jit(solution)/shard_map/pallas_call | solution.py:597
  136.4 0.0 copy-start
  136.4 1.9 %copy.6 = f32[32,4096]{1,0:T(8,128)} copy(f32[32,4096]{1,0:T(8,128)} %get-tuple-element.4) | data formatting | bytes 1048576
  138.3 0.0 copy-done
  138.3 0.8 copy.7
Async XLA Ops:
  136.4 1.9 %copy-start = (f32[32,4096]{1,0:T(8,128)S(1)}, f32[32,4096]{1,0:T(8,128)}, u32[]{:S(2)}) copy-start(f32[32,4096]{1,0:T(8,128)} %get-tuple-element.5) | copy-start | bytes 1572868

commit v3 on v0

v3 whole, which is shorter than its diff:
```python
import jax
import jax.numpy as jnp
from jax import lax
from jax.experimental import pallas as pl
from jax.experimental.pallas import tpu as pltpu
from jax.sharding import PartitionSpec as P

D = 4096
TOKENS = 8192
BLOCK = 512
HALF = 256
PART = 128

damping = 0.3
epsilon = 1e-06
divisor = 2.0

MESH = pl.DeviceIdType.MESH
F32 = jnp.float32
BF16 = jnp.bfloat16


class Ids:
    def __init__(self):
        self.next = 0

    def take(self, n):
        first = self.next
        self.next += n
        return first


IDS = Ids()
Z_ID = IDS.take(6)
X_ID = [[IDS.take(6) for _ in range(2)] for _ in range(2)]
D_ID = [IDS.take(4) for _ in range(2)]
Y1_ID = [IDS.take(2) for _ in range(2)]
Y2_ID = [IDS.take(4) for _ in range(2)]
ROW_ID = [IDS.take(6) for _ in range(2)]
COL_ID = [IDS.take(23) for _ in range(3)]
SQ_ID = [IDS.take(6) for _ in range(2)]
OUT_ID = [IDS.take(8) for _ in range(2)]
SUM_ID = IDS.take(16)
TOTAL_ID = IDS.take(4)
N_ID = IDS.next


class Line:
    arrivals = [(3, 0), (3, 1), (1, 1), (1, 0), (2, 0), (2, 1)]

    def __init__(self, send, wait, base, ref, plus, minus, arrived=None):
        self.send, self.wait, self.base, self.ref = send, wait, base, ref
        self.plus, self.minus, self.arrived = plus, minus, arrived

    def put(self, k, where, to):
        r = self.ref(*where)
        self.send(self.base + k, r, r, to)

    def take(self, k):
        r = self.ref(*self.arrivals[k])
        self.wait(self.base + k, r)
        if self.arrived is not None:
            self.arrived(k, r)

    def start(self):
        self.put(0, (0, 0), self.plus)
        self.put(2, (0, 1), self.minus)
        self.put(1, (0, 1), self.plus)
        self.put(3, (0, 0), self.minus)

    def near(self):
        self.take(0)
        self.put(4, (3, 0), self.plus)
        self.take(2)
        self.put(5, (1, 1), self.minus)

    def finish(self):
        for k in (1, 3, 4, 5):
            self.take(k)


class Plane(Line):
    arrivals = Line.arrivals + [
        (0, None, 1), (3, None, 1), (1, None, 1), (2, 0, 1), (2, 1, 1)
    ]

    def __init__(self, send, wait, base, ref, plus, minus, across, sibling, mirrored):
        super().__init__(send, wait, base, ref, plus, minus, self.pass_on)
        self.across, self.sibling, self.mirrored = across, sibling, mirrored

    def pass_on(self, k, r):
        self.send(self.base + 12 + k, r, r, self.sibling)

    def start(self):
        super().start()
        self.put(6, (0, None, 0), self.across)
        self.send(self.base + 11, self.ref(0, None, 0), self.ref(0, None, 0), self.sibling)

    def other(self):
        self.take(6)
        self.put(7, (0, None, 1), self.plus)
        self.put(8, (0, None, 1), self.minus)

    def far(self):
        self.take(4)
        self.put(9, (2, 0, 0), self.across)
        self.take(5)
        self.put(10, (2, 1, 0), self.across)

    def finish(self):
        for k in (1, 3, 7, 8, 9, 10):
            self.take(k)
        for k in range(11, 23):
            half = None if k in (11, 18, 19, 20) else 0
            self.wait(self.base + k, self.mirrored(half))


def kernel(
    act_ref, grad_ref, act_out, grad_out,
    xall, give, gram_part, drecv, y1s, y1r, y2s, y2r, scaled,
    rowbuf, colbuf, sqrow, sq, obuf, orecv, csend, crecv, totbuf,
    ssem, rsem, lsem,
):
    tok, blk = lax.axis_index("tok"), lax.axis_index("blk")
    c, y, zl = tok % 2, (tok // 2) % 4, tok // 8
    x, zh = blk // 2, blk % 2

    def tok_of(zl_, y_, c_):
        return zl_ * 8 + y_ * 2 + c_

    def blk_of(x_, zh_):
        return x_ * 2 + zh_

    x_plus = (tok, blk_of((x + 1) % 4, zh))
    x_minus = (tok, blk_of((x + 3) % 4, zh))
    zh_mate = (tok, blk_of(x, 1 - zh))
    y_plus = (tok_of(zl, (y + 1) % 4, c), blk)
    y_minus = (tok_of(zl, (y + 3) % 4, c), blk)
    zl_mate = (tok_of(1 - zl, y, c), blk)
    z_cross = (tok_of(1 - zl, y, c), blk_of(x, 1 - zh))
    sibling = (tok_of(zl, y, 1 - c), blk)

    def place(to):
        return {"tok": to[0], "blk": to[1]}

    out_tok = 4 * y + 2 * zh + c
    home = out_tok == tok
    line_slot = 2 * x + zl
    row_block = 2 * y + zh

    def loads(src, dst, first):
        out = []
        for s in range(2):
            for k in range(2):
                cols = pl.ds(HALF * k + PART * s, PART)
                out.append(
                    pltpu.make_async_copy(
                        src.at[:, cols], dst(s).at[:, pl.ds(PART * k, PART)],
                        lsem.at[first + 2 * s + k],
                    )
                )
        return out

    def own_block(s):
        return xall.at[0, x, s]

    def give_block(s):
        return give.at[s]

    def all_loads(own_ref, give_ref):
        return loads(own_ref, own_block, 0) + loads(give_ref, give_block, 4)

    @pl.when(zl == 0)
    def _():
        for copy in all_loads(act_ref, grad_ref):
            copy.start()

    @pl.when(zl == 1)
    def _():
        for copy in all_loads(grad_ref, act_ref):
            copy.start()

    barrier = pltpu.get_barrier_semaphore()

    def greet(to):
        pl.semaphore_signal(barrier, inc=1, device_id=place(to), device_id_type=MESH)

    def greet_tok(j, carry):
        greet(((tok + j) % 16, blk))
        return carry

    def greet_blk(j, carry):
        greet((tok, (blk + j) % 8))
        return carry

    lax.fori_loop(1, 16, greet_tok, 0)
    lax.fori_loop(1, 8, greet_blk, 0)
    greet(z_cross)

    def greet_source(j, carry):
        to = (tok_of(j % 2, tok // 4, c), blk_of(j // 2, (tok // 2) % 2))

        @pl.when(jnp.logical_not((to[0] == tok) & (to[1] == blk)))
        def _():
            greet(to)

        return carry

    lax.fori_loop(0, 8, greet_source, 0)
    for copy in all_loads(act_ref, grad_ref):
        copy.wait()
    pl.semaphore_wait(barrier, 15 + 7 + 1 + 8 - home.astype(jnp.int32))

    sent = []

    def remote(k, src, dst, to, k_there=None):
        return pltpu.make_async_remote_copy(
            src_ref=src, dst_ref=dst, send_sem=ssem.at[k],
            recv_sem=rsem.at[k if k_there is None else k_there],
            device_id=place(to), device_id_type=MESH,
        )

    def send(k, src, dst, to):
        copy = remote(k, src, dst, to)
        copy.start()
        sent.append(copy)

    def wait(k, dst):
        remote(k, dst, dst, sibling).wait_recv()

    token_half = (pl.ds(0, HALF), pl.ds(HALF, HALF))

    def x_line(s, t):
        def ref(step, half):
            return xall.at[t, (x + step) % 4, s, token_half[half]]

        return Line(send, wait, X_ID[s][t], ref, x_plus, x_minus)

    lines = [[x_line(s, t) for t in range(2)] for s in range(2)]

    def z_first(s):
        send(Z_ID + s, give.at[s], xall.at[1, x, s], zl_mate)

    def z_rest(s):
        send(Z_ID + 2 + s, give.at[s], xall.at[1, 4, s], z_cross)
        send(Z_ID + 4 + s, xall.at[0, x, s], xall.at[0, 4, s], zh_mate)

    def z_first_take(s):
        wait(Z_ID + s, xall.at[1, x, s])

    def z_rest_take(s):
        wait(Z_ID + 2 + s, xall.at[1, 4, s])
        wait(Z_ID + 4 + s, xall.at[0, 4, s])

    def column_sums():
        for which, ref in ((zl, own_block), (1 - zl, give_block)):
            for s in range(2):
                values = ref(s)[...].astype(F32)
                total = jnp.sum(values * values, axis=0, keepdims=True)
                for k in range(2):
                    csend[which, :, HALF * k + PART * s : HALF * k + PART * (s + 1)] = total[
                        :, PART * k : PART * (k + 1)
                    ]

    def sum_copy(j):
        return remote(SUM_ID + j, csend, crecv.at[j], ((tok + j) % 16, blk))

    def sums_start():
        def step(j, carry):
            sum_copy(j).start()
            return carry

        lax.fori_loop(1, 16, step, 0)

    total_to = [(tok, blk_of((x + j) % 4, zh)) for j in (1, 2, 3)] + [zh_mate]

    def total_copy(j):
        return remote(TOTAL_ID + j, totbuf.at[x], totbuf.at[x if j < 3 else 4], total_to[j])

    def totals_start():
        def step(j, carry):
            sum_copy(j).wait_recv()
            return carry

        lax.fori_loop(1, 16, step, 0)
        total = csend[...]
        for j in range(1, 16):
            total = total + crecv[j]
        totbuf[x] = total
        for j in range(4):
            total_copy(j).start()

    def totals_finish():
        for j in range(4):
            total_copy(j).wait_recv()

    col_slot = [jnp.where(zh == h, x, 4) for h in range(2)]

    def gram(s):
        def step(i, carry):
            to = (x + 3 + i) % 4
            for h in range(2):
                for s2 in range(2):
                    value = None
                    for t in range(2):
                        term = lax.dot_general(
                            xall[t, to, s], xall[t, col_slot[h], s2],
                            (((0,), (0,)), ((), ())), preferred_element_type=F32,
                        )
                        value = term if value is None else value + term
                    value = value.astype(BF16)
                    for k in range(2):
                        for k2 in range(2):
                            start = HALF * k2 + PART * s2
                            gram_part[s, to, k, h, :, start : start + PART] = value[
                                PART * k : PART * (k + 1), PART * k2 : PART * (k2 + 1)
                            ]
            d_copy(s, to).start()
            return carry

        lax.fori_loop(0, 4, step, 0)

    def d_copy(s, to):
        return remote(
            D_ID[s] + to, gram_part.at[s, to, 1 - c], drecv.at[s, to], sibling
        )

    def both(s, to, h):
        return gram_part[s, to, c, h].astype(F32) + drecv[s, to, h].astype(F32)

    y_far, y_up, y_down = (y + 2) % 4, (y + 1) % 4, (y + 3) % 4

    def reduce_start(s):
        d_copy(s, y_far).wait_recv()
        y1s[s, 0] = both(s, y_far, 0).astype(BF16)
        send(Y1_ID[s] + 0, y1s.at[s, 0], y1r.at[s, 0], y_plus)
        y1s[s, 1] = both(s, y_far, 1).astype(BF16)
        send(Y1_ID[s] + 1, y1s.at[s, 1], y1r.at[s, 1], y_minus)
        d_copy(s, y_up).wait_recv()
        y2s[s, 0] = both(s, y_up, 1).astype(BF16)
        send(Y2_ID[s] + 0, y2s.at[s, 0], y2r.at[s, 0], y_plus)
        d_copy(s, y_down).wait_recv()
        y2s[s, 2] = both(s, y_down, 0).astype(BF16)
        send(Y2_ID[s] + 2, y2s.at[s, 2], y2r.at[s, 2], y_minus)
        d_copy(s, y).wait_recv()

    def reduce_middle(s):
        wait(Y1_ID[s] + 0, y1r.at[s, 0])
        y2s[s, 1] = (both(s, y_up, 0) + y1r[s, 0].astype(F32)).astype(BF16)
        send(Y2_ID[s] + 1, y2s.at[s, 1], y2r.at[s, 1], y_plus)
        wait(Y1_ID[s] + 1, y1r.at[s, 1])
        y2s[s, 3] = (both(s, y_down, 1) + y1r[s, 1].astype(F32)).astype(BF16)
        send(Y2_ID[s] + 3, y2s.at[s, 3], y2r.at[s, 3], y_minus)

    def eye(s, h):
        shape = (PART, BLOCK)
        r = lax.broadcasted_iota(jnp.int32, shape, 0) + BLOCK * row_block + HALF * c + PART * s
        k = lax.broadcasted_iota(jnp.int32, shape, 1) + BLOCK * (2 * x + h)
        return (r == k).astype(F32)

    def inverse(sums):
        return lax.rsqrt(sums / TOKENS + epsilon)

    def lane_block(block):
        return pl.ds(pl.multiple_of(block * BLOCK, BLOCK), BLOCK)

    def normalise(s):
        for k in range(4):
            wait(Y2_ID[s] + k, y2r.at[s, k])
        rows = pl.ds(pl.multiple_of(HALF * c + PART * s, PART), PART)
        inv_row = jnp.broadcast_to(inverse(totbuf[y, zl, :, rows]), (PART, PART))
        inv_row = jnp.concatenate([jnp.transpose(inv_row)] * 4, axis=1)
        for h in range(2):
            inv_col = inverse(totbuf[col_slot[h], zl])
            first, second = ((1, 2), (0, 3))[h]
            g = both(s, y, h) + y2r[s, first].astype(F32) + y2r[s, second].astype(F32)
            damped = g / TOKENS * inv_row * inv_col + damping * eye(s, h)
            value = damped / divisor
            scaled[h, s] = value
            half = value.astype(BF16)
            rowbuf[s, :, lane_block(2 * x + h)] = half
            colbuf[h, row_block, c, s] = half

    def row_line(s):
        def ref(step, half):
            return rowbuf.at[s, :, lane_block(((x + step) % 4) * 2 + half)]

        return Line(send, wait, ROW_ID[s], ref, x_plus, x_minus)

    def col_plane(k, s, h=None):
        def piece(block, core, half):
            if h is None:
                r = colbuf.at[:, block, core, s]
                return r if half is None else r.at[half]
            r = colbuf.at[h, block, core, s]
            return r if half is None else r.at[pl.ds(half * (PART // 2), PART // 2)]

        def ref(step, half, other=0):
            return piece(((y + step) % 4) * 2 + (1 - zh if other else zh), c, half)

        def mirrored(half):
            return piece(0, 1 - c, half)

        return Plane(
            send, wait, COL_ID[k], ref, y_plus, y_minus, zh_mate, sibling, mirrored
        )

    def sq_line(h):
        def ref(step, half):
            return sqrow.at[pl.ds(PART * half, PART), lane_block(((x + step) % 4) * 2 + h)]

        return Line(send, wait, SQ_ID[h], ref, x_plus, x_minus)

    rows = [row_line(s) for s in range(2)]
    cols = [col_plane(0, 0), col_plane(1, 1, 0), col_plane(2, 1, 1)]
    sq_rows = [sq_line(h) for h in range(2)]

    def product(h, left):
        def step(k, carry):
            lanes = pl.ds(pl.multiple_of(k * HALF, HALF), HALF)
            sq[h, :, lanes] = jnp.dot(
                left[...].reshape(HALF, D), colbuf[h, :, :, :, :, lanes].reshape(D, HALF),
                preferred_element_type=F32,
            )
            return carry

        lax.fori_loop(0, 2, step, 0)

    def square(h):
        product(h, rowbuf)
        sqrow[:, lane_block(2 * x + h)] = sq[h].astype(BF16)
        sq_rows[h].start()
        for s in range(2):
            scaled[h, s] = (
                4.0 * eye(s, h) - 6.0 * scaled[h, s] + 4.0 * sq[h, PART * s : PART * (s + 1)]
            )

    def out_copy(h, b):
        return remote(
            OUT_ID[h] + b, obuf.at[h, pl.ds(b * 32, 32)], orecv.at[h, line_slot], (out_tok, b),
            OUT_ID[h] + line_slot,
        )

    def cube(h):
        product(h, sqrow)
        obuf[h] = (scaled[h].reshape(HALF, BLOCK) - sq[h]).astype(BF16)
        for b in range(8):
            me = home & (blk == b)

            @pl.when(me)
            def _():
                orecv[h, line_slot] = obuf[h, b * 32 : (b + 1) * 32]

            @pl.when(jnp.logical_not(me))
            def _():
                out_copy(h, b).start()

    def emit(h):
        for k in range(8):
            @pl.when(jnp.logical_not(home & (line_slot == k)))
            def _():
                wait(OUT_ID[h] + k, orecv.at[h, k])

        for k in range(8):
            out = (act_out, grad_out)[k % 2]
            start = (2 * (k // 2) + h) * BLOCK
            out[:, start : start + BLOCK] = orecv[h, k].astype(F32)

    z_first(0)
    lines[0][0].start()
    column_sums()
    sums_start()
    z_rest(0)
    z_first(1)
    z_rest(1)
    lines[0][0].near()
    z_first_take(0)
    lines[0][1].start()
    totals_start()
    lines[0][1].near()
    lines[1][0].start()
    z_first_take(1)
    lines[1][1].start()
    lines[0][0].finish()
    lines[0][1].finish()
    z_rest_take(0)
    z_rest_take(1)
    gram(0)
    lines[1][0].near()
    reduce_start(0)
    lines[1][1].near()
    reduce_middle(0)
    lines[1][0].finish()
    lines[1][1].finish()
    gram(1)
    totals_finish()
    normalise(0)
    cols[0].start()
    rows[0].start()
    reduce_start(1)
    cols[0].near()
    reduce_middle(1)
    cols[0].other()
    rows[0].near()
    cols[0].far()
    normalise(1)
    cols[1].start()
    rows[1].start()
    cols[0].finish()
    cols[1].near()
    cols[1].other()
    cols[2].start()
    rows[1].near()
    rows[0].finish()
    cols[1].far()
    cols[2].near()
    cols[2].other()
    rows[1].finish()
    cols[1].finish()
    square(0)
    cols[2].far()
    sq_rows[0].near()
    cols[2].finish()
    square(1)
    sq_rows[0].finish()
    sq_rows[1].near()
    sq_rows[1].finish()
    cube(0)
    cube(1)
    emit(0)
    emit(1)

    for copy in sent:
        copy.wait_send()

    def sums_left(j, carry):
        sum_copy(j).wait_send()
        return carry

    lax.fori_loop(1, 16, sums_left, 0)
    for j in range(4):
        total_copy(j).wait_send()
    for h in range(2):
        for k in range(4):
            d_copy(h, k).wait_send()
        for b in range(8):
            @pl.when(jnp.logical_not(home & (blk == b)))
            def _():
                out_copy(h, b).wait_send()


def body(activations, out_grads):
    hbm = pl.BlockSpec(memory_space=pltpu.HBM)
    vmem = pl.BlockSpec(memory_space=pltpu.VMEM)
    out = jax.ShapeDtypeStruct((32, D), F32)
    part = (PART, BLOCK)
    scratch = [
        pltpu.VMEM((2, 5, 2, BLOCK, HALF), BF16),
        pltpu.VMEM((2, BLOCK, HALF), BF16),
        pltpu.VMEM((2, 4, 2, 2, *part), BF16),
        pltpu.VMEM((2, 4, 2, *part), BF16),
        pltpu.VMEM((2, 2, *part), BF16),
        pltpu.VMEM((2, 2, *part), BF16),
        pltpu.VMEM((2, 4, *part), BF16),
        pltpu.VMEM((2, 4, *part), BF16),
        pltpu.VMEM((2, 2, *part), F32),
        pltpu.VMEM((2, PART, D), BF16),
        pltpu.VMEM((2, 8, 2, 2, *part), BF16),
        pltpu.VMEM((HALF, D), BF16),
        pltpu.VMEM((2, HALF, BLOCK), F32),
        pltpu.VMEM((2, HALF, BLOCK), BF16),
        pltpu.VMEM((2, 8, 32, BLOCK), BF16),
        pltpu.VMEM((2, 1, BLOCK), F32),
        pltpu.VMEM((16, 2, 1, BLOCK), F32),
        pltpu.VMEM((5, 2, 1, BLOCK), F32),
        pltpu.SemaphoreType.DMA((N_ID,)),
        pltpu.SemaphoreType.DMA((N_ID,)),
        pltpu.SemaphoreType.DMA((8,)),
    ]
    return pl.pallas_call(
        kernel,
        out_shape=(out, out),
        in_specs=[hbm, hbm],
        out_specs=(vmem, vmem),
        scratch_shapes=scratch,
        compiler_params=pltpu.CompilerParams(
            collective_id=0, has_side_effects=True, vmem_limit_bytes=62 * 1024 * 1024
        ),
    )(activations, out_grads)


def solution(mesh):
    placed = (P("tok", "blk"), P("tok", "blk"))
    return jax.shard_map(
        body,
        mesh=mesh,
        in_specs=placed,
        out_specs=(P(("tok", "blk"), None), P(("tok", "blk"), None)),
        check_vma=False,
    )
```

time: 492 us -> 131 us (0.27)
  waiting for transfers between devices: 379 us -> 0 us
  Pallas kernels: 0 us -> 125 us
  starting transfers between devices: 41.3 us -> 0 us
  matrix products: 30.8 us -> 0 us
  between operations: 14 us -> 0.65 us
  other arithmetic: 12.2 us -> 0 us
  local copies, waits for them, and re-layouts: 13.4 us -> 2.72 us
    all_gather x3 -> x0, waiting for transfers between devices: 201 us -> none  [the longest x1 123 us: side_by_side(): out = lax.all_gather(both, axis, axis=dim, tiled=True)]
    pallas_call x0 -> x1, Pallas kernels: none -> 125 us  [body(): pl.pallas_call(kernel, out_shape=(out, out), in_specs=[hbm, hbm], out_spe...]
    reduce_scatter x2 -> x0, waiting for transfers between devices: 99.2 us -> none  [damped_tile(): lax.psum_scatter(lax.dot_general(full, local, (((0,), (0,)), ((), ())), p...]
    all_to_all x8 -> x0, waiting for transfers between devices: 78.1 us -> none  [the longest x6 66.5 us: sent_to_all(): lax.all_to_all(jnp.broadcast_to(value[None], (length, *value.shape)), axi...]
    all_to_all x8 -> x0, starting transfers between devices: 41.1 us -> none  [the longest x6 34.2 us: sent_to_all(): lax.all_to_all(jnp.broadcast_to(value[None], (length, *value.shape)), axi...]
    dot_general x6 -> x0, matrix products: 30.8 us -> none  [the longest x2 13.2 us: damped_tile(): lax.dot_general(full, local, (((0,), (0,)), ((), ())), preferred_element_...]
    broadcast_in_dim x7 -> x0, local copies, waits for them, and re-layouts: 6.93 us -> none  [sent_to_all(): jnp.broadcast_to(value[None], (length, *value.shape))]
  transfers between devices with their start and end apart: 13 -> 0, of which waited for: 11 -> 0; matrix products, arithmetic and copies ran while one was open for 8% -> 0% of each run, Pallas kernels for 0% -> 0%
where the time goes in v3:
time: 131 us; the launch traced here: 129 us
  Pallas kernels  125 us (95%)
  local copies, waits for them, and re-layouts  2.72 us (2%)
    pallas_call x1, Pallas kernels, body(): pl.pallas_call(kernel, out_shape=(out, out), in_specs=[hbm, hbm], out_spe...  125 us
    unnamed x4, local copies, waits for them, and re-layouts  2.72 us

profile of v3, /device:TPU:0, one launch (start us, length us, event | category | flops | bytes accessed | tf_op | source)
XLA Modules:
  0.0 128.5 jit_solution(2387502577677194624)
XLA Ops:
  0.6 125.1 %shard_map.41 = (f32[32,4096]{1,0:T(8,128)}, f32[32,4096]{1,0:T(8,128)}) custom-call(bf16[512,512]{1,0:T(8,128)(2,1)} %act_ref.1, bf16[512,512]{1,0:T(8,128)(2,1)} %grad_ref.1), custom_call_target="tpu_custom_call" | custom-call | tf_op jit(solution)/shard_map/pallas_call | solution.py:580
  125.8 0.0 copy-start
  125.8 1.9 %copy.6 = f32[32,4096]{1,0:T(8,128)} copy(f32[32,4096]{1,0:T(8,128)} %get-tuple-element.4) | data formatting | bytes 1048576
  127.7 0.0 copy-done
  127.7 0.8 copy.7
Async XLA Ops:
  125.8 1.9 %copy-start = (f32[32,4096]{1,0:T(8,128)S(1)}, f32[32,4096]{1,0:T(8,128)}, u32[]{:S(2)}) copy-start(f32[32,4096]{1,0:T(8,128)} %get-tuple-element.5) | copy-start | bytes 1572868

commit v4 on v3

--- a/solution.py
+++ b/solution.py
@@ -33,9 +33,9 @@
 IDS = Ids()
 Z_ID = IDS.take(6)
 X_ID = [[IDS.take(6) for _ in range(2)] for _ in range(2)]
-D_ID = [IDS.take(4) for _ in range(2)]
-Y1_ID = [IDS.take(2) for _ in range(2)]
-Y2_ID = [IDS.take(4) for _ in range(2)]
+D_ID = [[IDS.take(4) for _ in range(2)] for _ in range(2)]
+Y1_ID = [[IDS.take(2) for _ in range(2)] for _ in range(2)]
+Y2_ID = [[IDS.take(4) for _ in range(2)] for _ in range(2)]
 ROW_ID = [IDS.take(6) for _ in range(2)]
 COL_ID = [IDS.take(23) for _ in range(3)]
 SQ_ID = [IDS.take(6) for _ in range(2)]
@@ -100,6 +100,8 @@
         self.take(6)
         self.put(7, (0, None, 1), self.plus)
         self.put(8, (0, None, 1), self.minus)
+        self.take(1)
+        self.take(3)
 
     def far(self):
         self.take(4)
@@ -108,7 +110,7 @@
         self.put(10, (2, 1, 0), self.across)
 
     def finish(self):
-        for k in (1, 3, 7, 8, 9, 10):
+        for k in (7, 8, 9, 10):
             self.take(k)
         for k in range(11, 23):
             half = None if k in (11, 18, 19, 20) else 0
@@ -116,9 +118,9 @@
 
 
 def kernel(
-    act_ref, grad_ref, act_out, grad_out,
+    act_ref, grad_ref, out_ref,
     xall, give, gram_part, drecv, y1s, y1r, y2s, y2r, scaled,
-    rowbuf, colbuf, sqrow, sq, obuf, orecv, csend, crecv, totbuf,
+    rowbuf, colbuf, sqrow, sq, obuf, csend, crecv, totbuf,
     ssem, rsem, lsem,
 ):
     tok, blk = lax.axis_index("tok"), lax.axis_index("blk")
@@ -143,10 +145,22 @@
     def place(to):
         return {"tok": to[0], "blk": to[1]}
 
-    out_tok = 4 * y + 2 * zh + c
-    home = out_tok == tok
+    def row_of(s, zh_, y_):
+        if s == 0:
+            return (y_ % 2) * 2 + y_ // 2
+        return (y_ // 2) * 2 + (y_ % 2 + y_ // 2 + zh_) % 2
+
+    def line_of(zh_, x_):
+        return (
+            (x_ % 2) * 2 + x_ // 2,
+            (x_ // 2) * 2 + (x_ % 2 + x_ // 2 + zh_) % 2,
+        )
+
+    row_block = [2 * row_of(s, zh, y) + zh for s in range(2)]
+    out_tok = [2 * row_block[s] + c for s in range(2)]
+    my_set = blk // 4
+    home = jnp.where(my_set == 0, out_tok[0], out_tok[1]) == tok
     line_slot = 2 * x + zl
-    row_block = 2 * y + zh
 
     def loads(src, dst, first):
         out = []
@@ -198,7 +212,9 @@
     greet(z_cross)
 
     def greet_source(j, carry):
-        to = (tok_of(j % 2, tok // 4, c), blk_of(j // 2, (tok // 2) % 2))
+        zh_ = (tok // 2) % 2
+        y_of = line_of(zh_, tok // 4)
+        to = (tok_of(j % 2, jnp.where(my_set == 0, y_of[0], y_of[1]), c), blk_of(j // 2, zh_))
 
         @pl.when(jnp.logical_not((to[0] == tok) & (to[1] == blk)))
         def _():
@@ -294,67 +310,72 @@
         for j in range(4):
             total_copy(j).wait_recv()
 
-    col_slot = [jnp.where(zh == h, x, 4) for h in range(2)]
-
-    def gram(s):
+    def gram(s, g):
+        cols = (x, 4)[g]
+
         def step(i, carry):
             to = (x + 3 + i) % 4
-            for h in range(2):
-                for s2 in range(2):
-                    value = None
-                    for t in range(2):
-                        term = lax.dot_general(
-                            xall[t, to, s], xall[t, col_slot[h], s2],
-                            (((0,), (0,)), ((), ())), preferred_element_type=F32,
-                        )
-                        value = term if value is None else value + term
-                    value = value.astype(BF16)
-                    for k in range(2):
-                        for k2 in range(2):
-                            start = HALF * k2 + PART * s2
-                            gram_part[s, to, k, h, :, start : start + PART] = value[
-                                PART * k : PART * (k + 1), PART * k2 : PART * (k2 + 1)
-                            ]
-            d_copy(s, to).start()
+            for s2 in range(2):
+                value = None
+                for t in range(2):
+                    term = lax.dot_general(
+                        xall[t, to, s], xall[t, cols, s2],
+                        (((0,), (0,)), ((), ())), preferred_element_type=F32,
+                    )
+                    value = term if value is None else value + term
+                value = value.astype(BF16)
+                for k in range(2):
+                    for k2 in range(2):
+                        start = HALF * k2 + PART * s2
+                        gram_part[s, g, to, k, :, start : start + PART] = value[
+                            PART * k : PART * (k + 1), PART * k2 : PART * (k2 + 1)
+                        ]
+            d_copy(s, g, to).start()
             return carry
 
         lax.fori_loop(0, 4, step, 0)
 
-    def d_copy(s, to):
+    def d_copy(s, g, to):
         return remote(
-            D_ID[s] + to, gram_part.at[s, to, 1 - c], drecv.at[s, to], sibling
+            D_ID[s][g] + to, gram_part.at[s, g, to, 1 - c], drecv.at[s, g, to], sibling
         )
 
-    def both(s, to, h):
-        return gram_part[s, to, c, h].astype(F32) + drecv[s, to, h].astype(F32)
-
-    y_far, y_up, y_down = (y + 2) % 4, (y + 1) % 4, (y + 3) % 4
-
-    def reduce_start(s):
-        d_copy(s, y_far).wait_recv()
-        y1s[s, 0] = both(s, y_far, 0).astype(BF16)
-        send(Y1_ID[s] + 0, y1s.at[s, 0], y1r.at[s, 0], y_plus)
-        y1s[s, 1] = both(s, y_far, 1).astype(BF16)
-        send(Y1_ID[s] + 1, y1s.at[s, 1], y1r.at[s, 1], y_minus)
-        d_copy(s, y_up).wait_recv()
-        y2s[s, 0] = both(s, y_up, 1).astype(BF16)
-        send(Y2_ID[s] + 0, y2s.at[s, 0], y2r.at[s, 0], y_plus)
-        d_copy(s, y_down).wait_recv()
-        y2s[s, 2] = both(s, y_down, 0).astype(BF16)
-        send(Y2_ID[s] + 2, y2s.at[s, 2], y2r.at[s, 2], y_minus)
-        d_copy(s, y).wait_recv()
-
-    def reduce_middle(s):
-        wait(Y1_ID[s] + 0, y1r.at[s, 0])
-        y2s[s, 1] = (both(s, y_up, 0) + y1r[s, 0].astype(F32)).astype(BF16)
-        send(Y2_ID[s] + 1, y2s.at[s, 1], y2r.at[s, 1], y_plus)
-        wait(Y1_ID[s] + 1, y1r.at[s, 1])
-        y2s[s, 3] = (both(s, y_down, 1) + y1r[s, 1].astype(F32)).astype(BF16)
-        send(Y2_ID[s] + 3, y2s.at[s, 3], y2r.at[s, 3], y_minus)
+    halves = (pl.ds(0, PART // 2), pl.ds(PART // 2, PART // 2))
+
+    def both(s, g, to, half):
+        mine = gram_part[s, g, to, c, halves[half]].astype(F32)
+        return mine + drecv[s, g, to, halves[half]].astype(F32)
+
+    def keep(s, step):
+        return row_of(s, zh, (y + step) % 4)
+
+    def reduce_start(s, g):
+        y1, y2, far, up, down = Y1_ID[s][g], Y2_ID[s][g], keep(s, 2), keep(s, 1), keep(s, 3)
+        d_copy(s, g, far).wait_recv()
+        y1s[s, g, 0] = both(s, g, far, 0).astype(BF16)
+        send(y1, y1s.at[s, g, 0], y1r.at[s, g, 0], y_plus)
+        y1s[s, g, 1] = both(s, g, far, 1).astype(BF16)
+        send(y1 + 1, y1s.at[s, g, 1], y1r.at[s, g, 1], y_minus)
+        d_copy(s, g, up).wait_recv()
+        y2s[s, g, 0] = both(s, g, up, 1).astype(BF16)
+        send(y2, y2s.at[s, g, 0], y2r.at[s, g, 0], y_plus)
+        d_copy(s, g, down).wait_recv()
+        y2s[s, g, 2] = both(s, g, down, 0).astype(BF16)
+        send(y2 + 2, y2s.at[s, g, 2], y2r.at[s, g, 2], y_minus)
+        d_copy(s, g, keep(s, 0)).wait_recv()
+
+    def reduce_middle(s, g):
+        y1, y2, up, down = Y1_ID[s][g], Y2_ID[s][g], keep(s, 1), keep(s, 3)
+        wait(y1, y1r.at[s, g, 0])
+        y2s[s, g, 1] = (both(s, g, up, 0) + y1r[s, g, 0].astype(F32)).astype(BF16)
+        send(y2 + 1, y2s.at[s, g, 1], y2r.at[s, g, 1], y_plus)
+        wait(y1 + 1, y1r.at[s, g, 1])
+        y2s[s, g, 3] = (both(s, g, down, 1) + y1r[s, g, 1].astype(F32)).astype(BF16)
+        send(y2 + 3, y2s.at[s, g, 3], y2r.at[s, g, 3], y_minus)
 
     def eye(s, h):
         shape = (PART, BLOCK)
-        r = lax.broadcasted_iota(jnp.int32, shape, 0) + BLOCK * row_block + HALF * c + PART * s
+        r = lax.broadcasted_iota(jnp.int32, shape, 0) + BLOCK * row_block[s] + HALF * c + PART * s
         k = lax.broadcasted_iota(jnp.int32, shape, 1) + BLOCK * (2 * x + h)
         return (r == k).astype(F32)
 
@@ -365,21 +386,23 @@
         return pl.ds(pl.multiple_of(block * BLOCK, BLOCK), BLOCK)
 
     def normalise(s):
-        for k in range(4):
-            wait(Y2_ID[s] + k, y2r.at[s, k])
         rows = pl.ds(pl.multiple_of(HALF * c + PART * s, PART), PART)
-        inv_row = jnp.broadcast_to(inverse(totbuf[y, zl, :, rows]), (PART, PART))
+        inv_row = jnp.broadcast_to(inverse(totbuf[keep(s, 0), zl, :, rows]), (PART, PART))
         inv_row = jnp.concatenate([jnp.transpose(inv_row)] * 4, axis=1)
-        for h in range(2):
-            inv_col = inverse(totbuf[col_slot[h], zl])
-            first, second = ((1, 2), (0, 3))[h]
-            g = both(s, y, h) + y2r[s, first].astype(F32) + y2r[s, second].astype(F32)
-            damped = g / TOKENS * inv_row * inv_col + damping * eye(s, h)
+        for g in range(2):
+            for k in range(4):
+                wait(Y2_ID[s][g] + k, y2r.at[s, g, k])
+            h = zh if g == 0 else 1 - zh
+            inv_col = inverse(totbuf[(x, 4)[g], zl])
+            low = both(s, g, keep(s, 0), 0) + y2r[s, g, 1].astype(F32) + y2r[s, g, 2].astype(F32)
+            high = both(s, g, keep(s, 0), 1) + y2r[s, g, 0].astype(F32) + y2r[s, g, 3].astype(F32)
+            total = jnp.concatenate([low, high], axis=0)
+            damped = total / TOKENS * inv_row * inv_col + damping * eye(s, h)
             value = damped / divisor
             scaled[h, s] = value
             half = value.astype(BF16)
             rowbuf[s, :, lane_block(2 * x + h)] = half
-            colbuf[h, row_block, c, s] = half
+            colbuf[h, row_block[s], c, s] = half
 
     def row_line(s):
         def ref(step, half):
@@ -393,10 +416,11 @@
                 r = colbuf.at[:, block, core, s]
                 return r if half is None else r.at[half]
             r = colbuf.at[h, block, core, s]
-            return r if half is None else r.at[pl.ds(half * (PART // 2), PART // 2)]
+            return r if half is None else r.at[halves[half]]
 
         def ref(step, half, other=0):
-            return piece(((y + step) % 4) * 2 + (1 - zh if other else zh), c, half)
+            zh_ = 1 - zh if other else zh
+            return piece(2 * row_of(s, zh_, (y + step) % 4) + zh_, c, half)
 
         def mirrored(half):
             return piece(0, 1 - c, half)
@@ -437,7 +461,8 @@
 
     def out_copy(h, b):
         return remote(
-            OUT_ID[h] + b, obuf.at[h, pl.ds(b * 32, 32)], orecv.at[h, line_slot], (out_tok, b),
+            OUT_ID[h] + b, obuf.at[h, pl.ds(b * 32, 32)],
+            out_ref.at[zl, :, lane_block(2 * x + h)], (out_tok[b // 4], b),
             OUT_ID[h] + line_slot,
         )
 
@@ -449,7 +474,7 @@
 
             @pl.when(me)
             def _():
-                orecv[h, line_slot] = obuf[h, b * 32 : (b + 1) * 32]
+                out_ref[zl, :, lane_block(2 * x + h)] = obuf[h, b * 32 : (b + 1) * 32]
 
             @pl.when(jnp.logical_not(me))
             def _():
@@ -459,19 +484,14 @@
         for k in range(8):
             @pl.when(jnp.logical_not(home & (line_slot == k)))
             def _():
-                wait(OUT_ID[h] + k, orecv.at[h, k])
-
-        for k in range(8):
-            out = (act_out, grad_out)[k % 2]
-            start = (2 * (k // 2) + h) * BLOCK
-            out[:, start : start + BLOCK] = orecv[h, k].astype(F32)
+                wait(OUT_ID[h] + k, out_ref.at[k % 2, :, pl.ds((2 * (k // 2) + h) * BLOCK, BLOCK)])
 
     z_first(0)
     lines[0][0].start()
     column_sums()
     sums_start()
+    z_first(1)
     z_rest(0)
-    z_first(1)
     z_rest(1)
     lines[0][0].near()
     z_first_take(0)
@@ -483,38 +503,44 @@
     lines[1][1].start()
     lines[0][0].finish()
     lines[0][1].finish()
+    gram(0, 0)
+    reduce_start(0, 0)
+    lines[1][0].near()
     z_rest_take(0)
     z_rest_take(1)
-    gram(0)
-    lines[1][0].near()
-    reduce_start(0)
+    gram(0, 1)
+    reduce_middle(0, 0)
+    reduce_start(0, 1)
     lines[1][1].near()
-    reduce_middle(0)
-    lines[1][0].finish()
-    lines[1][1].finish()
-    gram(1)
+    reduce_middle(0, 1)
     totals_finish()
     normalise(0)
     cols[0].start()
     rows[0].start()
-    reduce_start(1)
+    lines[1][0].finish()
+    lines[1][1].finish()
+    gram(1, 0)
+    gram(1, 1)
+    reduce_start(1, 0)
+    reduce_start(1, 1)
     cols[0].near()
-    reduce_middle(1)
+    reduce_middle(1, 0)
+    reduce_middle(1, 1)
     cols[0].other()
     rows[0].near()
     cols[0].far()
     normalise(1)
     cols[1].start()
     rows[1].start()
-    cols[0].finish()
     cols[1].near()
+    cols[2].start()
     cols[1].other()
-    cols[2].start()
     rows[1].near()
-    rows[0].finish()
     cols[1].far()
     cols[2].near()
     cols[2].other()
+    cols[0].finish()
+    rows[0].finish()
     rows[1].finish()
     cols[1].finish()
     square(0)
@@ -541,8 +567,8 @@
     for j in range(4):
         total_copy(j).wait_send()
     for h in range(2):
-        for k in range(4):
-            d_copy(h, k).wait_send()
+        for k in range(8):
+            d_copy(h, k // 4, k % 4).wait_send()
         for b in range(8):
             @pl.when(jnp.logical_not(home & (blk == b)))
             def _():
@@ -552,24 +578,23 @@
 def body(activations, out_grads):
     hbm = pl.BlockSpec(memory_space=pltpu.HBM)
     vmem = pl.BlockSpec(memory_space=pltpu.VMEM)
-    out = jax.ShapeDtypeStruct((32, D), F32)
     part = (PART, BLOCK)
+    half_part = (PART // 2, BLOCK)
     scratch = [
         pltpu.VMEM((2, 5, 2, BLOCK, HALF), BF16),
         pltpu.VMEM((2, BLOCK, HALF), BF16),
-        pltpu.VMEM((2, 4, 2, 2, *part), BF16),
-        pltpu.VMEM((2, 4, 2, *part), BF16),
-        pltpu.VMEM((2, 2, *part), BF16),
-        pltpu.VMEM((2, 2, *part), BF16),
-        pltpu.VMEM((2, 4, *part), BF16),
-        pltpu.VMEM((2, 4, *part), BF16),
+        pltpu.VMEM((2, 2, 4, 2, *part), BF16),
+        pltpu.VMEM((2, 2, 4, *part), BF16),
+        pltpu.VMEM((2, 2, 2, *half_part), BF16),
+        pltpu.VMEM((2, 2, 2, *half_part), BF16),
+        pltpu.VMEM((2, 2, 4, *half_part), BF16),
+        pltpu.VMEM((2, 2, 4, *half_part), BF16),
         pltpu.VMEM((2, 2, *part), F32),
         pltpu.VMEM((2, PART, D), BF16),
         pltpu.VMEM((2, 8, 2, 2, *part), BF16),
         pltpu.VMEM((HALF, D), BF16),
         pltpu.VMEM((2, HALF, BLOCK), F32),
         pltpu.VMEM((2, HALF, BLOCK), BF16),
-        pltpu.VMEM((2, 8, 32, BLOCK), BF16),
         pltpu.VMEM((2, 1, BLOCK), F32),
         pltpu.VMEM((16, 2, 1, BLOCK), F32),
         pltpu.VMEM((5, 2, 1, BLOCK), F32),
@@ -577,16 +602,17 @@
         pltpu.SemaphoreType.DMA((N_ID,)),
         pltpu.SemaphoreType.DMA((8,)),
     ]
-    return pl.pallas_call(
+    out = pl.pallas_call(
         kernel,
-        out_shape=(out, out),
+        out_shape=jax.ShapeDtypeStruct((2, 32, D), BF16),
         in_specs=[hbm, hbm],
-        out_specs=(vmem, vmem),
+        out_specs=vmem,
         scratch_shapes=scratch,
         compiler_params=pltpu.CompilerParams(
-            collective_id=0, has_side_effects=True, vmem_limit_bytes=62 * 1024 * 1024
+            collective_id=0, has_side_effects=True, vmem_limit_bytes=60 * 1024 * 1024
         ),
     )(activations, out_grads)
+    return out[0].astype(F32), out[1].astype(F32)
 
 
 def solution(mesh):

time: 131 us -> 126 us (0.962)
  Pallas kernels: 125 us -> 122 us
  local copies, waits for them, and re-layouts: 2.72 us -> 0 us
  other arithmetic: 0 us -> 2.07 us
    pallas_call x1, Pallas kernels: 125 us -> 122 us  [body(): pl.pallas_call(kernel, out_shape=jax.ShapeDtypeStruct((2, 32, D), BF16),...]
    unnamed x4 -> x0, local copies, waits for them, and re-layouts: 2.72 us -> none
    convert_element_type x0 -> x1, other arithmetic: none -> 2.07 us  [body(): return (out[0].astype(F32), out[1].astype(F32))]
where the time goes in v4:
time: 126 us; the launch traced here: 124 us
  Pallas kernels  122 us (97%)
  other arithmetic  2.07 us (2%)
    pallas_call x1, Pallas kernels, body(): pl.pallas_call(kernel, out_shape=jax.ShapeDtypeStruct((2, 32, D), BF16),...  122 us

profile of v4, /device:TPU:0, one launch (start us, length us, event | category | flops | bytes accessed | tf_op | source)
XLA Modules:
  0.0 124.4 jit_solution(11432066978794926568)
XLA Ops:
  0.6 121.7 %shard_map.41 = bf16[2,32,4096]{2,1,0:T(8,128)(2,1)} custom-call(bf16[512,512]{1,0:T(8,128)(2,1)} %act_ref.1, bf16[512,512]{1,0:T(8,128)(2,1)} %grad_ref.1), custom_call_target="tpu_custom_call" | custom-call | tf_op jit(solution)/shard_map/pallas_call | solution.py:605
  122.3 2.1 %bitcast_convert_fusion = (f32[32,4096]{1,0:T(8,128)}, f32[32,4096]{1,0:T(8,128)}) fusion(bf16[2,32,4096]{2,1,0:T(8,128)(2,1)} %shard_map.41), kind=kLoop, calls=%fused_computation | loop fusion | flops 262144 | bytes 1572864 | tf_op jit(solution)/shard_map/convert_element_type | solution.py:615

commit v5 on v4

--- a/solution.py
+++ b/solution.py
@@ -38,8 +38,8 @@
 Y2_ID = [[IDS.take(4) for _ in range(2)] for _ in range(2)]
 ROW_ID = [IDS.take(6) for _ in range(2)]
 COL_ID = [IDS.take(23) for _ in range(3)]
-SQ_ID = [IDS.take(6) for _ in range(2)]
-OUT_ID = [IDS.take(8) for _ in range(2)]
+SQ_ID = [IDS.take(6) for _ in range(3)]
+OUT_ID = IDS.take(8)
 SUM_ID = IDS.take(16)
 TOTAL_ID = IDS.take(4)
 N_ID = IDS.next
@@ -100,6 +100,8 @@
         self.take(6)
         self.put(7, (0, None, 1), self.plus)
         self.put(8, (0, None, 1), self.minus)
+
+    def rest(self):
         self.take(1)
         self.take(3)
 
@@ -109,9 +111,11 @@
         self.take(5)
         self.put(10, (2, 1, 0), self.across)
 
-    def finish(self):
+    def last(self):
         for k in (7, 8, 9, 10):
             self.take(k)
+
+    def passed(self):
         for k in range(11, 23):
             half = None if k in (11, 18, 19, 20) else 0
             self.wait(self.base + k, self.mirrored(half))
@@ -402,7 +406,7 @@
             scaled[h, s] = value
             half = value.astype(BF16)
             rowbuf[s, :, lane_block(2 * x + h)] = half
-            colbuf[h, row_block[s], c, s] = half
+            colbuf[h, keep(s, 0), zh, c, s] = half
 
     def row_line(s):
         def ref(step, half):
@@ -411,80 +415,131 @@
         return Line(send, wait, ROW_ID[s], ref, x_plus, x_minus)
 
     def col_plane(k, s, h=None):
-        def piece(block, core, half):
+        def piece(block, zh_, core, half):
             if h is None:
-                r = colbuf.at[:, block, core, s]
+                r = colbuf.at[:, block, zh_, core, s]
                 return r if half is None else r.at[half]
-            r = colbuf.at[h, block, core, s]
+            r = colbuf.at[h, block, zh_, core, s]
             return r if half is None else r.at[halves[half]]
 
         def ref(step, half, other=0):
             zh_ = 1 - zh if other else zh
-            return piece(2 * row_of(s, zh_, (y + step) % 4) + zh_, c, half)
+            return piece(row_of(s, zh_, (y + step) % 4), zh_, c, half)
 
         def mirrored(half):
-            return piece(0, 1 - c, half)
+            return piece(0, 0, 1 - c, half)
 
         return Plane(
             send, wait, COL_ID[k], ref, y_plus, y_minus, zh_mate, sibling, mirrored
         )
 
-    def sq_line(h):
+    def sq_line(k, h, s=None):
         def ref(step, half):
-            return sqrow.at[pl.ds(PART * half, PART), lane_block(((x + step) % 4) * 2 + h)]
-
-        return Line(send, wait, SQ_ID[h], ref, x_plus, x_minus)
+            if s is None:
+                part = pl.ds(PART * half, PART)
+            else:
+                part = pl.ds(PART * s + PART // 2 * half, PART // 2)
+            return sqrow.at[h, part, lane_block((x + step) % 4)]
+
+        return Line(send, wait, SQ_ID[k], ref, x_plus, x_minus)
 
     rows = [row_line(s) for s in range(2)]
     cols = [col_plane(0, 0), col_plane(1, 1, 0), col_plane(2, 1, 1)]
-    sq_rows = [sq_line(h) for h in range(2)]
-
-    def product(h, left):
+    sq_rows = [sq_line(0, 0), sq_line(1, 1, 0), sq_line(2, 1, 1)]
+
+    def square(h):
         def step(k, carry):
             lanes = pl.ds(pl.multiple_of(k * HALF, HALF), HALF)
             sq[h, :, lanes] = jnp.dot(
-                left[...].reshape(HALF, D), colbuf[h, :, :, :, :, lanes].reshape(D, HALF),
+                rowbuf[...].reshape(HALF, D),
+                colbuf[h, :, :, :, :, :, lanes].reshape(D, HALF),
                 preferred_element_type=F32,
             )
             return carry
 
         lax.fori_loop(0, 2, step, 0)
-
-    def square(h):
-        product(h, rowbuf)
-        sqrow[:, lane_block(2 * x + h)] = sq[h].astype(BF16)
-        sq_rows[h].start()
+        sqrow[h, :, lane_block(x)] = sq[h].astype(BF16)
+
+    def combine(h):
         for s in range(2):
             scaled[h, s] = (
                 4.0 * eye(s, h) - 6.0 * scaled[h, s] + 4.0 * sq[h, PART * s : PART * (s + 1)]
             )
 
-    def out_copy(h, b):
-        return remote(
-            OUT_ID[h] + b, obuf.at[h, pl.ds(b * 32, 32)],
-            out_ref.at[zl, :, lane_block(2 * x + h)], (out_tok[b // 4], b),
-            OUT_ID[h] + line_slot,
-        )
-
-    def cube(h):
-        product(h, sqrow)
-        obuf[h] = (scaled[h].reshape(HALF, BLOCK) - sq[h]).astype(BF16)
-        for b in range(8):
+    def cube_even():
+        for h in range(2):
+            def step(k, carry):
+                lanes = pl.ds(pl.multiple_of(k * HALF, HALF), HALF)
+                sq[h, :, lanes] = jnp.dot(
+                    sqrow[0], colbuf[h, :, 0, :, :, :, lanes].reshape(D // 2, HALF),
+                    preferred_element_type=F32,
+                )
+                return carry
+
+            lax.fori_loop(0, 2, step, 0)
+
+    def cube_odd(s):
+        part = slice(PART * s, PART * (s + 1))
+        for h in range(2):
+            def step(k, carry):
+                lanes = pl.ds(pl.multiple_of(k * HALF, HALF), HALF)
+                value = jnp.dot(
+                    sqrow[1, part], colbuf[h, :, 1, :, :, :, lanes].reshape(D // 2, HALF),
+                    preferred_element_type=F32,
+                )
+                value = scaled[h, s, :, lanes] - sq[h, part, lanes] - value
+                start = pl.multiple_of(BLOCK * h + k * HALF, HALF)
+                obuf[part, pl.ds(start, HALF)] = value.astype(BF16)
+                return carry
+
+            lax.fori_loop(0, 2, step, 0)
+        for b in range(4 * s, 4 * s + 4):
             me = home & (blk == b)
 
             @pl.when(me)
             def _():
-                out_ref[zl, :, lane_block(2 * x + h)] = obuf[h, b * 32 : (b + 1) * 32]
+                out_ref[zl, :, wide_block(x)] = obuf[b * 32 : (b + 1) * 32]
 
             @pl.when(jnp.logical_not(me))
             def _():
-                out_copy(h, b).start()
-
-    def emit(h):
+                out_copy(b).start()
+
+    def wide_block(block):
+        return pl.ds(pl.multiple_of(block * 2 * BLOCK, 2 * BLOCK), 2 * BLOCK)
+
+    def out_copy(b):
+        return remote(
+            OUT_ID + b, obuf.at[pl.ds(b * 32, 32)], out_ref.at[zl, :, wide_block(x)],
+            (out_tok[b // 4], b), OUT_ID + line_slot,
+        )
+
+    def emit():
         for k in range(8):
             @pl.when(jnp.logical_not(home & (line_slot == k)))
             def _():
-                wait(OUT_ID[h] + k, out_ref.at[k % 2, :, pl.ds((2 * (k // 2) + h) * BLOCK, BLOCK)])
+                wait(OUT_ID + k, out_ref.at[k % 2, :, wide_block(k // 2)])
+
+    def drain(n):
+        for copy in sent[:n]:
+            copy.wait_send()
+        del sent[:n]
+
+    def drain_small():
+        def step(j, carry):
+            sum_copy(j).wait_send()
+            return carry
+
+        lax.fori_loop(1, 16, step, 0)
+        for j in range(4):
+            total_copy(j).wait_send()
+
+        def step_d(j, carry):
+            for s in range(2):
+                for g in range(2):
+                    d_copy(s, g, j).wait_send()
+            return carry
+
+        lax.fori_loop(0, 4, step_d, 0)
 
     z_first(0)
     lines[0][0].start()
@@ -520,59 +575,62 @@
     lines[1][0].finish()
     lines[1][1].finish()
     gram(1, 0)
+    reduce_start(1, 0)
     gram(1, 1)
-    reduce_start(1, 0)
+    cols[0].near()
     reduce_start(1, 1)
-    cols[0].near()
     reduce_middle(1, 0)
+    cols[0].rest()
+    rows[0].near()
     reduce_middle(1, 1)
     cols[0].other()
-    rows[0].near()
-    cols[0].far()
     normalise(1)
     cols[1].start()
     rows[1].start()
+    cols[0].far()
+    drain(30)
     cols[1].near()
     cols[2].start()
+    cols[1].rest()
+    rows[1].near()
     cols[1].other()
-    rows[1].near()
+    cols[2].near()
     cols[1].far()
-    cols[2].near()
+    cols[2].rest()
     cols[2].other()
-    cols[0].finish()
+    cols[0].last()
+    cols[2].far()
+    cols[1].last()
+    cols[0].passed()
     rows[0].finish()
     rows[1].finish()
-    cols[1].finish()
+    cols[1].passed()
     square(0)
-    cols[2].far()
+    sq_rows[0].start()
+    combine(0)
+    cols[2].last()
     sq_rows[0].near()
-    cols[2].finish()
+    drain_small()
+    cols[2].passed()
     square(1)
+    sq_rows[1].start()
+    sq_rows[2].start()
     sq_rows[0].finish()
+    combine(1)
     sq_rows[1].near()
+    sq_rows[2].near()
+    cube_even()
+    drain(80)
     sq_rows[1].finish()
-    cube(0)
-    cube(1)
-    emit(0)
-    emit(1)
-
-    for copy in sent:
-        copy.wait_send()
-
-    def sums_left(j, carry):
-        sum_copy(j).wait_send()
-        return carry
-
-    lax.fori_loop(1, 16, sums_left, 0)
-    for j in range(4):
-        total_copy(j).wait_send()
-    for h in range(2):
-        for k in range(8):
-            d_copy(h, k // 4, k % 4).wait_send()
-        for b in range(8):
-            @pl.when(jnp.logical_not(home & (blk == b)))
-            def _():
-                out_copy(h, b).wait_send()
+    cube_odd(0)
+    sq_rows[2].finish()
+    cube_odd(1)
+    drain(len(sent))
+    emit()
+    for b in range(8):
+        @pl.when(jnp.logical_not(home & (blk == b)))
+        def _():
+            out_copy(b).wait_send()
 
 
 def body(activations, out_grads):
@@ -591,10 +649,10 @@
         pltpu.VMEM((2, 2, 4, *half_part), BF16),
         pltpu.VMEM((2, 2, *part), F32),
         pltpu.VMEM((2, PART, D), BF16),
-        pltpu.VMEM((2, 8, 2, 2, *part), BF16),
-        pltpu.VMEM((HALF, D), BF16),
+        pltpu.VMEM((2, 4, 2, 2, 2, *part), BF16),
+        pltpu.VMEM((2, HALF, D // 2), BF16),
         pltpu.VMEM((2, HALF, BLOCK), F32),
-        pltpu.VMEM((2, HALF, BLOCK), BF16),
+        pltpu.VMEM((HALF, 2 * BLOCK), BF16),
         pltpu.VMEM((2, 1, BLOCK), F32),
         pltpu.VMEM((16, 2, 1, BLOCK), F32),
         pltpu.VMEM((5, 2, 1, BLOCK), F32),

time: 126 us -> 127 us (level)
  the two profiles are of different devices: /device:TPU:0 before, /device:TPU:103 now
where the time goes in v5:
time: 127 us; the launch traced here: 126 us
  Pallas kernels  124 us (98%)
  other arithmetic  2.07 us (2%)
    pallas_call x1, Pallas kernels, body(): pl.pallas_call(kernel, out_shape=jax.ShapeDtypeStruct((2, 32, D), BF16),...  124 us

profile of v5, /device:TPU:103, one launch (start us, length us, event | category | flops | bytes accessed | tf_op | source)
XLA Modules:
  0.0 126.3 jit_solution(3334888954870535071)
XLA Ops:
  0.6 123.6 %shard_map.41 = bf16[2,32,4096]{2,1,0:T(8,128)(2,1)} custom-call(bf16[512,512]{1,0:T(8,128)(2,1)} %act_ref.1, bf16[512,512]{1,0:T(8,128)(2,1)} %grad_ref.1), custom_call_target="tpu_custom_call" | custom-call | tf_op jit(solution)/shard_map/pallas_call | solution.py:663
  124.3 2.1 %bitcast_convert_fusion = (f32[32,4096]{1,0:T(8,128)}, f32[32,4096]{1,0:T(8,128)}) fusion(bf16[2,32,4096]{2,1,0:T(8,128)(2,1)} %shard_map.41), kind=kLoop, calls=%fused_computation | loop fusion | flops 262144 | bytes 1572864 | tf_op jit(solution)/shard_map/convert_element_type | solution.py:673

commit v6 on v5

--- a/solution.py
+++ b/solution.py
@@ -32,35 +32,40 @@
 
 IDS = Ids()
 Z_ID = IDS.take(6)
-X_ID = [[IDS.take(6) for _ in range(2)] for _ in range(2)]
-D_ID = [[IDS.take(4) for _ in range(2)] for _ in range(2)]
+X_ID = [[IDS.take(3) for _ in range(2)] for _ in range(2)]
+D_ID = [[IDS.take(1) for _ in range(2)] for _ in range(2)]
 Y1_ID = [[IDS.take(2) for _ in range(2)] for _ in range(2)]
-Y2_ID = [[IDS.take(4) for _ in range(2)] for _ in range(2)]
-ROW_ID = [IDS.take(6) for _ in range(2)]
-COL_ID = [IDS.take(23) for _ in range(3)]
-SQ_ID = [IDS.take(6) for _ in range(3)]
-OUT_ID = IDS.take(8)
-SUM_ID = IDS.take(16)
-TOTAL_ID = IDS.take(4)
+Y2_ID = [[IDS.take(1) for _ in range(2)] for _ in range(2)]
+ROW_ID = [IDS.take(3) for _ in range(2)]
+COL_ID = [IDS.take(8) for _ in range(3)]
+SQ_ID = [IDS.take(3) for _ in range(3)]
+OUT_ID = IDS.take(1)
+SUM_ID = IDS.take(1)
+TOTAL_ID = IDS.take(1)
 N_ID = IDS.next
+
+(TO_X, TO_Z, TO_SIBLING, TO_Y1, TO_Y2, TO_ROWS, TO_PASS, TO_COLS, TO_SQ, TO_OUT, TO_SUM,
+ TO_TOTAL, N_TO) = range(13)
 
 
 class Line:
     arrivals = [(3, 0), (3, 1), (1, 1), (1, 0), (2, 0), (2, 1)]
-
-    def __init__(self, send, wait, base, ref, plus, minus, arrived=None):
-        self.send, self.wait, self.base, self.ref = send, wait, base, ref
-        self.plus, self.minus, self.arrived = plus, minus, arrived
+    number = [0, 2, 1, 2, 2, 2]
+
+    def __init__(self, send, wait, base, kind, ref, plus, minus, late):
+        self.send, self.wait, self.base, self.kind, self.ref = send, wait, base, kind, ref
+        self.plus, self.minus, self.late = plus, minus, late
 
     def put(self, k, where, to):
         r = self.ref(*where)
-        self.send(self.base + k, r, r, to)
+        self.send(self.base + self.number[k], r, r, to, self.kind)
+
+    def arrived(self, k):
+        pass
 
     def take(self, k):
-        r = self.ref(*self.arrivals[k])
-        self.wait(self.base + k, r)
-        if self.arrived is not None:
-            self.arrived(k, r)
+        self.wait(self.base + self.number[k], self.ref(*self.arrivals[k]))
+        self.arrived(k)
 
     def start(self):
         self.put(0, (0, 0), self.plus)
@@ -75,26 +80,30 @@
         self.put(5, (1, 1), self.minus)
 
     def finish(self):
-        for k in (1, 3, 4, 5):
-            self.take(k)
+        self.wait(self.base + 2, self.late)
 
 
 class Plane(Line):
     arrivals = Line.arrivals + [
         (0, None, 1), (3, None, 1), (1, None, 1), (2, 0, 1), (2, 1, 1)
     ]
-
-    def __init__(self, send, wait, base, ref, plus, minus, across, sibling, mirrored):
-        super().__init__(send, wait, base, ref, plus, minus, self.pass_on)
+    number = [0, 2, 1, 2, 3, 4, 5, 6, 6, 6, 6]
+
+    def __init__(self, send, wait, base, ref, plus, minus, late, across, sibling, mirrored):
+        super().__init__(send, wait, base, TO_COLS, ref, plus, minus, late)
         self.across, self.sibling, self.mirrored = across, sibling, mirrored
 
-    def pass_on(self, k, r):
-        self.send(self.base + 12 + k, r, r, self.sibling)
+    def arrived(self, k):
+        self.pass_on(self.arrivals[k])
+
+    def pass_on(self, where):
+        r = self.ref(*where)
+        self.send(self.base + 7, r, r, self.sibling, TO_PASS)
 
     def start(self):
         super().start()
         self.put(6, (0, None, 0), self.across)
-        self.send(self.base + 11, self.ref(0, None, 0), self.ref(0, None, 0), self.sibling)
+        self.pass_on((0, None, 0))
 
     def other(self):
         self.take(6)
@@ -102,8 +111,9 @@
         self.put(8, (0, None, 1), self.minus)
 
     def rest(self):
-        self.take(1)
-        self.take(3)
+        self.wait(self.base + 2, self.ref(3, None))
+        self.arrived(1)
+        self.arrived(3)
 
     def far(self):
         self.take(4)
@@ -112,13 +122,12 @@
         self.put(10, (2, 1, 0), self.across)
 
     def last(self):
+        self.wait(self.base + 6, self.late)
         for k in (7, 8, 9, 10):
-            self.take(k)
+            self.arrived(k)
 
     def passed(self):
-        for k in range(11, 23):
-            half = None if k in (11, 18, 19, 20) else 0
-            self.wait(self.base + k, self.mirrored(half))
+        self.wait(self.base + 7, self.mirrored)
 
 
 def kernel(
@@ -231,22 +240,20 @@
         copy.wait()
     pl.semaphore_wait(barrier, 15 + 7 + 1 + 8 - home.astype(jnp.int32))
 
-    sent = []
-
-    def remote(k, src, dst, to, k_there=None):
+    def remote(k, src, dst, to, kind):
         return pltpu.make_async_remote_copy(
-            src_ref=src, dst_ref=dst, send_sem=ssem.at[k],
-            recv_sem=rsem.at[k if k_there is None else k_there],
+            src_ref=src, dst_ref=dst, send_sem=ssem.at[kind], recv_sem=rsem.at[k],
             device_id=place(to), device_id_type=MESH,
         )
 
-    def send(k, src, dst, to):
-        copy = remote(k, src, dst, to)
-        copy.start()
-        sent.append(copy)
+    def send(k, src, dst, to, kind):
+        remote(k, src, dst, to, kind).start()
 
     def wait(k, dst):
-        remote(k, dst, dst, sibling).wait_recv()
+        remote(k, dst, dst, sibling, 0).wait_recv()
+
+    def left(kind, src):
+        remote(0, src, src, sibling, kind).wait_send()
 
     token_half = (pl.ds(0, HALF), pl.ds(HALF, HALF))
 
@@ -254,16 +261,18 @@
         def ref(step, half):
             return xall.at[t, (x + step) % 4, s, token_half[half]]
 
-        return Line(send, wait, X_ID[s][t], ref, x_plus, x_minus)
+        return Line(
+            send, wait, X_ID[s][t], TO_X, ref, x_plus, x_minus, xall.at[t, (x + 2) % 4]
+        )
 
     lines = [[x_line(s, t) for t in range(2)] for s in range(2)]
 
     def z_first(s):
-        send(Z_ID + s, give.at[s], xall.at[1, x, s], zl_mate)
+        send(Z_ID + s, give.at[s], xall.at[1, x, s], zl_mate, TO_Z)
 
     def z_rest(s):
-        send(Z_ID + 2 + s, give.at[s], xall.at[1, 4, s], z_cross)
-        send(Z_ID + 4 + s, xall.at[0, x, s], xall.at[0, 4, s], zh_mate)
+        send(Z_ID + 2 + s, give.at[s], xall.at[1, 4, s], z_cross, TO_Z)
+        send(Z_ID + 4 + s, xall.at[0, x, s], xall.at[0, 4, s], zh_mate, TO_Z)
 
     def z_first_take(s):
         wait(Z_ID + s, xall.at[1, x, s])
@@ -283,7 +292,7 @@
                     ]
 
     def sum_copy(j):
-        return remote(SUM_ID + j, csend, crecv.at[j], ((tok + j) % 16, blk))
+        return remote(SUM_ID, csend, crecv.at[j], ((tok + j) % 16, blk), TO_SUM)
 
     def sums_start():
         def step(j, carry):
@@ -295,14 +304,11 @@
     total_to = [(tok, blk_of((x + j) % 4, zh)) for j in (1, 2, 3)] + [zh_mate]
 
     def total_copy(j):
-        return remote(TOTAL_ID + j, totbuf.at[x], totbuf.at[x if j < 3 else 4], total_to[j])
+        slot = x if j < 3 else 4
+        return remote(TOTAL_ID, totbuf.at[x], totbuf.at[slot], total_to[j], TO_TOTAL)
 
     def totals_start():
-        def step(j, carry):
-            sum_copy(j).wait_recv()
-            return carry
-
-        lax.fori_loop(1, 16, step, 0)
+        wait(SUM_ID, crecv.at[pl.ds(1, 15)])
         total = csend[...]
         for j in range(1, 16):
             total = total + crecv[j]
@@ -311,8 +317,7 @@
             total_copy(j).start()
 
     def totals_finish():
-        for j in range(4):
-            total_copy(j).wait_recv()
+        wait(TOTAL_ID, totbuf.at[pl.ds(0, 4)])
 
     def gram(s, g):
         cols = (x, 4)[g]
@@ -341,7 +346,7 @@
 
     def d_copy(s, g, to):
         return remote(
-            D_ID[s][g] + to, gram_part.at[s, g, to, 1 - c], drecv.at[s, g, to], sibling
+            D_ID[s][g], gram_part.at[s, g, to, 1 - c], drecv.at[s, g, to], sibling, TO_SIBLING
         )
 
     halves = (pl.ds(0, PART // 2), pl.ds(PART // 2, PART // 2))
@@ -355,27 +360,24 @@
 
     def reduce_start(s, g):
         y1, y2, far, up, down = Y1_ID[s][g], Y2_ID[s][g], keep(s, 2), keep(s, 1), keep(s, 3)
-        d_copy(s, g, far).wait_recv()
+        wait(D_ID[s][g], drecv.at[s, g])
         y1s[s, g, 0] = both(s, g, far, 0).astype(BF16)
-        send(y1, y1s.at[s, g, 0], y1r.at[s, g, 0], y_plus)
+        send(y1, y1s.at[s, g, 0], y1r.at[s, g, 0], y_plus, TO_Y1)
         y1s[s, g, 1] = both(s, g, far, 1).astype(BF16)
-        send(y1 + 1, y1s.at[s, g, 1], y1r.at[s, g, 1], y_minus)
-        d_copy(s, g, up).wait_recv()
+        send(y1 + 1, y1s.at[s, g, 1], y1r.at[s, g, 1], y_minus, TO_Y1)
         y2s[s, g, 0] = both(s, g, up, 1).astype(BF16)
-        send(y2, y2s.at[s, g, 0], y2r.at[s, g, 0], y_plus)
-        d_copy(s, g, down).wait_recv()
+        send(y2, y2s.at[s, g, 0], y2r.at[s, g, 0], y_plus, TO_Y2)
         y2s[s, g, 2] = both(s, g, down, 0).astype(BF16)
-        send(y2 + 2, y2s.at[s, g, 2], y2r.at[s, g, 2], y_minus)
-        d_copy(s, g, keep(s, 0)).wait_recv()
+        send(y2, y2s.at[s, g, 2], y2r.at[s, g, 2], y_minus, TO_Y2)
 
     def reduce_middle(s, g):
         y1, y2, up, down = Y1_ID[s][g], Y2_ID[s][g], keep(s, 1), keep(s, 3)
         wait(y1, y1r.at[s, g, 0])
         y2s[s, g, 1] = (both(s, g, up, 0) + y1r[s, g, 0].astype(F32)).astype(BF16)
-        send(y2 + 1, y2s.at[s, g, 1], y2r.at[s, g, 1], y_plus)
+        send(y2, y2s.at[s, g, 1], y2r.at[s, g, 1], y_plus, TO_Y2)
         wait(y1 + 1, y1r.at[s, g, 1])
         y2s[s, g, 3] = (both(s, g, down, 1) + y1r[s, g, 1].astype(F32)).astype(BF16)
-        send(y2 + 3, y2s.at[s, g, 3], y2r.at[s, g, 3], y_minus)
+        send(y2, y2s.at[s, g, 3], y2r.at[s, g, 3], y_minus, TO_Y2)
 
     def eye(s, h):
         shape = (PART, BLOCK)
@@ -394,8 +396,7 @@
         inv_row = jnp.broadcast_to(inverse(totbuf[keep(s, 0), zl, :, rows]), (PART, PART))
         inv_row = jnp.concatenate([jnp.transpose(inv_row)] * 4, axis=1)
         for g in range(2):
-            for k in range(4):
-                wait(Y2_ID[s][g] + k, y2r.at[s, g, k])
+            wait(Y2_ID[s][g], y2r.at[s, g])
             h = zh if g == 0 else 1 - zh
             inv_col = inverse(totbuf[(x, 4)[g], zl])
             low = both(s, g, keep(s, 0), 0) + y2r[s, g, 1].astype(F32) + y2r[s, g, 2].astype(F32)
@@ -412,7 +413,8 @@
         def ref(step, half):
             return rowbuf.at[s, :, lane_block(((x + step) % 4) * 2 + half)]
 
-        return Line(send, wait, ROW_ID[s], ref, x_plus, x_minus)
+        late = rowbuf.at[s, :, pl.ds(0, 4 * BLOCK)]
+        return Line(send, wait, ROW_ID[s], TO_ROWS, ref, x_plus, x_minus, late)
 
     def col_plane(k, s, h=None):
         def piece(block, zh_, core, half):
@@ -426,11 +428,12 @@
             zh_ = 1 - zh if other else zh
             return piece(row_of(s, zh_, (y + step) % 4), zh_, c, half)
 
-        def mirrored(half):
-            return piece(0, 0, 1 - c, half)
-
+        if h is None:
+            late, mirrored = colbuf.at[:, pl.ds(0, 3), 0, c, s], colbuf.at[:, :, :, 1 - c, s]
+        else:
+            late, mirrored = colbuf.at[h, pl.ds(0, 3), 0, c, s], colbuf.at[h, :, :, 1 - c, s]
         return Plane(
-            send, wait, COL_ID[k], ref, y_plus, y_minus, zh_mate, sibling, mirrored
+            send, wait, COL_ID[k], ref, y_plus, y_minus, late, zh_mate, sibling, mirrored
         )
 
     def sq_line(k, h, s=None):
@@ -441,7 +444,8 @@
                 part = pl.ds(PART * s + PART // 2 * half, PART // 2)
             return sqrow.at[h, part, lane_block((x + step) % 4)]
 
-        return Line(send, wait, SQ_ID[k], ref, x_plus, x_minus)
+        late = sqrow.at[h, pl.ds(PART * (s or 0), PART if s is None else PART // 2)]
+        return Line(send, wait, SQ_ID[k], TO_SQ, ref, x_plus, x_minus, late)
 
     rows = [row_line(s) for s in range(2)]
     cols = [col_plane(0, 0), col_plane(1, 1, 0), col_plane(2, 1, 1)]
@@ -509,37 +513,33 @@
 
     def out_copy(b):
         return remote(
-            OUT_ID + b, obuf.at[pl.ds(b * 32, 32)], out_ref.at[zl, :, wide_block(x)],
-            (out_tok[b // 4], b), OUT_ID + line_slot,
+            OUT_ID, obuf.at[pl.ds(b * 32, 32)], out_ref.at[zl, :, wide_block(x)],
+            (out_tok[b // 4], b), TO_OUT,
         )
 
     def emit():
-        for k in range(8):
-            @pl.when(jnp.logical_not(home & (line_slot == k)))
-            def _():
-                wait(OUT_ID + k, out_ref.at[k % 2, :, wide_block(k // 2)])
-
-    def drain(n):
-        for copy in sent[:n]:
-            copy.wait_send()
-        del sent[:n]
-
-    def drain_small():
-        def step(j, carry):
-            sum_copy(j).wait_send()
-            return carry
-
-        lax.fori_loop(1, 16, step, 0)
-        for j in range(4):
-            total_copy(j).wait_send()
-
-        def step_d(j, carry):
-            for s in range(2):
-                for g in range(2):
-                    d_copy(s, g, j).wait_send()
-            return carry
-
-        lax.fori_loop(0, 4, step_d, 0)
+        @pl.when(home)
+        def _():
+            wait(OUT_ID, out_ref.at[:, :, pl.ds(0, 7 * BLOCK)])
+            left(TO_OUT, obuf.at[pl.ds(0, 7 * 32)])
+
+        @pl.when(jnp.logical_not(home))
+        def _():
+            wait(OUT_ID, out_ref)
+            left(TO_OUT, obuf)
+
+    def all_left():
+        left(TO_X, xall.at[:, pl.ds(0, 3)])
+        left(TO_Z, xall.at[0, pl.ds(0, 3)])
+        left(TO_SIBLING, gram_part.at[0])
+        left(TO_Y1, y1s)
+        left(TO_Y2, y2s)
+        left(TO_ROWS, rowbuf.at[:, pl.ds(0, 96)])
+        left(TO_PASS, colbuf.at[:, :, :, 0])
+        left(TO_COLS, colbuf.at[:, :, :, 0, :, pl.ds(0, 112)])
+        left(TO_SQ, sqrow.at[:, pl.ds(0, 192)])
+        left(TO_SUM, crecv.at[pl.ds(1, 15)])
+        left(TO_TOTAL, totbuf.at[pl.ds(0, 4)])
 
     z_first(0)
     lines[0][0].start()
@@ -561,10 +561,10 @@
     gram(0, 0)
     reduce_start(0, 0)
     lines[1][0].near()
+    reduce_middle(0, 0)
     z_rest_take(0)
     z_rest_take(1)
     gram(0, 1)
-    reduce_middle(0, 0)
     reduce_start(0, 1)
     lines[1][1].near()
     reduce_middle(0, 1)
@@ -575,8 +575,8 @@
     lines[1][0].finish()
     lines[1][1].finish()
     gram(1, 0)
+    gram(1, 1)
     reduce_start(1, 0)
-    gram(1, 1)
     cols[0].near()
     reduce_start(1, 1)
     reduce_middle(1, 0)
@@ -588,7 +588,6 @@
     cols[1].start()
     rows[1].start()
     cols[0].far()
-    drain(30)
     cols[1].near()
     cols[2].start()
     cols[1].rest()
@@ -599,18 +598,17 @@
     cols[2].rest()
     cols[2].other()
     cols[0].last()
+    cols[1].last()
     cols[2].far()
-    cols[1].last()
-    cols[0].passed()
     rows[0].finish()
     rows[1].finish()
+    cols[0].passed()
     cols[1].passed()
     square(0)
     sq_rows[0].start()
     combine(0)
     cols[2].last()
     sq_rows[0].near()
-    drain_small()
     cols[2].passed()
     square(1)
     sq_rows[1].start()
@@ -620,17 +618,12 @@
     sq_rows[1].near()
     sq_rows[2].near()
     cube_even()
-    drain(80)
     sq_rows[1].finish()
     cube_odd(0)
     sq_rows[2].finish()
     cube_odd(1)
-    drain(len(sent))
+    all_left()
     emit()
-    for b in range(8):
-        @pl.when(jnp.logical_not(home & (blk == b)))
-        def _():
-            out_copy(b).wait_send()
 
 
 def body(activations, out_grads):
@@ -656,7 +649,7 @@
         pltpu.VMEM((2, 1, BLOCK), F32),
         pltpu.VMEM((16, 2, 1, BLOCK), F32),
         pltpu.VMEM((5, 2, 1, BLOCK), F32),
-        pltpu.SemaphoreType.DMA((N_ID,)),
+        pltpu.SemaphoreType.DMA((N_TO,)),
         pltpu.SemaphoreType.DMA((N_ID,)),
         pltpu.SemaphoreType.DMA((8,)),
     ]

time: 127 us -> 125 us (0.984)
  Pallas kernels: 124 us -> 122 us
    pallas_call x1, Pallas kernels: 124 us -> 122 us  [body(): pl.pallas_call(kernel, out_shape=jax.ShapeDtypeStruct((2, 32, D), BF16),...]
where the time goes in v6:
time: 125 us
  Pallas kernels  122 us (98%)
  other arithmetic  2.07 us (2%)
    pallas_call x1, Pallas kernels, body(): pl.pallas_call(kernel, out_shape=jax.ShapeDtypeStruct((2, 32, D), BF16),...  122 us

profile of v6, /device:TPU:103, one launch (start us, length us, event | category | flops | bytes accessed | tf_op | source)
XLA Modules:
  0.0 124.8 jit_solution(2816995958910872285)
XLA Ops:
  0.6 122.1 %shard_map.41 = bf16[2,32,4096]{2,1,0:T(8,128)(2,1)} custom-call(bf16[512,512]{1,0:T(8,128)(2,1)} %act_ref.1, bf16[512,512]{1,0:T(8,128)(2,1)} %grad_ref.1), custom_call_target="tpu_custom_call" | custom-call | tf_op jit(solution)/shard_map/pallas_call | solution.py:656
  122.7 2.1 %bitcast_convert_fusion = (f32[32,4096]{1,0:T(8,128)}, f32[32,4096]{1,0:T(8,128)}) fusion(bf16[2,32,4096]{2,1,0:T(8,128)(2,1)} %shard_map.41), kind=kLoop, calls=%fused_computation | loop fusion | flops 262144 | bytes 1572864 | tf_op jit(solution)/shard_map/convert_element_type | solution.py:666

commit v7 on v6

--- a/solution.py
+++ b/solution.py
@@ -36,16 +36,17 @@
 D_ID = [[IDS.take(1) for _ in range(2)] for _ in range(2)]
 Y1_ID = [[IDS.take(2) for _ in range(2)] for _ in range(2)]
 Y2_ID = [[IDS.take(1) for _ in range(2)] for _ in range(2)]
-ROW_ID = [IDS.take(3) for _ in range(2)]
-COL_ID = [IDS.take(8) for _ in range(3)]
-SQ_ID = [IDS.take(3) for _ in range(3)]
+ROW_ID = [IDS.take(7) for _ in range(2)]
+LOW_ID = [IDS.take(1) for _ in range(2)]
+COL_ID = [[IDS.take(4) for _ in range(2)] for _ in range(2)]
+SQ_ID = [IDS.take(4) for _ in range(2)]
 OUT_ID = IDS.take(1)
 SUM_ID = IDS.take(1)
 TOTAL_ID = IDS.take(1)
 N_ID = IDS.next
 
-(TO_X, TO_Z, TO_SIBLING, TO_Y1, TO_Y2, TO_ROWS, TO_PASS, TO_COLS, TO_SQ, TO_OUT, TO_SUM,
- TO_TOTAL, N_TO) = range(13)
+(TO_X, TO_Z, TO_SIBLING, TO_Y1, TO_Y2, TO_ROWS, TO_LOW, TO_PASS, TO_COLS, TO_SQ, TO_SQ_PASS,
+ TO_OUT, TO_SUM, TO_TOTAL, N_TO) = range(15)
 
 
 class Line:
@@ -83,39 +84,53 @@
         self.wait(self.base + 2, self.late)
 
 
+class Passed(Line):
+    def __init__(self, send, wait, base, kind, ref, plus, minus, late, sibling, pass_kind, mirrored):
+        super().__init__(send, wait, base, kind, ref, plus, minus, late)
+        self.sibling, self.pass_kind, self.mirrored = sibling, pass_kind, mirrored
+
+    def pass_on(self, where):
+        r = self.ref(*where)
+        self.send(self.base + 3, r, r, self.sibling, self.pass_kind)
+
+    def arrived(self, k):
+        self.pass_on(self.arrivals[k])
+
+    def start(self):
+        super().start()
+        self.pass_on((0, 0))
+        self.pass_on((0, 1))
+
+    def finish(self):
+        super().finish()
+        for k in (1, 3, 4, 5):
+            self.arrived(k)
+
+    def passed(self):
+        self.wait(self.base + 3, self.mirrored)
+
+
 class Plane(Line):
     arrivals = Line.arrivals + [
         (0, None, 1), (3, None, 1), (1, None, 1), (2, 0, 1), (2, 1, 1)
     ]
     number = [0, 2, 1, 2, 3, 4, 5, 6, 6, 6, 6]
 
-    def __init__(self, send, wait, base, ref, plus, minus, late, across, sibling, mirrored):
-        super().__init__(send, wait, base, TO_COLS, ref, plus, minus, late)
-        self.across, self.sibling, self.mirrored = across, sibling, mirrored
-
-    def arrived(self, k):
-        self.pass_on(self.arrivals[k])
-
-    def pass_on(self, where):
-        r = self.ref(*where)
-        self.send(self.base + 7, r, r, self.sibling, TO_PASS)
+    def __init__(self, send, wait, base, kind, ref, plus, minus, late, across):
+        super().__init__(send, wait, base, kind, ref, plus, minus, late)
+        self.across = across
 
     def start(self):
+        self.put(6, (0, None, 0), self.across)
         super().start()
-        self.put(6, (0, None, 0), self.across)
-        self.pass_on((0, None, 0))
 
     def other(self):
         self.take(6)
         self.put(7, (0, None, 1), self.plus)
         self.put(8, (0, None, 1), self.minus)
 
-    def rest(self):
+    def far(self):
         self.wait(self.base + 2, self.ref(3, None))
-        self.arrived(1)
-        self.arrived(3)
-
-    def far(self):
         self.take(4)
         self.put(9, (2, 0, 0), self.across)
         self.take(5)
@@ -123,17 +138,12 @@
 
     def last(self):
         self.wait(self.base + 6, self.late)
-        for k in (7, 8, 9, 10):
-            self.arrived(k)
-
-    def passed(self):
-        self.wait(self.base + 7, self.mirrored)
 
 
 def kernel(
     act_ref, grad_ref, out_ref,
     xall, give, gram_part, drecv, y1s, y1r, y2s, y2r, scaled,
-    rowbuf, colbuf, sqrow, sq, obuf, csend, crecv, totbuf,
+    rowbuf, colbuf, sqcol, sq, low_out, low_in, obuf, csend, crecv, totbuf,
     ssem, rsem, lsem,
 ):
     tok, blk = lax.axis_index("tok"), lax.axis_index("blk")
@@ -158,22 +168,19 @@
     def place(to):
         return {"tok": to[0], "blk": to[1]}
 
-    def row_of(s, zh_, y_):
-        if s == 0:
-            return (y_ % 2) * 2 + y_ // 2
-        return (y_ // 2) * 2 + (y_ % 2 + y_ // 2 + zh_) % 2
-
-    def line_of(zh_, x_):
-        return (
-            (x_ % 2) * 2 + x_ // 2,
-            (x_ // 2) * 2 + (x_ % 2 + x_ // 2 + zh_) % 2,
-        )
-
-    row_block = [2 * row_of(s, zh, y) + zh for s in range(2)]
-    out_tok = [2 * row_block[s] + c for s in range(2)]
-    my_set = blk // 4
-    home = jnp.where(my_set == 0, out_tok[0], out_tok[1]) == tok
-    line_slot = 2 * x + zl
+    def row_of(s, y_):
+        return ((y_ + s) % 2) * 2 + y_ // 2
+
+    def keep(s, step):
+        return row_of(s, (y + step) % 4)
+
+    zh_of = (zh, 1 - zh)
+
+    def out_tok(e, s):
+        return 2 * (2 * keep(s, 0) + zh_of[e]) + c
+
+    source_y = ((tok // 4) % 2) * 2 + (tok // 8 + blk // 4) % 2
+    home = source_y == y
 
     def loads(src, dst, first):
         out = []
@@ -225,9 +232,7 @@
     greet(z_cross)
 
     def greet_source(j, carry):
-        zh_ = (tok // 2) % 2
-        y_of = line_of(zh_, tok // 4)
-        to = (tok_of(j % 2, jnp.where(my_set == 0, y_of[0], y_of[1]), c), blk_of(j // 2, zh_))
+        to = (tok_of(j % 2, source_y, c), j // 2)
 
         @pl.when(jnp.logical_not((to[0] == tok) & (to[1] == blk)))
         def _():
@@ -235,10 +240,10 @@
 
         return carry
 
-    lax.fori_loop(0, 8, greet_source, 0)
+    lax.fori_loop(0, 16, greet_source, 0)
     for copy in all_loads(act_ref, grad_ref):
         copy.wait()
-    pl.semaphore_wait(barrier, 15 + 7 + 1 + 8 - home.astype(jnp.int32))
+    pl.semaphore_wait(barrier, 15 + 7 + 1 + 16 - home.astype(jnp.int32))
 
     def remote(k, src, dst, to, kind):
         return pltpu.make_async_remote_copy(
@@ -355,9 +360,6 @@
         mine = gram_part[s, g, to, c, halves[half]].astype(F32)
         return mine + drecv[s, g, to, halves[half]].astype(F32)
 
-    def keep(s, step):
-        return row_of(s, zh, (y + step) % 4)
-
     def reduce_start(s, g):
         y1, y2, far, up, down = Y1_ID[s][g], Y2_ID[s][g], keep(s, 2), keep(s, 1), keep(s, 3)
         wait(D_ID[s][g], drecv.at[s, g])
@@ -379,11 +381,11 @@
         y2s[s, g, 3] = (both(s, g, down, 1) + y1r[s, g, 1].astype(F32)).astype(BF16)
         send(y2, y2s.at[s, g, 3], y2r.at[s, g, 3], y_minus, TO_Y2)
 
-    def eye(s, h):
+    def eye(s, zh_, h):
         shape = (PART, BLOCK)
-        r = lax.broadcasted_iota(jnp.int32, shape, 0) + BLOCK * row_block[s] + HALF * c + PART * s
-        k = lax.broadcasted_iota(jnp.int32, shape, 1) + BLOCK * (2 * x + h)
-        return (r == k).astype(F32)
+        r = lax.broadcasted_iota(jnp.int32, shape, 0) + HALF * c + PART * s
+        k = lax.broadcasted_iota(jnp.int32, shape, 1)
+        return (r + BLOCK * (2 * keep(s, 0) + zh_) == k + BLOCK * (2 * x + h)).astype(F32)
 
     def inverse(sums):
         return lax.rsqrt(sums / TOKENS + epsilon)
@@ -397,131 +399,131 @@
         inv_row = jnp.concatenate([jnp.transpose(inv_row)] * 4, axis=1)
         for g in range(2):
             wait(Y2_ID[s][g], y2r.at[s, g])
-            h = zh if g == 0 else 1 - zh
             inv_col = inverse(totbuf[(x, 4)[g], zl])
             low = both(s, g, keep(s, 0), 0) + y2r[s, g, 1].astype(F32) + y2r[s, g, 2].astype(F32)
             high = both(s, g, keep(s, 0), 1) + y2r[s, g, 0].astype(F32) + y2r[s, g, 3].astype(F32)
             total = jnp.concatenate([low, high], axis=0)
-            damped = total / TOKENS * inv_row * inv_col + damping * eye(s, h)
+            damped = total / TOKENS * inv_row * inv_col + damping * eye(s, zh, zh_of[g])
             value = damped / divisor
-            scaled[h, s] = value
             half = value.astype(BF16)
-            rowbuf[s, :, lane_block(2 * x + h)] = half
-            colbuf[h, keep(s, 0), zh, c, s] = half
-
-    def row_line(s):
+            rowbuf[zh, s, zh_of[g], :, lane_block(x)] = half
+            if g == 0:
+                scaled[0, s] = value
+                colbuf[keep(s, 0), zh, c, s] = half
+                cols[s][0].start()
+            else:
+                low_out[s] = (value - half.astype(F32)).astype(BF16)
+        rows_of[s].start()
+        send(LOW_ID[s], low_out.at[s], low_in.at[s], zh_mate, TO_LOW)
+
+    def partner(s):
+        half = rowbuf[1 - zh, s, zh, :, lane_block(x)]
+        colbuf[keep(s, 0), 1 - zh, c, s] = half
+        cols[s][1].start()
+
+    def partner_low(s):
+        wait(LOW_ID[s], low_in.at[s])
+        half = rowbuf[1 - zh, s, zh, :, lane_block(x)].astype(F32)
+        scaled[1, s] = half + low_in[s].astype(F32)
+
+    def row_plane(s):
+        def ref(step, half, other=0):
+            lanes = lane_block((x + step) % 4)
+            r = rowbuf.at[zh_of[other], s]
+            return r.at[:, :, lanes] if half is None else r.at[half, :, lanes]
+
+        late = rowbuf.at[1 - zh, s, :, :, pl.ds(0, 3 * BLOCK)]
+        return Plane(send, wait, ROW_ID[s], TO_ROWS, ref, x_plus, x_minus, late, zh_mate)
+
+    def col_line(s, e):
         def ref(step, half):
-            return rowbuf.at[s, :, lane_block(((x + step) % 4) * 2 + half)]
-
-        late = rowbuf.at[s, :, pl.ds(0, 4 * BLOCK)]
-        return Line(send, wait, ROW_ID[s], TO_ROWS, ref, x_plus, x_minus, late)
-
-    def col_plane(k, s, h=None):
-        def piece(block, zh_, core, half):
-            if h is None:
-                r = colbuf.at[:, block, zh_, core, s]
-                return r if half is None else r.at[half]
-            r = colbuf.at[h, block, zh_, core, s]
-            return r if half is None else r.at[halves[half]]
-
-        def ref(step, half, other=0):
-            zh_ = 1 - zh if other else zh
-            return piece(row_of(s, zh_, (y + step) % 4), zh_, c, half)
-
-        if h is None:
-            late, mirrored = colbuf.at[:, pl.ds(0, 3), 0, c, s], colbuf.at[:, :, :, 1 - c, s]
-        else:
-            late, mirrored = colbuf.at[h, pl.ds(0, 3), 0, c, s], colbuf.at[h, :, :, 1 - c, s]
-        return Plane(
-            send, wait, COL_ID[k], ref, y_plus, y_minus, late, zh_mate, sibling, mirrored
+            return colbuf.at[keep(s, step), zh_of[e], c, s, halves[half]]
+
+        late = colbuf.at[pl.ds(0, 2), zh_of[e], c, s]
+        return Passed(
+            send, wait, COL_ID[s][e], TO_COLS, ref, y_plus, y_minus, late, sibling, TO_PASS,
+            colbuf.at[:, zh_of[e], 1 - c, s],
         )
 
-    def sq_line(k, h, s=None):
+    def sq_line(e):
         def ref(step, half):
-            if s is None:
-                part = pl.ds(PART * half, PART)
-            else:
-                part = pl.ds(PART * s + PART // 2 * half, PART // 2)
-            return sqrow.at[h, part, lane_block((x + step) % 4)]
-
-        late = sqrow.at[h, pl.ds(PART * (s or 0), PART if s is None else PART // 2)]
-        return Line(send, wait, SQ_ID[k], TO_SQ, ref, x_plus, x_minus, late)
-
-    rows = [row_line(s) for s in range(2)]
-    cols = [col_plane(0, 0), col_plane(1, 1, 0), col_plane(2, 1, 1)]
-    sq_rows = [sq_line(0, 0), sq_line(1, 1, 0), sq_line(2, 1, 1)]
-
-    def square(h):
+            return sqcol.at[keep(half, step), zh_of[e], c, half]
+
+        late = sqcol.at[pl.ds(0, 2), zh_of[e], c]
+        return Passed(
+            send, wait, SQ_ID[e], TO_SQ, ref, y_plus, y_minus, late, sibling, TO_SQ_PASS,
+            sqcol.at[:, zh_of[e], 1 - c],
+        )
+
+    rows_of = [row_plane(s) for s in range(2)]
+    cols = [[col_line(s, e) for e in range(2)] for s in range(2)]
+    sq_cols = [sq_line(e) for e in range(2)]
+
+    def dot(e, p, right, lanes):
+        return jnp.dot(
+            rowbuf[zh_of[e], :, p].reshape(HALF, D // 2),
+            right[:, p, :, :, :, lanes].reshape(D // 2, HALF),
+            preferred_element_type=F32,
+        )
+
+    def over_lanes(body):
         def step(k, carry):
-            lanes = pl.ds(pl.multiple_of(k * HALF, HALF), HALF)
-            sq[h, :, lanes] = jnp.dot(
-                rowbuf[...].reshape(HALF, D),
-                colbuf[h, :, :, :, :, :, lanes].reshape(D, HALF),
-                preferred_element_type=F32,
+            body(pl.ds(pl.multiple_of(k * HALF, HALF), HALF))
+            return carry
+
+        lax.fori_loop(0, 2, step, 0)
+
+    def square(e):
+        def some(lanes):
+            sq[e, :, lanes] = dot(e, 0, colbuf, lanes) + dot(e, 1, colbuf, lanes)
+
+        over_lanes(some)
+        for s in range(2):
+            sqcol[keep(s, 0), zh_of[e], c, s] = sq[e, PART * s : PART * (s + 1)].astype(BF16)
+        sq_cols[e].start()
+
+    def combine(e):
+        for s in range(2):
+            scaled[e, s] = (
+                4.0 * eye(s, zh_of[e], zh) - 6.0 * scaled[e, s]
+                + 4.0 * sq[e, PART * s : PART * (s + 1)]
             )
-            return carry
-
-        lax.fori_loop(0, 2, step, 0)
-        sqrow[h, :, lane_block(x)] = sq[h].astype(BF16)
-
-    def combine(h):
-        for s in range(2):
-            scaled[h, s] = (
-                4.0 * eye(s, h) - 6.0 * scaled[h, s] + 4.0 * sq[h, PART * s : PART * (s + 1)]
-            )
-
-    def cube_even():
-        for h in range(2):
-            def step(k, carry):
-                lanes = pl.ds(pl.multiple_of(k * HALF, HALF), HALF)
-                sq[h, :, lanes] = jnp.dot(
-                    sqrow[0], colbuf[h, :, 0, :, :, :, lanes].reshape(D // 2, HALF),
-                    preferred_element_type=F32,
-                )
-                return carry
-
-            lax.fori_loop(0, 2, step, 0)
-
-    def cube_odd(s):
-        part = slice(PART * s, PART * (s + 1))
-        for h in range(2):
-            def step(k, carry):
-                lanes = pl.ds(pl.multiple_of(k * HALF, HALF), HALF)
-                value = jnp.dot(
-                    sqrow[1, part], colbuf[h, :, 1, :, :, :, lanes].reshape(D // 2, HALF),
-                    preferred_element_type=F32,
-                )
-                value = scaled[h, s, :, lanes] - sq[h, part, lanes] - value
-                start = pl.multiple_of(BLOCK * h + k * HALF, HALF)
-                obuf[part, pl.ds(start, HALF)] = value.astype(BF16)
-                return carry
-
-            lax.fori_loop(0, 2, step, 0)
-        for b in range(4 * s, 4 * s + 4):
-            me = home & (blk == b)
+
+    def cube_first():
+        for e in range(2):
+            def some(lanes):
+                sq[e, :, lanes] = dot(e, zh, sqcol, lanes)
+
+            over_lanes(some)
+
+    def cube_second(e):
+        def some(lanes):
+            value = scaled[e, :, :, lanes].reshape(HALF, HALF) - sq[e, :, lanes]
+            obuf[e, :, lanes] = (value - dot(e, 1 - zh, sqcol, lanes)).astype(BF16)
+
+        over_lanes(some)
+        for b in range(8):
+            me = (out_tok(e, b // 4) == tok) & (blk == b)
 
             @pl.when(me)
             def _():
-                out_ref[zl, :, wide_block(x)] = obuf[b * 32 : (b + 1) * 32]
+                out_ref[zl, :, lane_block(2 * x + zh)] = obuf[e, b * 32 : (b + 1) * 32]
 
             @pl.when(jnp.logical_not(me))
             def _():
-                out_copy(b).start()
-
-    def wide_block(block):
-        return pl.ds(pl.multiple_of(block * 2 * BLOCK, 2 * BLOCK), 2 * BLOCK)
-
-    def out_copy(b):
+                out_copy(e, b).start()
+
+    def out_copy(e, b):
         return remote(
-            OUT_ID, obuf.at[pl.ds(b * 32, 32)], out_ref.at[zl, :, wide_block(x)],
-            (out_tok[b // 4], b), TO_OUT,
+            OUT_ID, obuf.at[e, pl.ds(b * 32, 32)], out_ref.at[zl, :, lane_block(2 * x + zh)],
+            (out_tok(e, b // 4), b), TO_OUT,
         )
 
     def emit():
         @pl.when(home)
         def _():
-            wait(OUT_ID, out_ref.at[:, :, pl.ds(0, 7 * BLOCK)])
-            left(TO_OUT, obuf.at[pl.ds(0, 7 * 32)])
+            wait(OUT_ID, out_ref.at[:, :, pl.ds(0, 15 * HALF)])
+            left(TO_OUT, obuf.at[:, pl.ds(0, 15 * 16)])
 
         @pl.when(jnp.logical_not(home))
         def _():
@@ -534,10 +536,12 @@
         left(TO_SIBLING, gram_part.at[0])
         left(TO_Y1, y1s)
         left(TO_Y2, y2s)
-        left(TO_ROWS, rowbuf.at[:, pl.ds(0, 96)])
-        left(TO_PASS, colbuf.at[:, :, :, 0])
-        left(TO_COLS, colbuf.at[:, :, :, 0, :, pl.ds(0, 112)])
-        left(TO_SQ, sqrow.at[:, pl.ds(0, 192)])
+        left(TO_ROWS, rowbuf.at[:, :, :, pl.ds(0, 112)])
+        left(TO_LOW, low_out)
+        left(TO_PASS, colbuf.at[pl.ds(0, 2)])
+        left(TO_COLS, colbuf.at[pl.ds(0, 3), 0])
+        left(TO_SQ, sqcol.at[pl.ds(0, 3), 0])
+        left(TO_SQ_PASS, sqcol.at[pl.ds(0, 2)])
         left(TO_SUM, crecv.at[pl.ds(1, 15)])
         left(TO_TOTAL, totbuf.at[pl.ds(0, 4)])
 
@@ -561,67 +565,60 @@
     gram(0, 0)
     reduce_start(0, 0)
     lines[1][0].near()
-    reduce_middle(0, 0)
     z_rest_take(0)
     z_rest_take(1)
     gram(0, 1)
+    reduce_middle(0, 0)
     reduce_start(0, 1)
     lines[1][1].near()
     reduce_middle(0, 1)
     totals_finish()
     normalise(0)
-    cols[0].start()
-    rows[0].start()
     lines[1][0].finish()
     lines[1][1].finish()
     gram(1, 0)
     gram(1, 1)
     reduce_start(1, 0)
-    cols[0].near()
+    cols[0][0].near()
+    rows_of[0].near()
     reduce_start(1, 1)
     reduce_middle(1, 0)
-    cols[0].rest()
-    rows[0].near()
+    rows_of[0].other()
+    partner(0)
     reduce_middle(1, 1)
-    cols[0].other()
+    cols[0][0].finish()
+    rows_of[0].far()
+    cols[0][1].near()
     normalise(1)
-    cols[1].start()
-    rows[1].start()
-    cols[0].far()
-    cols[1].near()
-    cols[2].start()
-    cols[1].rest()
-    rows[1].near()
-    cols[1].other()
-    cols[2].near()
-    cols[1].far()
-    cols[2].rest()
-    cols[2].other()
-    cols[0].last()
-    cols[1].last()
-    cols[2].far()
-    rows[0].finish()
-    rows[1].finish()
-    cols[0].passed()
-    cols[1].passed()
+    rows_of[1].near()
+    cols[1][0].near()
+    cols[0][1].finish()
+    rows_of[1].other()
+    partner(1)
+    cols[1][0].finish()
+    cols[1][1].near()
+    rows_of[1].far()
+    cols[1][1].finish()
+    for s in range(2):
+        for e in range(2):
+            cols[s][e].passed()
     square(0)
-    sq_rows[0].start()
     combine(0)
-    cols[2].last()
-    sq_rows[0].near()
-    cols[2].passed()
+    sq_cols[0].near()
+    rows_of[0].last()
+    rows_of[1].last()
     square(1)
-    sq_rows[1].start()
-    sq_rows[2].start()
-    sq_rows[0].finish()
+    sq_cols[0].finish()
+    partner_low(0)
+    partner_low(1)
     combine(1)
-    sq_rows[1].near()
-    sq_rows[2].near()
-    cube_even()
-    sq_rows[1].finish()
-    cube_odd(0)
-    sq_rows[2].finish()
-    cube_odd(1)
+    sq_cols[1].near()
+    sq_cols[0].passed()
+    cube_first()
+    sq_cols[1].finish()
+    sq_cols[1].passed()
+    cube_second(0)
+    cube_second(1)
     all_left()
     emit()
 
@@ -641,11 +638,13 @@
         pltpu.VMEM((2, 2, 4, *half_part), BF16),
         pltpu.VMEM((2, 2, 4, *half_part), BF16),
         pltpu.VMEM((2, 2, *part), F32),
-        pltpu.VMEM((2, PART, D), BF16),
-        pltpu.VMEM((2, 4, 2, 2, 2, *part), BF16),
-        pltpu.VMEM((2, HALF, D // 2), BF16),
+        pltpu.VMEM((2, 2, 2, PART, D // 2), BF16),
+        pltpu.VMEM((4, 2, 2, 2, *part), BF16),
+        pltpu.VMEM((4, 2, 2, 2, *part), BF16),
         pltpu.VMEM((2, HALF, BLOCK), F32),
-        pltpu.VMEM((HALF, 2 * BLOCK), BF16),
+        pltpu.VMEM((2, *part), BF16),
+        pltpu.VMEM((2, *part), BF16),
+        pltpu.VMEM((2, HALF, BLOCK), BF16),
         pltpu.VMEM((2, 1, BLOCK), F32),
         pltpu.VMEM((16, 2, 1, BLOCK), F32),
         pltpu.VMEM((5, 2, 1, BLOCK), F32),

time: 125 us -> 118 us (0.944)
  the two profiles are of different devices: /device:TPU:103 before, /device:TPU:0 now
where the time goes in v7:
time: 118 us
  Pallas kernels  115 us (97%)
  other arithmetic  2.07 us (2%)
    pallas_call x1, Pallas kernels, body(): pl.pallas_call(kernel, out_shape=jax.ShapeDtypeStruct((2, 32, D), BF16),...  115 us

profile of v7, /device:TPU:0, one launch (start us, length us, event | category | flops | bytes accessed | tf_op | source)
XLA Modules:
  0.0 117.8 jit_solution(13764393281321368025)
XLA Ops:
  0.6 115.1 %shard_map.41 = bf16[2,32,4096]{2,1,0:T(8,128)(2,1)} custom-call(bf16[512,512]{1,0:T(8,128)(2,1)} %act_ref.1, bf16[512,512]{1,0:T(8,128)(2,1)} %grad_ref.1), custom_call_target="tpu_custom_call" | custom-call | tf_op jit(solution)/shard_map/pallas_call | solution.py:655
  115.7 2.1 %bitcast_convert_fusion = (f32[32,4096]{1,0:T(8,128)}, f32[32,4096]{1,0:T(8,128)}) fusion(bf16[2,32,4096]{2,1,0:T(8,128)(2,1)} %shard_map.41), kind=kLoop, calls=%fused_computation | loop fusion | flops 262144 | bytes 1572864 | tf_op jit(solution)/shard_map/convert_element_type | solution.py:665

commit v8 on v7

--- a/solution.py
+++ b/solution.py
@@ -36,7 +36,7 @@
 D_ID = [[IDS.take(1) for _ in range(2)] for _ in range(2)]
 Y1_ID = [[IDS.take(2) for _ in range(2)] for _ in range(2)]
 Y2_ID = [[IDS.take(1) for _ in range(2)] for _ in range(2)]
-ROW_ID = [IDS.take(7) for _ in range(2)]
+ROW_ID = [IDS.take(8) for _ in range(2)]
 LOW_ID = [IDS.take(1) for _ in range(2)]
 COL_ID = [[IDS.take(4) for _ in range(2)] for _ in range(2)]
 SQ_ID = [IDS.take(4) for _ in range(2)]
@@ -111,21 +111,27 @@
 
 
 class Plane(Line):
-    arrivals = Line.arrivals + [
-        (0, None, 1), (3, None, 1), (1, None, 1), (2, 0, 1), (2, 1, 1)
-    ]
+    arrivals = Line.arrivals + [None, (3, None, 1), (1, None, 1), (2, 0, 1), (2, 1, 1)]
     number = [0, 2, 1, 2, 3, 4, 5, 6, 6, 6, 6]
 
-    def __init__(self, send, wait, base, kind, ref, plus, minus, late, across):
+    def __init__(self, send, wait, base, kind, ref, plus, minus, late, across, needed):
         super().__init__(send, wait, base, kind, ref, plus, minus, late)
-        self.across = across
+        self.across, self.needed = across, needed
+
+    def cross(self):
+        r = self.ref(0, 1 - self.needed, 0)
+        self.send(self.base + 5, r, r, self.across, self.kind)
 
     def start(self):
-        self.put(6, (0, None, 0), self.across)
+        r = self.ref(0, self.needed, 0)
+        self.send(self.base + 7, r, r, self.across, self.kind)
         super().start()
 
+    def take_needed(self):
+        self.wait(self.base + 5, self.ref(0, self.needed, 1))
+
     def other(self):
-        self.take(6)
+        self.wait(self.base + 7, self.ref(0, 1 - self.needed, 1))
         self.put(7, (0, None, 1), self.plus)
         self.put(8, (0, None, 1), self.minus)
 
@@ -397,7 +403,7 @@
         rows = pl.ds(pl.multiple_of(HALF * c + PART * s, PART), PART)
         inv_row = jnp.broadcast_to(inverse(totbuf[keep(s, 0), zl, :, rows]), (PART, PART))
         inv_row = jnp.concatenate([jnp.transpose(inv_row)] * 4, axis=1)
-        for g in range(2):
+        for g in (0, 1) if s == 0 else (1, 0):
             wait(Y2_ID[s][g], y2r.at[s, g])
             inv_col = inverse(totbuf[(x, 4)[g], zl])
             low = both(s, g, keep(s, 0), 0) + y2r[s, g, 1].astype(F32) + y2r[s, g, 2].astype(F32)
@@ -412,6 +418,7 @@
                 colbuf[keep(s, 0), zh, c, s] = half
                 cols[s][0].start()
             else:
+                rows_of[s].cross()
                 low_out[s] = (value - half.astype(F32)).astype(BF16)
         rows_of[s].start()
         send(LOW_ID[s], low_out.at[s], low_in.at[s], zh_mate, TO_LOW)
@@ -433,7 +440,9 @@
             return r.at[:, :, lanes] if half is None else r.at[half, :, lanes]
 
         late = rowbuf.at[1 - zh, s, :, :, pl.ds(0, 3 * BLOCK)]
-        return Plane(send, wait, ROW_ID[s], TO_ROWS, ref, x_plus, x_minus, late, zh_mate)
+        return Plane(
+            send, wait, ROW_ID[s], TO_ROWS, ref, x_plus, x_minus, late, zh_mate, zh
+        )
 
     def col_line(s, e):
         def ref(step, half):
@@ -576,26 +585,28 @@
     normalise(0)
     lines[1][0].finish()
     lines[1][1].finish()
+    gram(1, 1)
     gram(1, 0)
-    gram(1, 1)
-    reduce_start(1, 0)
+    reduce_start(1, 1)
     cols[0][0].near()
     rows_of[0].near()
-    reduce_start(1, 1)
+    reduce_start(1, 0)
+    reduce_middle(1, 1)
+    rows_of[0].take_needed()
+    partner(0)
     reduce_middle(1, 0)
     rows_of[0].other()
-    partner(0)
-    reduce_middle(1, 1)
     cols[0][0].finish()
     rows_of[0].far()
+    normalise(1)
     cols[0][1].near()
-    normalise(1)
+    cols[1][0].near()
     rows_of[1].near()
-    cols[1][0].near()
     cols[0][1].finish()
-    rows_of[1].other()
+    rows_of[1].take_needed()
     partner(1)
     cols[1][0].finish()
+    rows_of[1].other()
     cols[1][1].near()
     rows_of[1].far()
     cols[1][1].finish()
@@ -603,11 +614,11 @@
         for e in range(2):
             cols[s][e].passed()
     square(0)
-    combine(0)
-    sq_cols[0].near()
     rows_of[0].last()
     rows_of[1].last()
     square(1)
+    combine(0)
+    sq_cols[0].near()
     sq_cols[0].finish()
     partner_low(0)
     partner_low(1)

time: 118 us -> 119 us (level)
  no operation moved by 1% of the time
where the time goes in v8:
time: 119 us; the launch traced here: 118 us
  Pallas kernels  116 us (97%)
  other arithmetic  2.07 us (2%)
    pallas_call x1, Pallas kernels, body(): pl.pallas_call(kernel, out_shape=jax.ShapeDtypeStruct((2, 32, D), BF16),...  116 us

profile of v8, /device:TPU:0, one launch (start us, length us, event | category | flops | bytes accessed | tf_op | source)
XLA Modules:
  0.0 118.4 jit_solution(1656979090693601089)
XLA Ops:
  0.6 115.7 %shard_map.41 = bf16[2,32,4096]{2,1,0:T(8,128)(2,1)} custom-call(bf16[512,512]{1,0:T(8,128)(2,1)} %act_ref.1, bf16[512,512]{1,0:T(8,128)(2,1)} %grad_ref.1), custom_call_target="tpu_custom_call" | custom-call | tf_op jit(solution)/shard_map/pallas_call | solution.py:666
  116.4 2.1 %bitcast_convert_fusion = (f32[32,4096]{1,0:T(8,128)}, f32[32,4096]{1,0:T(8,128)}) fusion(bf16[2,32,4096]{2,1,0:T(8,128)(2,1)} %shard_map.41), kind=kLoop, calls=%fused_computation | loop fusion | flops 262144 | bytes 1572864 | tf_op jit(solution)/shard_map/convert_element_type | solution.py:676

commit v9 on v8

--- a/solution.py
+++ b/solution.py
@@ -38,8 +38,8 @@
 Y2_ID = [[IDS.take(1) for _ in range(2)] for _ in range(2)]
 ROW_ID = [IDS.take(8) for _ in range(2)]
 LOW_ID = [IDS.take(1) for _ in range(2)]
-COL_ID = [[IDS.take(4) for _ in range(2)] for _ in range(2)]
-SQ_ID = [IDS.take(4) for _ in range(2)]
+COL_ID = [[IDS.take(5) for _ in range(2)] for _ in range(2)]
+SQ_ID = [IDS.take(5) for _ in range(2)]
 OUT_ID = IDS.take(1)
 SUM_ID = IDS.take(1)
 TOTAL_ID = IDS.take(1)
@@ -85,6 +85,8 @@
 
 
 class Passed(Line):
+    number = [0, 2, 1, 2, 4, 4]
+
     def __init__(self, send, wait, base, kind, ref, plus, minus, late, sibling, pass_kind, mirrored):
         super().__init__(send, wait, base, kind, ref, plus, minus, late)
         self.sibling, self.pass_kind, self.mirrored = sibling, pass_kind, mirrored
@@ -101,10 +103,15 @@
         self.pass_on((0, 0))
         self.pass_on((0, 1))
 
+    def rest(self):
+        self.wait(self.base + 2, self.late)
+        self.arrived(1)
+        self.arrived(3)
+
     def finish(self):
-        super().finish()
-        for k in (1, 3, 4, 5):
-            self.arrived(k)
+        self.wait(self.base + 4, self.late)
+        self.arrived(4)
+        self.arrived(5)
 
     def passed(self):
         self.wait(self.base + 3, self.mirrored)
@@ -366,13 +373,16 @@
         mine = gram_part[s, g, to, c, halves[half]].astype(F32)
         return mine + drecv[s, g, to, halves[half]].astype(F32)
 
-    def reduce_start(s, g):
-        y1, y2, far, up, down = Y1_ID[s][g], Y2_ID[s][g], keep(s, 2), keep(s, 1), keep(s, 3)
+    def reduce_first(s, g):
+        y1, far = Y1_ID[s][g], keep(s, 2)
         wait(D_ID[s][g], drecv.at[s, g])
         y1s[s, g, 0] = both(s, g, far, 0).astype(BF16)
         send(y1, y1s.at[s, g, 0], y1r.at[s, g, 0], y_plus, TO_Y1)
         y1s[s, g, 1] = both(s, g, far, 1).astype(BF16)
         send(y1 + 1, y1s.at[s, g, 1], y1r.at[s, g, 1], y_minus, TO_Y1)
+
+    def reduce_own(s, g):
+        y2, up, down = Y2_ID[s][g], keep(s, 1), keep(s, 3)
         y2s[s, g, 0] = both(s, g, up, 1).astype(BF16)
         send(y2, y2s.at[s, g, 0], y2r.at[s, g, 0], y_plus, TO_Y2)
         y2s[s, g, 2] = both(s, g, down, 0).astype(BF16)
@@ -448,7 +458,7 @@
         def ref(step, half):
             return colbuf.at[keep(s, step), zh_of[e], c, s, halves[half]]
 
-        late = colbuf.at[pl.ds(0, 2), zh_of[e], c, s]
+        late = colbuf.at[0, zh_of[e], c, s]
         return Passed(
             send, wait, COL_ID[s][e], TO_COLS, ref, y_plus, y_minus, late, sibling, TO_PASS,
             colbuf.at[:, zh_of[e], 1 - c, s],
@@ -458,7 +468,7 @@
         def ref(step, half):
             return sqcol.at[keep(half, step), zh_of[e], c, half]
 
-        late = sqcol.at[pl.ds(0, 2), zh_of[e], c]
+        late = sqcol.at[0, zh_of[e], c]
         return Passed(
             send, wait, SQ_ID[e], TO_SQ, ref, y_plus, y_minus, late, sibling, TO_SQ_PASS,
             sqcol.at[:, zh_of[e], 1 - c],
@@ -572,13 +582,15 @@
     lines[0][0].finish()
     lines[0][1].finish()
     gram(0, 0)
-    reduce_start(0, 0)
+    reduce_first(0, 0)
+    reduce_own(0, 0)
     lines[1][0].near()
     z_rest_take(0)
     z_rest_take(1)
     gram(0, 1)
     reduce_middle(0, 0)
-    reduce_start(0, 1)
+    reduce_first(0, 1)
+    reduce_own(0, 1)
     lines[1][1].near()
     reduce_middle(0, 1)
     totals_finish()
@@ -587,28 +599,34 @@
     lines[1][1].finish()
     gram(1, 1)
     gram(1, 0)
-    reduce_start(1, 1)
-    cols[0][0].near()
+    reduce_first(1, 1)
+    reduce_first(1, 0)
+    reduce_own(1, 1)
+    reduce_own(1, 0)
     rows_of[0].near()
-    reduce_start(1, 0)
     reduce_middle(1, 1)
     rows_of[0].take_needed()
+    rows_of[0].other()
+    reduce_middle(1, 0)
+    cols[0][0].near()
     partner(0)
-    reduce_middle(1, 0)
-    rows_of[0].other()
-    cols[0][0].finish()
+    cols[0][0].rest()
     rows_of[0].far()
     normalise(1)
+    cols[0][0].finish()
     cols[0][1].near()
     cols[1][0].near()
+    cols[0][1].rest()
     rows_of[1].near()
-    cols[0][1].finish()
     rows_of[1].take_needed()
     partner(1)
+    cols[0][1].finish()
+    cols[1][0].rest()
+    rows_of[1].other()
     cols[1][0].finish()
-    rows_of[1].other()
     cols[1][1].near()
     rows_of[1].far()
+    cols[1][1].rest()
     cols[1][1].finish()
     for s in range(2):
         for e in range(2):
@@ -617,13 +635,15 @@
     rows_of[0].last()
     rows_of[1].last()
     square(1)
+    sq_cols[0].near()
     combine(0)
-    sq_cols[0].near()
-    sq_cols[0].finish()
     partner_low(0)
     partner_low(1)
     combine(1)
     sq_cols[1].near()
+    sq_cols[0].rest()
+    sq_cols[0].finish()
+    sq_cols[1].rest()
     sq_cols[0].passed()
     cube_first()
     sq_cols[1].finish()

time: 119 us -> 115 us (0.966)
  Pallas kernels: 116 us -> 112 us
    pallas_call x1, Pallas kernels: 116 us -> 112 us  [body(): pl.pallas_call(kernel, out_shape=jax.ShapeDtypeStruct((2, 32, D), BF16),...]
where the time goes in v9:
time: 115 us; the launch traced here: 114 us
  Pallas kernels  112 us (97%)
  other arithmetic  2.07 us (2%)
    pallas_call x1, Pallas kernels, body(): pl.pallas_call(kernel, out_shape=jax.ShapeDtypeStruct((2, 32, D), BF16),...  112 us

profile of v9, /device:TPU:0, one launch (start us, length us, event | category | flops | bytes accessed | tf_op | source)
XLA Modules:
  0.0 114.4 jit_solution(939745549782240184)
XLA Ops:
  0.6 111.7 %shard_map.41 = bf16[2,32,4096]{2,1,0:T(8,128)(2,1)} custom-call(bf16[512,512]{1,0:T(8,128)(2,1)} %act_ref.1, bf16[512,512]{1,0:T(8,128)(2,1)} %grad_ref.1), custom_call_target="tpu_custom_call" | custom-call | tf_op jit(solution)/shard_map/pallas_call | solution.py:686
  112.3 2.1 %bitcast_convert_fusion = (f32[32,4096]{1,0:T(8,128)}, f32[32,4096]{1,0:T(8,128)}) fusion(bf16[2,32,4096]{2,1,0:T(8,128)(2,1)} %shard_map.41), kind=kLoop, calls=%fused_computation | loop fusion | flops 262144 | bytes 1572864 | tf_op jit(solution)/shard_map/convert_element_type | solution.py:696

commit v10 on v9

--- a/solution.py
+++ b/solution.py
@@ -32,7 +32,7 @@
 
 IDS = Ids()
 Z_ID = IDS.take(6)
-X_ID = [[IDS.take(3) for _ in range(2)] for _ in range(2)]
+X_ID = [[IDS.take(4) for _ in range(2)] for _ in range(2)]
 D_ID = [[IDS.take(1) for _ in range(2)] for _ in range(2)]
 Y1_ID = [[IDS.take(2) for _ in range(2)] for _ in range(2)]
 Y2_ID = [[IDS.take(1) for _ in range(2)] for _ in range(2)]
@@ -51,7 +51,7 @@
 
 class Line:
     arrivals = [(3, 0), (3, 1), (1, 1), (1, 0), (2, 0), (2, 1)]
-    number = [0, 2, 1, 2, 2, 2]
+    number = [0, 2, 1, 2, 3, 3]
 
     def __init__(self, send, wait, base, kind, ref, plus, minus, late):
         self.send, self.wait, self.base, self.kind, self.ref = send, wait, base, kind, ref
@@ -80,8 +80,11 @@
         self.take(2)
         self.put(5, (1, 1), self.minus)
 
+    def rest(self):
+        self.wait(self.base + 2, self.late)
+
     def finish(self):
-        self.wait(self.base + 2, self.late)
+        self.wait(self.base + 3, self.late)
 
 
 class Passed(Line):
@@ -280,7 +283,7 @@
             return xall.at[t, (x + step) % 4, s, token_half[half]]
 
         return Line(
-            send, wait, X_ID[s][t], TO_X, ref, x_plus, x_minus, xall.at[t, (x + 2) % 4]
+            send, wait, X_ID[s][t], TO_X, ref, x_plus, x_minus, xall.at[t, (x + 2) % 4, s]
         )
 
     lines = [[x_line(s, t) for t in range(2)] for s in range(2)]
@@ -337,30 +340,29 @@
     def totals_finish():
         wait(TOTAL_ID, totbuf.at[pl.ds(0, 4)])
 
-    def gram(s, g):
-        cols = (x, 4)[g]
-
+    def gram(s, gs, begin, end):
         def step(i, carry):
             to = (x + 3 + i) % 4
-            for s2 in range(2):
-                value = None
-                for t in range(2):
-                    term = lax.dot_general(
-                        xall[t, to, s], xall[t, cols, s2],
-                        (((0,), (0,)), ((), ())), preferred_element_type=F32,
-                    )
-                    value = term if value is None else value + term
-                value = value.astype(BF16)
-                for k in range(2):
-                    for k2 in range(2):
-                        start = HALF * k2 + PART * s2
-                        gram_part[s, g, to, k, :, start : start + PART] = value[
-                            PART * k : PART * (k + 1), PART * k2 : PART * (k2 + 1)
-                        ]
-            d_copy(s, g, to).start()
+            for g in gs:
+                for s2 in range(2):
+                    value = None
+                    for t in range(2):
+                        term = lax.dot_general(
+                            xall[t, to, s], xall[t, (x, 4)[g], s2],
+                            (((0,), (0,)), ((), ())), preferred_element_type=F32,
+                        )
+                        value = term if value is None else value + term
+                    value = value.astype(BF16)
+                    for k in range(2):
+                        for k2 in range(2):
+                            start = HALF * k2 + PART * s2
+                            gram_part[s, g, to, k, :, start : start + PART] = value[
+                                PART * k : PART * (k + 1), PART * k2 : PART * (k2 + 1)
+                            ]
+                d_copy(s, g, to).start()
             return carry
 
-        lax.fori_loop(0, 4, step, 0)
+        lax.fori_loop(begin, end, step, 0)
 
     def d_copy(s, g, to):
         return remote(
@@ -579,26 +581,30 @@
     lines[1][0].start()
     z_first_take(1)
     lines[1][1].start()
+    lines[0][0].rest()
     lines[0][0].finish()
+    lines[0][1].rest()
     lines[0][1].finish()
-    gram(0, 0)
+    gram(0, (0,), 0, 4)
     reduce_first(0, 0)
     reduce_own(0, 0)
     lines[1][0].near()
     z_rest_take(0)
     z_rest_take(1)
-    gram(0, 1)
+    gram(0, (1,), 0, 4)
     reduce_middle(0, 0)
     reduce_first(0, 1)
     reduce_own(0, 1)
     lines[1][1].near()
     reduce_middle(0, 1)
     totals_finish()
+    lines[1][0].rest()
+    lines[1][1].rest()
+    gram(1, (1, 0), 0, 3)
     normalise(0)
     lines[1][0].finish()
     lines[1][1].finish()
-    gram(1, 1)
-    gram(1, 0)
+    gram(1, (1, 0), 3, 4)
     reduce_first(1, 1)
     reduce_first(1, 0)
     reduce_own(1, 1)
@@ -685,7 +691,7 @@
     ]
     out = pl.pallas_call(
         kernel,
-        out_shape=jax.ShapeDtypeStruct((2, 32, D), BF16),
+        out_shape=pltpu.VMEM((2, 32, D), BF16),
         in_specs=[hbm, hbm],
         out_specs=vmem,
         scratch_shapes=scratch,

time: 115 us -> 113 us (0.983); the launches traced: 114 us -> 111 us
  Pallas kernels: 112 us -> 109 us
    pallas_call x1, Pallas kernels: 112 us -> 109 us  [body(): pl.pallas_call(kernel, out_shape=pltpu.VMEM((2, 32, D), BF16), in_specs=[...]
where the time goes in v10:
time: 113 us; the launch traced here: 111 us
  Pallas kernels  109 us (96%)
    pallas_call x1, Pallas kernels, body(): pl.pallas_call(kernel, out_shape=pltpu.VMEM((2, 32, D), BF16), in_specs=[...  109 us

profile of v10, /device:TPU:0, one launch (start us, length us, event | category | flops | bytes accessed | tf_op | source)
XLA Modules:
  0.0 111.0 jit_solution(10589962931734995321)
XLA Ops:
  0.6 109.3 %shard_map.41 = bf16[2,32,4096]{2,1,0:T(8,128)(2,1)S(1)} custom-call(bf16[512,512]{1,0:T(8,128)(2,1)} %act_ref.1, bf16[512,512]{1,0:T(8,128)(2,1)} %grad_ref.1), custom_call_target="tpu_custom_call" | custom-call | tf_op jit(solution)/shard_map/pallas_call | solution.py:692
  110.0 1.0 bitcast_convert_fusion

commit v11 on v10

--- a/solution.py
+++ b/solution.py
@@ -411,27 +411,28 @@
     def lane_block(block):
         return pl.ds(pl.multiple_of(block * BLOCK, BLOCK), BLOCK)
 
-    def normalise(s):
+    def normalise(s, g):
         rows = pl.ds(pl.multiple_of(HALF * c + PART * s, PART), PART)
         inv_row = jnp.broadcast_to(inverse(totbuf[keep(s, 0), zl, :, rows]), (PART, PART))
         inv_row = jnp.concatenate([jnp.transpose(inv_row)] * 4, axis=1)
-        for g in (0, 1) if s == 0 else (1, 0):
-            wait(Y2_ID[s][g], y2r.at[s, g])
-            inv_col = inverse(totbuf[(x, 4)[g], zl])
-            low = both(s, g, keep(s, 0), 0) + y2r[s, g, 1].astype(F32) + y2r[s, g, 2].astype(F32)
-            high = both(s, g, keep(s, 0), 1) + y2r[s, g, 0].astype(F32) + y2r[s, g, 3].astype(F32)
-            total = jnp.concatenate([low, high], axis=0)
-            damped = total / TOKENS * inv_row * inv_col + damping * eye(s, zh, zh_of[g])
-            value = damped / divisor
-            half = value.astype(BF16)
-            rowbuf[zh, s, zh_of[g], :, lane_block(x)] = half
-            if g == 0:
-                scaled[0, s] = value
-                colbuf[keep(s, 0), zh, c, s] = half
-                cols[s][0].start()
-            else:
-                rows_of[s].cross()
-                low_out[s] = (value - half.astype(F32)).astype(BF16)
+        wait(Y2_ID[s][g], y2r.at[s, g])
+        inv_col = inverse(totbuf[(x, 4)[g], zl])
+        low = both(s, g, keep(s, 0), 0) + y2r[s, g, 1].astype(F32) + y2r[s, g, 2].astype(F32)
+        high = both(s, g, keep(s, 0), 1) + y2r[s, g, 0].astype(F32) + y2r[s, g, 3].astype(F32)
+        total = jnp.concatenate([low, high], axis=0)
+        damped = total / TOKENS * inv_row * inv_col + damping * eye(s, zh, zh_of[g])
+        value = damped / divisor
+        half = value.astype(BF16)
+        rowbuf[zh, s, zh_of[g], :, lane_block(x)] = half
+        if g == 0:
+            scaled[0, s] = value
+            colbuf[keep(s, 0), zh, c, s] = half
+            cols[s][0].start()
+        else:
+            rows_of[s].cross()
+            low_out[s] = (value - half.astype(F32)).astype(BF16)
+
+    def rows_start(s):
         rows_of[s].start()
         send(LOW_ID[s], low_out.at[s], low_in.at[s], zh_mate, TO_LOW)
 
@@ -494,9 +495,18 @@
 
         lax.fori_loop(0, 2, step, 0)
 
+    def square_first():
+        def some(lanes):
+            sq[0, :, lanes] = dot(0, zh, colbuf, lanes)
+
+        over_lanes(some)
+
     def square(e):
         def some(lanes):
-            sq[e, :, lanes] = dot(e, 0, colbuf, lanes) + dot(e, 1, colbuf, lanes)
+            if e == 0:
+                sq[e, :, lanes] = sq[e, :, lanes] + dot(e, 1 - zh, colbuf, lanes)
+            else:
+                sq[e, :, lanes] = dot(e, 0, colbuf, lanes) + dot(e, 1, colbuf, lanes)
 
         over_lanes(some)
         for s in range(2):
@@ -523,7 +533,7 @@
             obuf[e, :, lanes] = (value - dot(e, 1 - zh, sqcol, lanes)).astype(BF16)
 
         over_lanes(some)
-        for b in range(8):
+        for b in (0, 4, 2, 6, 1, 5, 3, 7):
             me = (out_tok(e, b // 4) == tok) & (blk == b)
 
             @pl.when(me)
@@ -591,17 +601,21 @@
     lines[1][0].near()
     z_rest_take(0)
     z_rest_take(1)
+    reduce_middle(0, 0)
     gram(0, (1,), 0, 4)
-    reduce_middle(0, 0)
+    totals_finish()
     reduce_first(0, 1)
     reduce_own(0, 1)
     lines[1][1].near()
+    normalise(0, 0)
     reduce_middle(0, 1)
-    totals_finish()
     lines[1][0].rest()
     lines[1][1].rest()
     gram(1, (1, 0), 0, 3)
-    normalise(0)
+    cols[0][0].near()
+    normalise(0, 1)
+    rows_start(0)
+    cols[0][0].rest()
     lines[1][0].finish()
     lines[1][1].finish()
     gram(1, (1, 0), 3, 4)
@@ -609,34 +623,36 @@
     reduce_first(1, 0)
     reduce_own(1, 1)
     reduce_own(1, 0)
+    reduce_middle(1, 1)
     rows_of[0].near()
-    reduce_middle(1, 1)
+    reduce_middle(1, 0)
     rows_of[0].take_needed()
+    partner(0)
     rows_of[0].other()
-    reduce_middle(1, 0)
-    cols[0][0].near()
-    partner(0)
-    cols[0][0].rest()
+    cols[0][0].finish()
+    normalise(1, 1)
+    normalise(1, 0)
+    rows_start(1)
+    cols[0][1].near()
     rows_of[0].far()
-    normalise(1)
-    cols[0][0].finish()
-    cols[0][1].near()
     cols[1][0].near()
     cols[0][1].rest()
     rows_of[1].near()
     rows_of[1].take_needed()
     partner(1)
-    cols[0][1].finish()
     cols[1][0].rest()
     rows_of[1].other()
+    cols[1][1].near()
+    cols[0][1].finish()
     cols[1][0].finish()
-    cols[1][1].near()
     rows_of[1].far()
+    cols[0][0].passed()
+    cols[1][0].passed()
+    square_first()
     cols[1][1].rest()
     cols[1][1].finish()
-    for s in range(2):
-        for e in range(2):
-            cols[s][e].passed()
+    cols[0][1].passed()
+    cols[1][1].passed()
     square(0)
     rows_of[0].last()
     rows_of[1].last()

time: 113 us -> 112 us (level); the launches traced: 111 us -> 112 us
  no operation moved by 1% of the time
where the time goes in v11:
time: 112 us
  Pallas kernels  110 us (98%)
    pallas_call x1, Pallas kernels, body(): pl.pallas_call(kernel, out_shape=pltpu.VMEM((2, 32, D), BF16), in_specs=[...  110 us

profile of v11, /device:TPU:0, one launch (start us, length us, event | category | flops | bytes accessed | tf_op | source)
XLA Modules:
  0.0 111.7 jit_solution(8200307685138036952)
XLA Ops:
  0.6 110.0 %shard_map.41 = bf16[2,32,4096]{2,1,0:T(8,128)(2,1)S(1)} custom-call(bf16[512,512]{1,0:T(8,128)(2,1)} %act_ref.1, bf16[512,512]{1,0:T(8,128)(2,1)} %grad_ref.1), custom_call_target="tpu_custom_call" | custom-call | tf_op jit(solution)/shard_map/pallas_call | solution.py:708
  110.7 1.0 bitcast_convert_fusion

commit v12 on v10

--- a/solution.py
+++ b/solution.py
@@ -239,27 +239,12 @@
         greet(((tok + j) % 16, blk))
         return carry
 
-    def greet_blk(j, carry):
-        greet((tok, (blk + j) % 8))
-        return carry
-
     lax.fori_loop(1, 16, greet_tok, 0)
-    lax.fori_loop(1, 8, greet_blk, 0)
-    greet(z_cross)
-
-    def greet_source(j, carry):
-        to = (tok_of(j % 2, source_y, c), j // 2)
-
-        @pl.when(jnp.logical_not((to[0] == tok) & (to[1] == blk)))
-        def _():
-            greet(to)
-
-        return carry
-
-    lax.fori_loop(0, 16, greet_source, 0)
+    for to in (x_plus, x_minus, zh_mate, z_cross):
+        greet(to)
     for copy in all_loads(act_ref, grad_ref):
         copy.wait()
-    pl.semaphore_wait(barrier, 15 + 7 + 1 + 16 - home.astype(jnp.int32))
+    pl.semaphore_wait(barrier, 15 + 4)
 
     def remote(k, src, dst, to, kind):
         return pltpu.make_async_remote_copy(
@@ -494,9 +479,18 @@
 
         lax.fori_loop(0, 2, step, 0)
 
+    def square_first():
+        def some(lanes):
+            sq[0, :, lanes] = dot(0, zh, colbuf, lanes)
+
+        over_lanes(some)
+
     def square(e):
         def some(lanes):
-            sq[e, :, lanes] = dot(e, 0, colbuf, lanes) + dot(e, 1, colbuf, lanes)
+            if e == 0:
+                sq[e, :, lanes] = sq[e, :, lanes] + dot(e, 1 - zh, colbuf, lanes)
+            else:
+                sq[e, :, lanes] = dot(e, 0, colbuf, lanes) + dot(e, 1, colbuf, lanes)
 
         over_lanes(some)
         for s in range(2):
@@ -523,7 +517,7 @@
             obuf[e, :, lanes] = (value - dot(e, 1 - zh, sqcol, lanes)).astype(BF16)
 
         over_lanes(some)
-        for b in range(8):
+        for b in (0, 4, 2, 6, 1, 5, 3, 7):
             me = (out_tok(e, b // 4) == tok) & (blk == b)
 
             @pl.when(me)
@@ -609,34 +603,36 @@
     reduce_first(1, 0)
     reduce_own(1, 1)
     reduce_own(1, 0)
+    reduce_middle(1, 1)
     rows_of[0].near()
-    reduce_middle(1, 1)
+    reduce_middle(1, 0)
     rows_of[0].take_needed()
+    partner(0)
+    cols[0][0].near()
     rows_of[0].other()
-    reduce_middle(1, 0)
-    cols[0][0].near()
-    partner(0)
     cols[0][0].rest()
+    normalise(1)
+    cols[0][1].near()
     rows_of[0].far()
-    normalise(1)
+    cols[1][0].near()
     cols[0][0].finish()
-    cols[0][1].near()
-    cols[1][0].near()
     cols[0][1].rest()
     rows_of[1].near()
     rows_of[1].take_needed()
     partner(1)
-    cols[0][1].finish()
     cols[1][0].rest()
     rows_of[1].other()
+    cols[1][1].near()
+    cols[0][1].finish()
     cols[1][0].finish()
-    cols[1][1].near()
     rows_of[1].far()
+    cols[0][0].passed()
+    cols[1][0].passed()
+    square_first()
     cols[1][1].rest()
     cols[1][1].finish()
-    for s in range(2):
-        for e in range(2):
-            cols[s][e].passed()
+    cols[0][1].passed()
+    cols[1][1].passed()
     square(0)
     rows_of[0].last()
     rows_of[1].last()

time: 113 us -> 109 us (0.965)
  Pallas kernels: 109 us -> 106 us
    pallas_call x1, Pallas kernels: 109 us -> 106 us  [body(): pl.pallas_call(kernel, out_shape=pltpu.VMEM((2, 32, D), BF16), in_specs=[...]
where the time goes in v12:
time: 109 us; the launch traced here: 108 us
  Pallas kernels  106 us (97%)
    pallas_call x1, Pallas kernels, body(): pl.pallas_call(kernel, out_shape=pltpu.VMEM((2, 32, D), BF16), in_specs=[...  106 us

profile of v12, /device:TPU:0, one launch (start us, length us, event | category | flops | bytes accessed | tf_op | source)
XLA Modules:
  0.0 108.1 jit_solution(10260126173757999710)
XLA Ops:
  0.6 106.4 %shard_map.41 = bf16[2,32,4096]{2,1,0:T(8,128)(2,1)S(1)} custom-call(bf16[512,512]{1,0:T(8,128)(2,1)} %act_ref.1, bf16[512,512]{1,0:T(8,128)(2,1)} %grad_ref.1), custom_call_target="tpu_custom_call" | custom-call | tf_op jit(solution)/shard_map/pallas_call | solution.py:688
  107.1 1.0 bitcast_convert_fusion

commit v13 on v11

--- a/solution.py
+++ b/solution.py
@@ -106,6 +106,15 @@
         self.pass_on((0, 0))
         self.pass_on((0, 1))
 
+    def start_direct(self, far):
+        self.start()
+        self.put(4, (0, 0), far)
+        self.put(5, (0, 1), far)
+
+    def near_direct(self):
+        self.take(0)
+        self.take(2)
+
     def rest(self):
         self.wait(self.base + 2, self.late)
         self.arrived(1)
@@ -124,26 +133,37 @@
     arrivals = Line.arrivals + [None, (3, None, 1), (1, None, 1), (2, 0, 1), (2, 1, 1)]
     number = [0, 2, 1, 2, 3, 4, 5, 6, 6, 6, 6]
 
-    def __init__(self, send, wait, base, kind, ref, plus, minus, late, across, needed):
+    def __init__(self, send, wait, base, kind, ref, plus, minus, late, across):
         super().__init__(send, wait, base, kind, ref, plus, minus, late)
-        self.across, self.needed = across, needed
-
-    def cross(self):
-        r = self.ref(0, 1 - self.needed, 0)
-        self.send(self.base + 5, r, r, self.across, self.kind)
-
-    def start(self):
-        r = self.ref(0, self.needed, 0)
-        self.send(self.base + 7, r, r, self.across, self.kind)
-        super().start()
+        self.across = across
+
+    def cross(self, half):
+        r = self.ref(0, half, 0)
+        self.send(self.base + (7, 5)[half], r, r, self.across, self.kind)
+
+    def start_half(self, half):
+        if half == 0:
+            self.put(0, (0, 0), self.plus)
+            self.put(3, (0, 0), self.minus)
+        else:
+            self.put(2, (0, 1), self.minus)
+            self.put(1, (0, 1), self.plus)
 
     def take_needed(self):
-        self.wait(self.base + 5, self.ref(0, self.needed, 1))
+        self.wait(self.base + 5, self.ref(0, 1, 1))
 
     def other(self):
-        self.wait(self.base + 7, self.ref(0, 1 - self.needed, 1))
+        self.wait(self.base + 7, self.ref(0, 0, 1))
         self.put(7, (0, None, 1), self.plus)
         self.put(8, (0, None, 1), self.minus)
+
+    def near_half(self, half):
+        if half == 0:
+            self.take(0)
+            self.put(4, (3, 0), self.plus)
+        else:
+            self.take(2)
+            self.put(5, (1, 1), self.minus)
 
     def far(self):
         self.wait(self.base + 2, self.ref(3, None))
@@ -177,6 +197,7 @@
     zh_mate = (tok, blk_of(x, 1 - zh))
     y_plus = (tok_of(zl, (y + 1) % 4, c), blk)
     y_minus = (tok_of(zl, (y + 3) % 4, c), blk)
+    y_far = (tok_of(zl, (y + 2) % 4, c), blk)
     zl_mate = (tok_of(1 - zl, y, c), blk)
     z_cross = (tok_of(1 - zl, y, c), blk_of(x, 1 - zh))
     sibling = (tok_of(zl, y, 1 - c), blk)
@@ -239,27 +260,12 @@
         greet(((tok + j) % 16, blk))
         return carry
 
-    def greet_blk(j, carry):
-        greet((tok, (blk + j) % 8))
-        return carry
-
     lax.fori_loop(1, 16, greet_tok, 0)
-    lax.fori_loop(1, 8, greet_blk, 0)
-    greet(z_cross)
-
-    def greet_source(j, carry):
-        to = (tok_of(j % 2, source_y, c), j // 2)
-
-        @pl.when(jnp.logical_not((to[0] == tok) & (to[1] == blk)))
-        def _():
-            greet(to)
-
-        return carry
-
-    lax.fori_loop(0, 16, greet_source, 0)
+    for to in (x_plus, x_minus, zh_mate, z_cross):
+        greet(to)
     for copy in all_loads(act_ref, grad_ref):
         copy.wait()
-    pl.semaphore_wait(barrier, 15 + 7 + 1 + 16 - home.astype(jnp.int32))
+    pl.semaphore_wait(barrier, 15 + 4)
 
     def remote(k, src, dst, to, kind):
         return pltpu.make_async_remote_copy(
@@ -429,17 +435,25 @@
             colbuf[keep(s, 0), zh, c, s] = half
             cols[s][0].start()
         else:
-            rows_of[s].cross()
+            rows_of[s].cross(1)
             low_out[s] = (value - half.astype(F32)).astype(BF16)
+        rows_of[s].start_half(g)
 
     def rows_start(s):
-        rows_of[s].start()
+        rows_of[s].cross(0)
+        if s == 0:
+            low_send(s)
+
+    def low_send(s):
         send(LOW_ID[s], low_out.at[s], low_in.at[s], zh_mate, TO_LOW)
 
     def partner(s):
         half = rowbuf[1 - zh, s, zh, :, lane_block(x)]
         colbuf[keep(s, 0), 1 - zh, c, s] = half
-        cols[s][1].start()
+        if s == 0:
+            cols[s][1].start()
+        else:
+            cols[s][1].start_direct(y_far)
 
     def partner_low(s):
         wait(LOW_ID[s], low_in.at[s])
@@ -450,11 +464,11 @@
         def ref(step, half, other=0):
             lanes = lane_block((x + step) % 4)
             r = rowbuf.at[zh_of[other], s]
-            return r.at[:, :, lanes] if half is None else r.at[half, :, lanes]
+            return r.at[:, :, lanes] if half is None else r.at[zh_of[(half + other) % 2], :, lanes]
 
         late = rowbuf.at[1 - zh, s, :, :, pl.ds(0, 3 * BLOCK)]
         return Plane(
-            send, wait, ROW_ID[s], TO_ROWS, ref, x_plus, x_minus, late, zh_mate, zh
+            send, wait, ROW_ID[s], TO_ROWS, ref, x_plus, x_minus, late, zh_mate
         )
 
     def col_line(s, e):
@@ -601,21 +615,19 @@
     lines[1][0].near()
     z_rest_take(0)
     z_rest_take(1)
+    gram(0, (1,), 0, 4)
     reduce_middle(0, 0)
-    gram(0, (1,), 0, 4)
-    totals_finish()
     reduce_first(0, 1)
     reduce_own(0, 1)
     lines[1][1].near()
+    totals_finish()
+    reduce_middle(0, 1)
     normalise(0, 0)
-    reduce_middle(0, 1)
     lines[1][0].rest()
     lines[1][1].rest()
     gram(1, (1, 0), 0, 3)
-    cols[0][0].near()
     normalise(0, 1)
     rows_start(0)
-    cols[0][0].rest()
     lines[1][0].finish()
     lines[1][1].finish()
     gram(1, (1, 0), 3, 4)
@@ -623,29 +635,34 @@
     reduce_first(1, 0)
     reduce_own(1, 1)
     reduce_own(1, 0)
+    rows_of[0].near_half(0)
+    cols[0][0].near()
     reduce_middle(1, 1)
-    rows_of[0].near()
+    rows_of[0].near_half(1)
     reduce_middle(1, 0)
     rows_of[0].take_needed()
     partner(0)
     rows_of[0].other()
-    cols[0][0].finish()
+    cols[0][0].rest()
+    rows_of[0].far()
     normalise(1, 1)
     normalise(1, 0)
     rows_start(1)
     cols[0][1].near()
-    rows_of[0].far()
+    cols[0][0].finish()
     cols[1][0].near()
-    cols[0][1].rest()
-    rows_of[1].near()
     rows_of[1].take_needed()
     partner(1)
+    rows_of[1].near_half(1)
+    cols[0][1].rest()
+    rows_of[1].near_half(0)
+    rows_of[1].other()
     cols[1][0].rest()
-    rows_of[1].other()
-    cols[1][1].near()
+    cols[1][1].near_direct()
     cols[0][1].finish()
     cols[1][0].finish()
     rows_of[1].far()
+    low_send(1)
     cols[0][0].passed()
     cols[1][0].passed()
     square_first()

time: 112 us -> 109 us (0.973)
  Pallas kernels: 110 us -> 107 us
    pallas_call x1, Pallas kernels: 110 us -> 107 us  [body(): pl.pallas_call(kernel, out_shape=pltpu.VMEM((2, 32, D), BF16), in_specs=[...]
where the time goes in v13:
time: 109 us; the launch traced here: 108 us
  Pallas kernels  107 us (98%)
    pallas_call x1, Pallas kernels, body(): pl.pallas_call(kernel, out_shape=pltpu.VMEM((2, 32, D), BF16), in_specs=[...  107 us

profile of v13, /device:TPU:0, one launch (start us, length us, event | category | flops | bytes accessed | tf_op | source)
XLA Modules:
  0.0 108.5 jit_solution(17135130645393884413)
XLA Ops:
  0.6 106.8 %shard_map.41 = bf16[2,32,4096]{2,1,0:T(8,128)(2,1)S(1)} custom-call(bf16[512,512]{1,0:T(8,128)(2,1)} %act_ref.1, bf16[512,512]{1,0:T(8,128)(2,1)} %grad_ref.1), custom_call_target="tpu_custom_call" | custom-call | tf_op jit(solution)/shard_map/pallas_call | solution.py:725
  107.4 1.0 bitcast_convert_fusion

commit v14 on v13

--- a/solution.py
+++ b/solution.py
@@ -105,6 +105,13 @@
         super().start()
         self.pass_on((0, 0))
         self.pass_on((0, 1))
+
+    def start_set(self, half):
+        for k, to in ((0, self.plus), (3, self.minus)) if half == 0 else (
+            (2, self.minus), (1, self.plus)
+        ):
+            self.put(k, (0, half), to)
+        self.pass_on((0, half))
 
     def start_direct(self, far):
         self.start()
@@ -516,16 +523,28 @@
         over_lanes(some)
 
     def square(e):
-        def some(lanes):
-            if e == 0:
-                sq[e, :, lanes] = sq[e, :, lanes] + dot(e, 1 - zh, colbuf, lanes)
-            else:
+        if e == 1:
+            def some(lanes):
                 sq[e, :, lanes] = dot(e, 0, colbuf, lanes) + dot(e, 1, colbuf, lanes)
 
-        over_lanes(some)
+            over_lanes(some)
+            for s in range(2):
+                sqcol[keep(s, 0), zh_of[e], c, s] = sq[e, PART * s : PART * (s + 1)].astype(BF16)
+            sq_cols[e].start()
+            return
         for s in range(2):
-            sqcol[keep(s, 0), zh_of[e], c, s] = sq[e, PART * s : PART * (s + 1)].astype(BF16)
-        sq_cols[e].start()
+            rows = pl.ds(PART * s, PART)
+
+            def some_rows(lanes):
+                sq[e, rows, lanes] = sq[e, rows, lanes] + jnp.dot(
+                    rowbuf[zh_of[e], s, 1 - zh],
+                    colbuf[:, 1 - zh, :, :, :, lanes].reshape(D // 2, HALF),
+                    preferred_element_type=F32,
+                )
+
+            over_lanes(some_rows)
+            sqcol[keep(s, 0), zh_of[e], c, s] = sq[e, rows].astype(BF16)
+            sq_cols[e].start_set(s)
 
     def combine(e):
         for s in range(2):

time: 109 us -> 108 us (level)
  no operation moved by 1% of the time
where the time goes in v14:
time: 108 us
  Pallas kernels  107 us (99%)
    pallas_call x1, Pallas kernels, body(): pl.pallas_call(kernel, out_shape=pltpu.VMEM((2, 32, D), BF16), in_specs=[...  107 us

profile of v14, /device:TPU:0, one launch (start us, length us, event | category | flops | bytes accessed | tf_op | source)
XLA Modules:
  0.0 108.3 jit_solution(5535115598057998830)
XLA Ops:
  0.6 106.6 %shard_map.41 = bf16[2,32,4096]{2,1,0:T(8,128)(2,1)S(1)} custom-call(bf16[512,512]{1,0:T(8,128)(2,1)} %act_ref.1, bf16[512,512]{1,0:T(8,128)(2,1)} %grad_ref.1), custom_call_target="tpu_custom_call" | custom-call | tf_op jit(solution)/shard_map/pallas_call | solution.py:744
  107.2 1.0 bitcast_convert_fusion

commit v15 on v14

--- a/solution.py
+++ b/solution.py
@@ -440,7 +440,10 @@
         if g == 0:
             scaled[0, s] = value
             colbuf[keep(s, 0), zh, c, s] = half
-            cols[s][0].start()
+            if s == 0:
+                cols[s][0].start()
+            else:
+                cols[s][0].start_direct(y_far)
         else:
             rows_of[s].cross(1)
             low_out[s] = (value - half.astype(F32)).astype(BF16)
@@ -669,9 +672,9 @@
     rows_start(1)
     cols[0][1].near()
     cols[0][0].finish()
-    cols[1][0].near()
     rows_of[1].take_needed()
     partner(1)
+    cols[1][0].near_direct()
     rows_of[1].near_half(1)
     cols[0][1].rest()
     rows_of[1].near_half(0)

time: 108 us -> 110 us (1.019)
  Pallas kernels: 107 us -> 109 us
    pallas_call x1, Pallas kernels: 107 us -> 109 us  [body(): pl.pallas_call(kernel, out_shape=pltpu.VMEM((2, 32, D), BF16), in_specs=[...]
where the time goes in v15:
time: 110 us
  Pallas kernels  109 us (99%)
    pallas_call x1, Pallas kernels, body(): pl.pallas_call(kernel, out_shape=pltpu.VMEM((2, 32, D), BF16), in_specs=[...  109 us

profile of v15, /device:TPU:0, one launch (start us, length us, event | category | flops | bytes accessed | tf_op | source)
XLA Modules:
  0.0 110.2 jit_solution(18148555259178268729)
XLA Ops:
  0.6 108.5 %shard_map.41 = bf16[2,32,4096]{2,1,0:T(8,128)(2,1)S(1)} custom-call(bf16[512,512]{1,0:T(8,128)(2,1)} %act_ref.1, bf16[512,512]{1,0:T(8,128)(2,1)} %grad_ref.1), custom_call_target="tpu_custom_call" | custom-call | tf_op jit(solution)/shard_map/pallas_call | solution.py:747
  109.1 1.0 bitcast_convert_fusion
